TPU v7x, 32 devices: a whole 2x2x4 slice. The times are simulated.
32 devices in a mesh: grp: 4 (over y, x), mem: 8 (over z, core).
Axes of the slice: x: 2, y: 2, z: 4, core: 2. Of those that a mesh axis runs over, the one named last changes fastest.
Arguments:
- values: bfloat16 [32, 8, 32, 128], P(('grp', 'mem')), may hold values from -6 to 6
- slots: int32 [32, 8, 32], P(('grp', 'mem')), may hold values from 0 to 7167
- counts: int32 [32, 8], P(('grp', 'mem')), may hold values from 0 to 32, as said below
Outputs:
- averaged: float32 [57344, 128], P('mem')
- returned: bfloat16 [32, 8, 32, 128], P(('grp', 'mem'))
Inputs may be any that keep to these rules, and one draw needn't show every extreme that they name: `counts`: every device has at least one list with exactly 32 valid entries.
All inputs are finite; a program needn't handle non-finite values.
Results may differ from a plain program's by a relative error of at most 0.0024.
Values may be sent and summed in bfloat16 or wider, within the bound.
No kernel may reach another device: no remote copies, remote signals or barrier semaphores. Data moves between devices by JAX's collectives and lax.ppermute only.
A program may use at most 64 MiB of HBM per device.

v0:
```python
import math

import jax
import jax.numpy as jnp
from jax import lax
from jax.sharding import PartitionSpec as P

BUCKET = 7168


def tiled_sums(rows_in, slot_in):
    lane_count = rows_in.shape[1]
    tile = math.gcd(BUCKET, 1024)

    def one_tile(first):
        wanted = first + lax.broadcasted_iota(jnp.int32, (tile, 1), 0)
        onehot = (wanted == slot_in[None, :]).astype(jnp.bfloat16)
        return jnp.dot(onehot, rows_in, preferred_element_type=jnp.float32)

    starts = jnp.arange(BUCKET // tile, dtype=jnp.int32) * tile
    return lax.map(one_tile, starts).reshape(BUCKET, lane_count)


def live_counts(slot_in):
    live_in = (slot_in >= 0).astype(jnp.float32)
    return jax.ops.segment_sum(live_in, jnp.maximum(slot_in, 0), num_segments=BUCKET)


def per_device(values, slots, counts):
    blocks_out = values[0]
    slot_ids = slots[0]
    list_counts = counts[0]
    members, capacity, lane_count = blocks_out.shape
    is_valid = lax.broadcasted_iota(jnp.int32, (members, capacity), 1) < list_counts[:, None]
    send_blocks = jnp.where(is_valid[:, :, None], blocks_out, jnp.zeros_like(blocks_out))
    send_slots = jnp.where(is_valid, slot_ids, -1)
    got_blocks, got_slots = (
        lax.all_to_all(send_blocks, "mem", split_axis=0, concat_axis=0, tiled=True),
        lax.all_to_all(send_slots, "mem", split_axis=0, concat_axis=0, tiled=True),
    )
    rows_in = got_blocks.reshape(members * capacity, lane_count)
    slot_in = got_slots.reshape(members * capacity)
    slot_count = None
    local_sums = tiled_sums(rows_in, slot_in)
    payload = (local_sums, live_counts(slot_in))
    reduced = lax.psum(payload, "grp")
    total_count = reduced[1]
    averaged = reduced[0] / jnp.maximum(total_count, 1.0)[:, None]
    owned_rows = jnp.take(averaged, jnp.maximum(slot_in, 0), axis=0)
    back_rows = jnp.where((slot_in >= 0)[:, None], owned_rows, 0.0).astype(jnp.bfloat16)
    back_rows = back_rows.reshape(members, capacity, lane_count)
    returned = lax.all_to_all(back_rows, "mem", split_axis=0, concat_axis=0, tiled=True)
    return (averaged, returned[None])


def solution(mesh):
    return jax.shard_map(
        per_device,
        mesh=mesh,
        in_specs=(
            P(("grp", "mem"), None, None, None),
            P(("grp", "mem"), None, None),
            P(("grp", "mem"), None),
        ),
        out_specs=(P("mem", None), P(("grp", "mem"), None, None, None)),
        check_vma=False,
    )
```

profile of v0, /device:TPU:0, one launch (start us, length us, event | category | flops | bytes accessed | tf_op | source)
XLA Modules:
  0.0 168.0 jit_solution(9887654835759522025)
XLA Ops:
  7.2 1.4 compare_select_fusion
  8.5 6.4 %all-to-all-start = ((s32[8,1,32]{2,1,0:T(1,128)}), s32[8,1,32]{2,1,0:T(1,128)S(1)}, u32[]{:S(2)}, u32[]{:S(2)}) async-start(s32[8,1,32]{2,1,0:T(1,128)} %compare_select_fusion), calls=%async_computation | async-start | bytes 8192 | tf_op jit(solution)/shard_map/all_to_all | solution.py:39
  14.9 0.7 iota_compare_fusion
  15.6 1.6 bitcast_select_fusion
  17.2 3.2 %all-to-all-done = s32[8,1,32]{2,1,0:T(1,128)S(1)} async-done(((s32[8,1,32]{2,1,0:T(1,128)}), s32[8,1,32]{2,1,0:T(1,128)S(1)}, u32[]{:S(2)}, u32[]{:S(2)}) %all-to-all-start) | async-done | bytes 1056 | tf_op jit(solution)/shard_map/all_to_all | solution.py:39
  20.4 3.4 %all-to-all-start.1 = ((bf16[8,32,128]{2,1,0:T(8,128)(2,1)}), bf16[8,32,128]{2,1,0:T(8,128)(2,1)S(1)}, u32[]{:S(2)}, u32[]{:S(2)}) async-start(bf16[8,32,128]{2,1,0:T(8,128)(2,1)} %bitcast_select_fusion), calls=%async_computation.1 | async-start | bytes 131072 | tf_op jit(solution)/shard_map/all_to_all | solution.py:38
  23.9 5.7 %all-to-all-done.1 = bf16[8,32,128]{2,1,0:T(8,128)(2,1)S(1)} async-done(((bf16[8,32,128]{2,1,0:T(8,128)(2,1)}), bf16[8,32,128]{2,1,0:T(8,128)(2,1)S(1)}, u32[]{:S(2)}, u32[]{:S(2)}) %all-to-all-start.1) | async-done | bytes 65568 | tf_op jit(solution)/shard_map/all_to_all | solution.py:38
  29.6 16.7 %while.11 = (s32[]{:T(128)}, f32[7,1024,128]{2,1,0:T(8,128)}, s32[7]{0:T(128)S(1)}, s32[8,32]{1,0:T(8,128)}, bf16[256,128]{1,0:T(8,128)(2,1)S(1)}, /*index=5*/s32[256]{0:T(256)S(1)}, s32[]{:T(128)}) while((s32[]{:T(128)}, f32[7,1024,128]{2,1,0:T(8,128)}, s32[7]{0:T(128)S(1)}, s32[8,32]{1,0:T(8,128)}, bf16[256,128]{1,0:T(8,128)(2,1)S(1)}, ...), condition=%wide.wide.region_1.2_spmd, body=%wide.wide.region_0.1_spmd.sunk | while | flops 67372032 | bytes 599645 | solution.py:21
  29.6 0.6 dynamic_slice.6
  30.2 0.6 iota_add_fusion.3
  30.8 1.2 fusion.16
  32.0 0.6 dynamic_slice.6
  32.6 0.6 iota_add_fusion.3
  33.2 1.2 fusion.16
  35.0 0.6 iota_add_fusion.3
  35.6 1.2 fusion.16
  37.4 0.6 iota_add_fusion.3
  38.0 1.2 fusion.16
  39.7 0.6 iota_add_fusion.3
  40.4 1.2 fusion.16
  42.1 0.6 iota_add_fusion.3
  42.8 1.2 fusion.16
  44.5 0.6 iota_add_fusion.3
  45.2 1.2 fusion.16
  46.4 0.6 copy-done.1
  47.2 2.2 %scatter_custom_fusion = f32[7168]{0:T(1024)S(1)} fusion(s32[256]{0:T(256)S(1)} %reshape.145, f32[256]{0:T(256)S(1)} %reshape.147, f32[]{:T(128)} %constant.16.clone.1), kind=kCustom, calls=%fused_computation.14 | custom fusion | flops 256 | bytes 28676 | tf_op jit(solution)/shard_map/scatter-add | solution.py:26
  49.4 17.8 %psum.15 = f32[7168]{0:T(1024)S(1)} all-reduce(f32[7168]{0:T(1024)S(1)} %scatter_custom_fusion), channel_id=1, replica_groups=mesh['grp'=4,'mem'=8] {'grp'}, use_global_device_ids=true, to_apply=%region_4.5 | all-reduce | flops 7168 | bytes 57344 | tf_op jit(solution)/shard_map/psum | solution.py:46
  67.2 74.4 %all-reduce.2.cloned.1.call-done = f32[7168,128]{1,0:T(8,128)} async-done(((f32[7168,128]{1,0:T(8,128)}), f32[7168,128]{1,0:T(8,128)}) %all-reduce.2.cloned.1.call-update) | async-done | bytes 3670032 | tf_op jit(solution)/shard_map/psum | solution.py:46
  141.6 5.7 %broadcast_divide_fusion = f32[7168,128]{1,0:T(8,128)} fusion(f32[7168,128]{1,0:T(8,128)} %all-reduce.2.cloned.1.call-done, f32[7168]{0:T(1024)S(1)} %broadcast_maximum_fusion), kind=kLoop, calls=%fused_computation.8 | loop fusion | flops 917504 | bytes 7368704 | tf_op jit(solution)/shard_map/div | solution.py:48
  147.3 2.8 %gather_fusion = bf16[256,128]{1,0:T(8,128)(2,1)S(1)} fusion(f32[7168,128]{1,0:T(8,128)} %broadcast_divide_fusion, s32[1024]{0:T(1024)S(1)} %pad_clamp_fusion), kind=kCustom, calls=%fused_computation | custom fusion | bytes 132096 | tf_op jit(solution)/shard_map/jit(_take)/gather | solution.py:49
  150.2 10.3 %all_to_all.19 = bf16[8,32,128]{2,1,0:T(8,128)(2,1)S(1)} all-to-all(bf16[8,32,128]{2,1,0:T(8,128)(2,1)S(1)} %select_convert_fusion), channel_id=1, replica_groups=mesh['grp'=4,'mem'=8] {'mem'}, dimensions={0} | all-to-all | bytes 131072 | tf_op jit(solution)/shard_map/all_to_all | solution.py:52
  160.5 0.6 copy.16
  (21 shorter events, 3.4 us)
Async XLA Ops:
  8.5 11.9 %all-to-all-start = ((s32[8,1,32]{2,1,0:T(1,128)}), s32[8,1,32]{2,1,0:T(1,128)S(1)}, u32[]{:S(2)}, u32[]{:S(2)}) async-start(s32[8,1,32]{2,1,0:T(1,128)} %compare_select_fusion), calls=%async_computation | async-start | bytes 8192 | tf_op jit(solution)/shard_map/all_to_all | solution.py:39
  20.4 9.2 %copy-start = (s32[8,1,32]{2,1,0:T(1,128)}, s32[8,1,32]{2,1,0:T(1,128)S(1)}, u32[]{:S(2)}) copy-start(s32[8,1,32]{2,1,0:T(1,128)S(1)} %all-to-all-done) | copy-start | bytes 3076
  20.4 9.2 %all-to-all-start.1 = ((bf16[8,32,128]{2,1,0:T(8,128)(2,1)}), bf16[8,32,128]{2,1,0:T(8,128)(2,1)S(1)}, u32[]{:S(2)}, u32[]{:S(2)}) async-start(bf16[8,32,128]{2,1,0:T(8,128)(2,1)} %bitcast_select_fusion), calls=%async_computation.1 | async-start | bytes 131072 | tf_op jit(solution)/shard_map/all_to_all | solution.py:38
  23.8 117.8 %all-reduce.2.cloned.1.call-start = ((), (), s32[]{:S(2)}) async-start(), calls=%async_computation.3 | async-start | bytes 7340032 | tf_op jit(solution)/shard_map/psum | solution.py:46
  46.3 0.7 copy-start.1
Sparse Core Ops, SparseCore 0:
  46.5 95.0 all-reduce.1
where the time goes:
time: 169 us; the launch traced here: 168 us
  waiting for transfers between devices  83.3 us (49%)
  blocking collectives  28.1 us (17%)
  other arithmetic  16.3 us (10%)
  between operations  14.1 us (8%)
  starting transfers between devices  9.75 us (6%)
  local copies, waits for them, and re-layouts  8.35 us (5%)
  matrix products  8.07 us (5%)
    psum x1, waiting for transfers between devices, per_device(): reduced = lax.psum(payload, 'grp')  74.4 us
    psum x1, blocking collectives, per_device(): reduced = lax.psum(payload, 'grp')  17.8 us
    all_to_all x1, blocking collectives, per_device(): lax.all_to_all(back_rows, 'mem', split_axis=0, concat_axis=0, tiled=True)  10.3 us
    dot_general x7, matrix products, one_tile(): return jnp.dot(onehot, rows_in, preferred_element_type=jnp.float32)  8.07 us
    all_to_all x1, starting transfers between devices, per_device(): lax.all_to_all(send_slots, 'mem', split_axis=0, concat_axis=0, tiled=True)  6.35 us
    div x1, other arithmetic, per_device(): averaged = reduced[0] / jnp.maximum(total_count, 1.0)[:, None]  5.72 us
    all_to_all x1, waiting for transfers between devices, per_device(): lax.all_to_all(send_blocks, 'mem', split_axis=0, concat_axis=0, tiled=True)  5.7 us
    add x7, other arithmetic, one_tile(): wanted = first + lax.broadcasted_iota(jnp.int32, (tile, 1), 0)  4.53 us
  transfers between devices with their start and end apart: 3, of which 3 were waited for; matrix products, arithmetic and copies ran while one was open for 3% of the time, Pallas kernels for 0%

commit v1 on v0

v1 whole, which is shorter than its diff:
```python
import functools
import math

import jax
import jax.numpy as jnp
from jax import lax
from jax.experimental import pallas as pl
from jax.experimental.pallas import tpu as pltpu
from jax.sharding import PartitionSpec as P

BUCKET = 7168
LANES = 128
META = 8


def vmem_spec():
    return pl.BlockSpec(memory_space=pltpu.VMEM)


def pack_kernel(groups, values_ref, slots_ref, counts_ref, out_ref):
    members, capacity, lanes = values_ref.shape
    shape = (members, members)
    diagonal = lax.broadcasted_iota(jnp.int32, shape, 0) == lax.broadcasted_iota(jnp.int32, shape, 1)
    count = jnp.sum(jnp.where(diagonal, counts_ref[...].astype(jnp.float32), 0.0), axis=1, keepdims=True)
    slot = slots_ref[...]
    place = lax.broadcasted_iota(jnp.int32, slot.shape, 1).astype(jnp.float32)
    live = place < count
    high = jnp.where(live, (slot // LANES).astype(jnp.float32), -1.0)
    low = jnp.where(live, (slot % LANES).astype(jnp.float32), 0.0)
    repeats = lanes // capacity
    high = jnp.concatenate([high] * repeats, axis=1)
    low = jnp.concatenate([low] * repeats, axis=1)
    row = lax.broadcasted_iota(jnp.int32, (members, META, lanes), 1)
    meta = jnp.where(row == 0, high[:, None, :], jnp.where(row == 1, low[:, None, :], 0.0))
    meta = meta.astype(jnp.bfloat16)
    for group in range(groups):
        rows = pl.ds(group * members, members)
        out_ref[rows, pl.ds(0, capacity), :] = values_ref[...]
        out_ref[rows, pl.ds(capacity, META), :] = meta


def pack(values, slots, counts, groups):
    members, capacity, lanes = values.shape
    return pl.pallas_call(
        functools.partial(pack_kernel, groups),
        out_shape=jax.ShapeDtypeStruct((groups * members, capacity + META, lanes), jnp.bfloat16),
        in_specs=[vmem_spec()] * 3,
        out_specs=vmem_spec(),
        name="pack",
    )(values, slots, counts)


def slots_of(lists_ref, first, senders, capacity):
    meta = lists_ref[pl.ds(first, senders), pl.ds(capacity, META), :].astype(jnp.float32)
    return meta[:, 0, :] * LANES + meta[:, 1, :]


def load_entries(lists_ref, rhs_ref, key_ref):
    senders, rows, lanes = lists_ref.shape
    capacity = rows - META
    slot = slots_of(lists_ref, 0, senders, capacity)
    per_block = lanes // capacity
    part = lax.broadcasted_iota(jnp.int32, (1, lanes), 1) // capacity
    for block in range(senders // per_block):
        key = slot[block * per_block : block * per_block + 1]
        for k in range(1, per_block):
            at = block * per_block + k
            key = jnp.where(part == k, slot[at : at + 1], key)
        key_ref[:, block * lanes : (block + 1) * lanes] = key
    rhs_ref[:, :lanes] = lists_ref[:, pl.ds(0, capacity), :].reshape(senders * capacity, lanes)
    rhs_ref[:, lanes:] = jnp.ones((senders * capacity, lanes), jnp.bfloat16)


def average(wanted, key_ref, rhs_ref):
    lanes = rhs_ref.shape[1] // 2
    onehot = (wanted == key_ref[...]).astype(jnp.float32).astype(jnp.bfloat16)
    both = jnp.dot(onehot, rhs_ref[...], preferred_element_type=jnp.float32)
    return both[:, :lanes] / jnp.maximum(both[:, lanes:], 1.0)


def answer_kernel(axis, step, lists_ref, out_ref, rhs_ref, key_ref):
    senders, rows, lanes = lists_ref.shape
    capacity = rows - META

    @pl.when(pl.program_id(0) == 0)
    def _():
        load_entries(lists_ref, rhs_ref, key_ref)

    members = step * pl.num_programs(0)
    first = lax.axis_index(axis) * members + pl.program_id(0) * step
    slot = slots_of(lists_ref, first, step, capacity)
    shape = (step, capacity, lanes)
    here = lax.broadcasted_iota(jnp.int32, shape, 2) == lax.broadcasted_iota(jnp.int32, shape, 1)
    column = jnp.sum(jnp.where(here, slot[:, None, :], 0.0), axis=2, keepdims=True)
    column = jnp.where(column < 0.0, -1.0, column).reshape(step * capacity, 1)
    out_ref[...] = average(column, key_ref, rhs_ref).astype(jnp.bfloat16).reshape(out_ref.shape)


def answer(lists, members, axis):
    senders, rows, lanes = lists.shape
    capacity = rows - META
    entries = senders * capacity
    step = math.gcd(members, 8)
    return pl.pallas_call(
        functools.partial(answer_kernel, axis, step),
        grid=(members // step,),
        out_shape=jax.ShapeDtypeStruct((members, capacity, lanes), jnp.bfloat16),
        in_specs=[vmem_spec()],
        out_specs=pl.BlockSpec((step, capacity, lanes), lambda i: (i, 0, 0)),
        scratch_shapes=[pltpu.VMEM((entries, 2 * lanes), jnp.bfloat16), pltpu.VMEM((1, entries), jnp.float32)],
        name="answer",
    )(lists)


def dense_kernel(lists_ref, out_ref, rhs_ref, key_ref):
    @pl.when(pl.program_id(0) == 0)
    def _():
        load_entries(lists_ref, rhs_ref, key_ref)

    tile = out_ref.shape[0]
    wanted = (lax.broadcasted_iota(jnp.int32, (tile, 1), 0) + pl.program_id(0) * tile).astype(jnp.float32)
    out_ref[...] = average(wanted, key_ref, rhs_ref)


def dense(lists):
    senders, rows, lanes = lists.shape
    capacity = rows - META
    entries = senders * capacity
    tile = math.gcd(BUCKET, 512)
    return pl.pallas_call(
        dense_kernel,
        grid=(BUCKET // tile,),
        out_shape=jax.ShapeDtypeStruct((BUCKET, lanes), jnp.float32),
        in_specs=[vmem_spec()],
        out_specs=pl.BlockSpec((tile, lanes), lambda i: (i, 0)),
        scratch_shapes=[pltpu.VMEM((entries, 2 * lanes), jnp.bfloat16), pltpu.VMEM((1, entries), jnp.float32)],
        cost_estimate=pl.CostEstimate(flops=4 * BUCKET * entries * lanes, bytes_accessed=4 * BUCKET * lanes, transcendentals=0),
        name="dense",
    )(lists)


def per_device(groups, values, slots, counts):
    members = values.shape[1]
    lists = pack(values[0], slots[0], counts, groups)
    got = lax.all_to_all(lists, ("grp", "mem"), split_axis=0, concat_axis=0, tiled=True)
    back = answer(got, members, "grp")
    returned = lax.all_to_all(back, "mem", split_axis=0, concat_axis=0, tiled=True)
    averaged = dense(got)
    return (averaged, returned[None])


def solution(mesh):
    return jax.shard_map(
        functools.partial(per_device, mesh.shape["grp"]),
        mesh=mesh,
        in_specs=(
            P(("grp", "mem"), None, None, None),
            P(("grp", "mem"), None, None),
            P(("grp", "mem"), None),
        ),
        out_specs=(P("mem", None), P(("grp", "mem"), None, None, None)),
        check_vma=False,
    )
```

time: 169 us -> 37.9 us (0.22)
  waiting for transfers between devices: 83.3 us -> 0.01 us
  other arithmetic: 16.3 us -> 0 us
  between operations: 14.1 us -> 0.64 us
  Pallas kernels: 0 us -> 13.4 us
  blocking collectives: 28.1 us -> 19.5 us
  matrix products: 8.07 us -> 0 us
  local copies, waits for them, and re-layouts: 8.35 us -> 0.63 us
  starting transfers between devices: 9.75 us -> 3.35 us
    psum x1 -> x0, waiting for transfers between devices: 74.4 us -> none  [per_device(): reduced = lax.psum(payload, 'grp')]
    psum x1 -> x0, blocking collectives: 17.8 us -> none  [per_device(): reduced = lax.psum(payload, 'grp')]
    pallas_call x0 -> x3, Pallas kernels: none -> 13.4 us  [the longest x1 9.6 us: dense(): pl.pallas_call(dense_kernel, grid=(BUCKET // tile,), out_shape=jax.ShapeD...]
    all_to_all x1, blocking collectives: 10.3 us -> 19.5 us  [per_device(): lax.all_to_all(lists, ('grp', 'mem'), split_axis=0, concat_axis=0, tiled=...]
    all_to_all x2 -> x1, waiting for transfers between devices: 8.91 us -> 0.01 us  [per_device(): lax.all_to_all(back, 'mem', split_axis=0, concat_axis=0, tiled=True)]
    dot_general x7 -> x0, matrix products: 8.07 us -> none  [one_tile(): return jnp.dot(onehot, rows_in, preferred_element_type=jnp.float32)]
    all_to_all x2 -> x1, starting transfers between devices: 9.71 us -> 3.35 us  [per_device(): lax.all_to_all(back, 'mem', split_axis=0, concat_axis=0, tiled=True)]
    div x1 -> x0, other arithmetic: 5.72 us -> none  [per_device(): averaged = reduced[0] / jnp.maximum(total_count, 1.0)[:, None]]
  transfers between devices with their start and end apart: 3 -> 1, of which waited for: 3 -> 0; matrix products, arithmetic and copies ran while one was open for 3% -> 0% of each run, Pallas kernels for 0% -> 26%
where the time goes in v1:
time: 37.9 us; the launch traced here: 37.5 us
  blocking collectives  19.5 us (51%)
  Pallas kernels  13.4 us (35%)
  starting transfers between devices  3.35 us (9%)
  between operations  0.64 us (2%)
  local copies, waits for them, and re-layouts  0.63 us (2%)
    all_to_all x1, blocking collectives, per_device(): lax.all_to_all(lists, ('grp', 'mem'), split_axis=0, concat_axis=0, tiled=...  19.5 us
    pallas_call x1, Pallas kernels, dense(): pl.pallas_call(dense_kernel, grid=(BUCKET // tile,), out_shape=jax.ShapeD...  9.6 us
    all_to_all x1, starting transfers between devices, per_device(): lax.all_to_all(back, 'mem', split_axis=0, concat_axis=0, tiled=True)  3.35 us
    pallas_call x1, Pallas kernels, answer(): pl.pallas_call(functools.partial(answer_kernel, axis, step), grid=(member...  2.07 us
    pallas_call x1, Pallas kernels, pack(): pl.pallas_call(functools.partial(pack_kernel, groups), out_shape=jax.Shap...  1.75 us
  transfers between devices with their start and end apart: 1, of which 0 were waited for; matrix products, arithmetic and copies ran while one was open for 0% of the time, Pallas kernels for 26%

profile of v1, /device:TPU:0, one launch (start us, length us, event | category | flops | bytes accessed | tf_op | source)
XLA Modules:
  0.0 37.5 jit_solution(1716575891926150428)
XLA Ops:
  0.6 1.8 %pack.1 = bf16[32,40,128]{2,1,0:T(8,128)(2,1)} custom-call(bf16[8,32,128]{2,1,0:T(8,128)(2,1)} %bitcast.4, s32[8,32]{1,0:T(8,128)} %bitcast.5, s32[1,8]{1,0:T(1,128)} %counts_ref.1), custom_call_target="tpu_custom_call" | custom-call | tf_op jit(solution)/shard_map/pack/pallas_call | solution.py:44
  2.4 19.5 %all_to_all.10.lists_ref = bf16[32,40,128]{2,1,0:T(8,128)(2,1)} all-to-all(bf16[32,40,128]{2,1,0:T(8,128)(2,1)} %pack.1), channel_id=1, replica_groups=mesh['grp'=4,'mem'=8] {'grp','mem'}, dimensions={0} | all-to-all | bytes 655360 | tf_op jit(solution)/shard_map/all_to_all | solution.py:145
  21.8 2.1 %answer.1 = bf16[8,32,128]{2,1,0:T(8,128)(2,1)} custom-call(bf16[32,40,128]{2,1,0:T(8,128)(2,1)} %all_to_all.10.lists_ref), custom_call_target="tpu_custom_call" | custom-call | tf_op jit(solution)/shard_map/answer/pallas_call | solution.py:104
  23.9 3.4 %all-to-all-start.1 = ((bf16[8,32,128]{2,1,0:T(8,128)(2,1)}), bf16[8,32,128]{2,1,0:T(8,128)(2,1)S(1)}, u32[]{:S(2)}, u32[]{:S(2)}) async-start(bf16[8,32,128]{2,1,0:T(8,128)(2,1)} %answer.1), calls=%async_computation.1 | async-start | bytes 131072 | tf_op jit(solution)/shard_map/all_to_all | solution.py:147
  27.3 9.6 %dense.1 = f32[7168,128]{1,0:T(8,128)} custom-call(bf16[32,40,128]{2,1,0:T(8,128)(2,1)} %all_to_all.10.lists_ref), custom_call_target="tpu_custom_call" | custom-call | flops 3758096384 | bytes 3670016 | tf_op jit(solution)/shard_map/dense/pallas_call | solution.py:130
  36.9 0.0 all-to-all-done.1
  36.9 0.6 %copy.6 = bf16[1,8,32,128]{3,2,1,0:T(8,128)(2,1)} copy(bf16[1,8,32,128]{3,2,1,0:T(8,128)(2,1)S(1)} %bitcast.3) | data formatting | bytes 131072
Async XLA Ops:
  23.9 13.0 %all-to-all-start.1 = ((bf16[8,32,128]{2,1,0:T(8,128)(2,1)}), bf16[8,32,128]{2,1,0:T(8,128)(2,1)S(1)}, u32[]{:S(2)}, u32[]{:S(2)}) async-start(bf16[8,32,128]{2,1,0:T(8,128)(2,1)} %answer.1), calls=%async_computation.1 | async-start | bytes 131072 | tf_op jit(solution)/shard_map/all_to_all | solution.py:147

commit v2 on v1

--- a/solution.py
+++ b/solution.py
@@ -9,12 +9,16 @@
 from jax.sharding import PartitionSpec as P
 
 BUCKET = 7168
-LANES = 128
+DIGIT = 256
 META = 8
 
 
 def vmem_spec():
     return pl.BlockSpec(memory_space=pltpu.VMEM)
+
+
+def grant(size):
+    return pltpu.CompilerParams(vmem_limit_bytes=size)
 
 
 def pack_kernel(groups, values_ref, slots_ref, counts_ref, out_ref):
@@ -25,8 +29,8 @@
     slot = slots_ref[...]
     place = lax.broadcasted_iota(jnp.int32, slot.shape, 1).astype(jnp.float32)
     live = place < count
-    high = jnp.where(live, (slot // LANES).astype(jnp.float32), -1.0)
-    low = jnp.where(live, (slot % LANES).astype(jnp.float32), 0.0)
+    high = jnp.where(live, (slot // DIGIT).astype(jnp.float32), -1.0)
+    low = jnp.where(live, (slot % DIGIT).astype(jnp.float32), 0.0)
     repeats = lanes // capacity
     high = jnp.concatenate([high] * repeats, axis=1)
     low = jnp.concatenate([low] * repeats, axis=1)
@@ -46,27 +50,49 @@
         out_shape=jax.ShapeDtypeStruct((groups * members, capacity + META, lanes), jnp.bfloat16),
         in_specs=[vmem_spec()] * 3,
         out_specs=vmem_spec(),
+        compiler_params=grant(8 * 2**20),
         name="pack",
     )(values, slots, counts)
 
 
-def slots_of(lists_ref, first, senders, capacity):
+def digits_of(lists_ref, first, senders):
+    capacity = lists_ref.shape[1] - META
     meta = lists_ref[pl.ds(first, senders), pl.ds(capacity, META), :].astype(jnp.float32)
-    return meta[:, 0, :] * LANES + meta[:, 1, :]
-
-
-def load_entries(lists_ref, rhs_ref, key_ref):
-    senders, rows, lanes = lists_ref.shape
-    capacity = rows - META
-    slot = slots_of(lists_ref, 0, senders, capacity)
+    return meta[:, 0, :], meta[:, 1, :]
+
+
+def as_row(digit, capacity):
+    senders, lanes = digit.shape
     per_block = lanes // capacity
     part = lax.broadcasted_iota(jnp.int32, (1, lanes), 1) // capacity
+    blocks = []
     for block in range(senders // per_block):
-        key = slot[block * per_block : block * per_block + 1]
+        row = digit[block * per_block : block * per_block + 1]
         for k in range(1, per_block):
             at = block * per_block + k
-            key = jnp.where(part == k, slot[at : at + 1], key)
-        key_ref[:, block * lanes : (block + 1) * lanes] = key
+            row = jnp.where(part == k, digit[at : at + 1], row)
+        blocks.append(row)
+    return jnp.concatenate(blocks, axis=1)
+
+
+def as_column(digit, capacity):
+    senders, lanes = digit.shape
+    shape = (senders, capacity, lanes)
+    here = lax.broadcasted_iota(jnp.int32, shape, 2) == lax.broadcasted_iota(jnp.int32, shape, 1)
+    picked = jnp.where(here, digit[:, None, :], 0.0).astype(jnp.bfloat16).reshape(senders * capacity, lanes)
+    return jnp.dot(picked, jnp.ones((lanes, lanes), jnp.bfloat16), preferred_element_type=jnp.float32)
+
+
+def load_keys(lists_ref, key_ref):
+    senders, rows, lanes = lists_ref.shape
+    high, low = digits_of(lists_ref, 0, senders)
+    key_ref[...] = as_row(high * DIGIT + low, rows - META)
+
+
+def load_entries(lists_ref, rhs_ref, key_ref):
+    senders, rows, lanes = lists_ref.shape
+    capacity = rows - META
+    load_keys(lists_ref, key_ref)
     rhs_ref[:, :lanes] = lists_ref[:, pl.ds(0, capacity), :].reshape(senders * capacity, lanes)
     rhs_ref[:, lanes:] = jnp.ones((senders * capacity, lanes), jnp.bfloat16)
 
@@ -78,22 +104,31 @@
     return both[:, :lanes] / jnp.maximum(both[:, lanes:], 1.0)
 
 
-def answer_kernel(axis, step, lists_ref, out_ref, rhs_ref, key_ref):
+def answer_kernel(axis, step, lists_ref, out_ref, key_ref):
     senders, rows, lanes = lists_ref.shape
     capacity = rows - META
 
     @pl.when(pl.program_id(0) == 0)
     def _():
-        load_entries(lists_ref, rhs_ref, key_ref)
+        load_keys(lists_ref, key_ref)
 
     members = step * pl.num_programs(0)
     first = lax.axis_index(axis) * members + pl.program_id(0) * step
-    slot = slots_of(lists_ref, first, step, capacity)
-    shape = (step, capacity, lanes)
-    here = lax.broadcasted_iota(jnp.int32, shape, 2) == lax.broadcasted_iota(jnp.int32, shape, 1)
-    column = jnp.sum(jnp.where(here, slot[:, None, :], 0.0), axis=2, keepdims=True)
-    column = jnp.where(column < 0.0, -1.0, column).reshape(step * capacity, 1)
-    out_ref[...] = average(column, key_ref, rhs_ref).astype(jnp.bfloat16).reshape(out_ref.shape)
+    high, low = digits_of(lists_ref, first, step)
+    column = as_column(high, capacity) * DIGIT + as_column(low, capacity)
+    column = jnp.where(column < 0.0, -1.0, column)
+    onehot = jnp.concatenate(
+        [
+            (column == key_ref[:, at : at + lanes]).astype(jnp.float32).astype(jnp.bfloat16)
+            for at in range(0, senders * capacity, lanes)
+        ],
+        axis=1,
+    )
+    entries = lists_ref[:, pl.ds(0, capacity), :].reshape(senders * capacity, lanes)
+    sums = jnp.dot(onehot, entries, preferred_element_type=jnp.float32)
+    count = jnp.dot(onehot, jnp.ones_like(entries), preferred_element_type=jnp.float32)
+    mean = sums / jnp.maximum(count, 1.0)
+    out_ref[...] = mean.astype(jnp.bfloat16).reshape(out_ref.shape)
 
 
 def answer(lists, members, axis):
@@ -107,7 +142,8 @@
         out_shape=jax.ShapeDtypeStruct((members, capacity, lanes), jnp.bfloat16),
         in_specs=[vmem_spec()],
         out_specs=pl.BlockSpec((step, capacity, lanes), lambda i: (i, 0, 0)),
-        scratch_shapes=[pltpu.VMEM((entries, 2 * lanes), jnp.bfloat16), pltpu.VMEM((1, entries), jnp.float32)],
+        scratch_shapes=[pltpu.VMEM((1, entries), jnp.float32)],
+        compiler_params=grant(48 * entries * lanes),
         name="answer",
     )(lists)
 
@@ -122,10 +158,71 @@
     out_ref[...] = average(wanted, key_ref, rhs_ref)
 
 
+def dense_whole_kernel(lists_ref, out_ref, same_ref, high_ref, mean_ref, sems):
+    senders, rows, lanes = lists_ref.shape
+    capacity = rows - META
+    entries = senders * capacity
+    high, low = digits_of(lists_ref, 0, senders)
+    low_row = as_row(low, capacity)
+    wanted = lax.broadcasted_iota(jnp.int32, (DIGIT, lanes), 0).astype(jnp.float32)
+    for at in range(0, entries, lanes):
+        same = (wanted == low_row[:, at : at + lanes]).astype(jnp.float32)
+        same_ref[:, at : at + lanes] = same.astype(jnp.bfloat16)
+    high_column = as_column(high, capacity)
+    high_ref[...] = high_column.astype(jnp.bfloat16)
+    lane = lax.broadcasted_iota(jnp.int32, (entries, lanes), 1).astype(jnp.float32)
+    in_tile = (high_column == lane).astype(jnp.float32).astype(jnp.bfloat16)
+    count = jnp.dot(same_ref[...], in_tile, preferred_element_type=jnp.float32)
+    inverse = 1.0 / jnp.maximum(count, 1.0)
+    copies = []
+    for pair in range(BUCKET // (2 * DIGIT)):
+        values = lists_ref[:, pl.ds(0, capacity), :].reshape(entries, lanes)
+        tile_of = high_ref[...]
+        zero = jnp.zeros_like(values)
+        picked = jnp.concatenate([jnp.where(tile_of == 2 * pair + k, values, zero) for k in range(2)], axis=1)
+        sums = jnp.dot(same_ref[...], picked, preferred_element_type=jnp.float32)
+        for k in range(2):
+            tile = 2 * pair + k
+            where = pl.ds(tile * DIGIT, DIGIT)
+            mean_ref[where, :] = sums[:, k * lanes : (k + 1) * lanes] * inverse[:, tile : tile + 1]
+        where = pl.ds(2 * pair * DIGIT, 2 * DIGIT)
+        copy = pltpu.make_async_copy(mean_ref.at[where], out_ref.at[where], sems.at[pair])
+        copy.start()
+        copies.append(copy)
+    for copy in copies:
+        copy.wait()
+
+
+def dense_whole(lists):
+    senders, rows, lanes = lists.shape
+    entries = senders * (rows - META)
+    return pl.pallas_call(
+        dense_whole_kernel,
+        out_shape=jax.ShapeDtypeStruct((BUCKET, lanes), jnp.float32),
+        in_specs=[vmem_spec()],
+        out_specs=pl.BlockSpec(memory_space=pltpu.HBM),
+        scratch_shapes=[
+            pltpu.VMEM((DIGIT, entries), jnp.bfloat16),
+            pltpu.VMEM((entries, lanes), jnp.bfloat16),
+            pltpu.VMEM((BUCKET, lanes), jnp.float32),
+            pltpu.SemaphoreType.DMA((BUCKET // (2 * DIGIT),)),
+        ],
+        cost_estimate=dense_cost(entries, lanes),
+        compiler_params=grant(16 * 2**20),
+        name="dense_whole",
+    )(lists)
+
+
+def dense_cost(entries, lanes):
+    return pl.CostEstimate(flops=2 * BUCKET * entries * lanes, bytes_accessed=4 * BUCKET * lanes, transcendentals=0)
+
+
 def dense(lists):
     senders, rows, lanes = lists.shape
     capacity = rows - META
     entries = senders * capacity
+    if entries <= 1024 and BUCKET % (2 * DIGIT) == 0 and BUCKET // DIGIT <= lanes:
+        return dense_whole(lists)
     tile = math.gcd(BUCKET, 512)
     return pl.pallas_call(
         dense_kernel,
@@ -134,7 +231,7 @@
         in_specs=[vmem_spec()],
         out_specs=pl.BlockSpec((tile, lanes), lambda i: (i, 0)),
         scratch_shapes=[pltpu.VMEM((entries, 2 * lanes), jnp.bfloat16), pltpu.VMEM((1, entries), jnp.float32)],
-        cost_estimate=pl.CostEstimate(flops=4 * BUCKET * entries * lanes, bytes_accessed=4 * BUCKET * lanes, transcendentals=0),
+        cost_estimate=dense_cost(entries, lanes),
         name="dense",
     )(lists)
 

time: 37.9 us -> 33.6 us (0.89)
  Pallas kernels: 13.4 us -> 5.64 us
  local copies, waits for them, and re-layouts: 0.63 us -> 2.8 us
  waiting for transfers between devices: 0.01 us -> 1.65 us
    pallas_call x1, Pallas kernels: 9.6 us -> 4.19 us  [dense_whole(): pl.pallas_call(dense_whole_kernel, out_shape=jax.ShapeDtypeStruct((BUCKET...]
    unnamed x1 -> x7, local copies, waits for them, and re-layouts: 0.63 us -> 2.8 us
    all_to_all x1, waiting for transfers between devices: 0.01 us -> 1.65 us  [per_device(): lax.all_to_all(back, 'mem', split_axis=0, concat_axis=0, tiled=True)]
    pallas_call x1, Pallas kernels: 1.75 us -> 0.17 us  [pack(): pl.pallas_call(functools.partial(pack_kernel, groups), out_shape=jax.Shap...]
    pallas_call x1, Pallas kernels: 2.07 us -> 1.28 us  [answer(): pl.pallas_call(functools.partial(answer_kernel, axis, step), grid=(member...]
  transfers between devices with their start and end apart: 1 -> 1, of which waited for: 0 -> 1; matrix products, arithmetic and copies ran while one was open for 0% -> 0% of each run, Pallas kernels for 26% -> 13%
where the time goes in v2:
time: 33.6 us; the launch traced here: 33.3 us
  blocking collectives  19.2 us (57%)
  Pallas kernels  5.64 us (17%)
  starting transfers between devices  3.35 us (10%)
  local copies, waits for them, and re-layouts  2.8 us (8%)
  waiting for transfers between devices  1.65 us (5%)
  between operations  0.67 us (2%)
    all_to_all x1, blocking collectives, per_device(): lax.all_to_all(lists, ('grp', 'mem'), split_axis=0, concat_axis=0, tiled=...  19.2 us
    pallas_call x1, Pallas kernels, dense_whole(): pl.pallas_call(dense_whole_kernel, out_shape=jax.ShapeDtypeStruct((BUCKET...  4.19 us
    all_to_all x1, starting transfers between devices, per_device(): lax.all_to_all(back, 'mem', split_axis=0, concat_axis=0, tiled=True)  3.35 us
    unnamed x7, local copies, waits for them, and re-layouts  2.8 us
    all_to_all x1, waiting for transfers between devices, per_device(): lax.all_to_all(back, 'mem', split_axis=0, concat_axis=0, tiled=True)  1.65 us
    pallas_call x1, Pallas kernels, answer(): pl.pallas_call(functools.partial(answer_kernel, axis, step), grid=(member...  1.28 us
  transfers between devices with their start and end apart: 1, of which 1 were waited for; matrix products, arithmetic and copies ran while one was open for 0% of the time, Pallas kernels for 13%

profile of v2, /device:TPU:0, one launch (start us, length us, event | category | flops | bytes accessed | tf_op | source)
XLA Modules:
  0.0 33.3 jit_solution(12924664765318391873)
XLA Ops:
  0.6 0.0 copy-start
  0.6 0.8 %copy-done = bf16[1,8,32,128]{3,2,1,0:T(8,128)(2,1)S(1)} copy-done((bf16[1,8,32,128]{3,2,1,0:T(8,128)(2,1)S(1)}, bf16[1,8,32,128]{3,2,1,0:T(8,128)(2,1)}, u32[]{:S(2)}) %copy-start) | copy-done | bytes 65560
  1.5 0.0 copy-start.1
  1.5 0.7 %copy-done.1 = s32[1,8,32]{2,1,0:T(8,128)S(1)} copy-done((s32[1,8,32]{2,1,0:T(8,128)S(1)}, s32[1,8,32]{2,1,0:T(8,128)}, u32[]{:S(2)}) %copy-start.1) | copy-done | bytes 1048
  2.2 0.0 copy-start.2
  2.2 0.7 %copy-done.2 = s32[1,8]{1,0:T(1,128)S(1)} copy-done((s32[1,8]{1,0:T(1,128)S(1)}, s32[1,8]{1,0:T(1,128)}, u32[]{:S(2)}) %copy-start.2) | copy-done | bytes 56
  2.8 0.2 pack.1
  3.0 19.2 %all_to_all.10.lists_ref = bf16[32,40,128]{2,1,0:T(8,128)(2,1)S(1)} all-to-all(bf16[32,40,128]{2,1,0:T(8,128)(2,1)S(1)} %pack.1), channel_id=1, replica_groups=mesh['grp'=4,'mem'=8] {'grp','mem'}, dimensions={0} | all-to-all | bytes 655360 | tf_op jit(solution)/shard_map/all_to_all | solution.py:242
  22.1 1.3 %answer.1 = bf16[8,32,128]{2,1,0:T(8,128)(2,1)} custom-call(bf16[32,40,128]{2,1,0:T(8,128)(2,1)S(1)} %all_to_all.10.lists_ref), custom_call_target="tpu_custom_call" | custom-call | tf_op jit(solution)/shard_map/answer/pallas_call | solution.py:139
  23.4 3.4 %all-to-all-start.1 = ((bf16[8,32,128]{2,1,0:T(8,128)(2,1)}), bf16[8,32,128]{2,1,0:T(8,128)(2,1)S(1)}, u32[]{:S(2)}, u32[]{:S(2)}) async-start(bf16[8,32,128]{2,1,0:T(8,128)(2,1)} %answer.1), calls=%async_computation.1 | async-start | bytes 131072 | tf_op jit(solution)/shard_map/all_to_all | solution.py:244
  26.8 4.2 %dense_whole.1 = f32[7168,128]{1,0:T(8,128)} custom-call(bf16[32,40,128]{2,1,0:T(8,128)(2,1)S(1)} %all_to_all.10.lists_ref), custom_call_target="tpu_custom_call" | custom-call | flops 1879048192 | bytes 3670016 | tf_op jit(solution)/shard_map/dense_whole/pallas_call | solution.py:199
  31.0 1.7 %all-to-all-done.1 = bf16[8,32,128]{2,1,0:T(8,128)(2,1)S(1)} async-done(((bf16[8,32,128]{2,1,0:T(8,128)(2,1)}), bf16[8,32,128]{2,1,0:T(8,128)(2,1)S(1)}, u32[]{:S(2)}, u32[]{:S(2)}) %all-to-all-start.1) | async-done | bytes 65568 | tf_op jit(solution)/shard_map/all_to_all | solution.py:244
  32.6 0.6 %copy.6 = bf16[1,8,32,128]{3,2,1,0:T(8,128)(2,1)} copy(bf16[1,8,32,128]{3,2,1,0:T(8,128)(2,1)S(1)} %bitcast.5) | data formatting | bytes 131072
Async XLA Ops:
  0.6 0.8 %copy-start = (bf16[1,8,32,128]{3,2,1,0:T(8,128)(2,1)S(1)}, bf16[1,8,32,128]{3,2,1,0:T(8,128)(2,1)}, u32[]{:S(2)}) copy-start(bf16[1,8,32,128]{3,2,1,0:T(8,128)(2,1)} %param.3) | copy-start | bytes 196612
  1.5 0.7 %copy-start.1 = (s32[1,8,32]{2,1,0:T(8,128)S(1)}, s32[1,8,32]{2,1,0:T(8,128)}, u32[]{:S(2)}) copy-start(s32[1,8,32]{2,1,0:T(8,128)} %param.4) | copy-start | bytes 3076
  2.2 0.7 %copy-start.2 = (s32[1,8]{1,0:T(1,128)S(1)}, s32[1,8]{1,0:T(1,128)}, u32[]{:S(2)}) copy-start(s32[1,8]{1,0:T(1,128)} %counts_ref.1) | copy-start | bytes 100
  23.4 9.2 %all-to-all-start.1 = ((bf16[8,32,128]{2,1,0:T(8,128)(2,1)}), bf16[8,32,128]{2,1,0:T(8,128)(2,1)S(1)}, u32[]{:S(2)}, u32[]{:S(2)}) async-start(bf16[8,32,128]{2,1,0:T(8,128)(2,1)} %answer.1), calls=%async_computation.1 | async-start | bytes 131072 | tf_op jit(solution)/shard_map/all_to_all | solution.py:244

commit v3 on v2

--- a/solution.py
+++ b/solution.py
@@ -17,26 +17,21 @@
     return pl.BlockSpec(memory_space=pltpu.VMEM)
 
 
+def hbm_spec():
+    return pl.BlockSpec(memory_space=pltpu.HBM)
+
+
 def grant(size):
     return pltpu.CompilerParams(vmem_limit_bytes=size)
 
 
-def pack_kernel(groups, values_ref, slots_ref, counts_ref, out_ref):
+def pack_kernel(groups, values_ref, high_ref, low_ref, out_ref):
     members, capacity, lanes = values_ref.shape
-    shape = (members, members)
-    diagonal = lax.broadcasted_iota(jnp.int32, shape, 0) == lax.broadcasted_iota(jnp.int32, shape, 1)
-    count = jnp.sum(jnp.where(diagonal, counts_ref[...].astype(jnp.float32), 0.0), axis=1, keepdims=True)
-    slot = slots_ref[...]
-    place = lax.broadcasted_iota(jnp.int32, slot.shape, 1).astype(jnp.float32)
-    live = place < count
-    high = jnp.where(live, (slot // DIGIT).astype(jnp.float32), -1.0)
-    low = jnp.where(live, (slot % DIGIT).astype(jnp.float32), 0.0)
     repeats = lanes // capacity
-    high = jnp.concatenate([high] * repeats, axis=1)
-    low = jnp.concatenate([low] * repeats, axis=1)
+    high = jnp.concatenate([high_ref[...]] * repeats, axis=1)
+    low = jnp.concatenate([low_ref[...]] * repeats, axis=1)
     row = lax.broadcasted_iota(jnp.int32, (members, META, lanes), 1)
-    meta = jnp.where(row == 0, high[:, None, :], jnp.where(row == 1, low[:, None, :], 0.0))
-    meta = meta.astype(jnp.bfloat16)
+    meta = jnp.where(row == 0, high[:, None, :], low[:, None, :]).astype(jnp.bfloat16)
     for group in range(groups):
         rows = pl.ds(group * members, members)
         out_ref[rows, pl.ds(0, capacity), :] = values_ref[...]
@@ -45,6 +40,9 @@
 
 def pack(values, slots, counts, groups):
     members, capacity, lanes = values.shape
+    live = lax.broadcasted_iota(jnp.int32, slots.shape, 1) < counts[:, None]
+    high = jnp.where(live, slots // DIGIT, -1).astype(jnp.float32)
+    low = jnp.where(live, slots % DIGIT, 0).astype(jnp.float32)
     return pl.pallas_call(
         functools.partial(pack_kernel, groups),
         out_shape=jax.ShapeDtypeStruct((groups * members, capacity + META, lanes), jnp.bfloat16),
@@ -52,7 +50,7 @@
         out_specs=vmem_spec(),
         compiler_params=grant(8 * 2**20),
         name="pack",
-    )(values, slots, counts)
+    )(values, high, low)
 
 
 def digits_of(lists_ref, first, senders):
@@ -104,23 +102,18 @@
     return both[:, :lanes] / jnp.maximum(both[:, lanes:], 1.0)
 
 
-def answer_kernel(axis, step, lists_ref, out_ref, key_ref):
+def answer_some(lists_ref, key_ref, asking):
     senders, rows, lanes = lists_ref.shape
     capacity = rows - META
-
-    @pl.when(pl.program_id(0) == 0)
-    def _():
-        load_keys(lists_ref, key_ref)
-
-    members = step * pl.num_programs(0)
-    first = lax.axis_index(axis) * members + pl.program_id(0) * step
-    high, low = digits_of(lists_ref, first, step)
+    digits = [digits_of(lists_ref, at, 1) for at in asking]
+    high = jnp.concatenate([pair[0] for pair in digits], axis=0)
+    low = jnp.concatenate([pair[1] for pair in digits], axis=0)
     column = as_column(high, capacity) * DIGIT + as_column(low, capacity)
     column = jnp.where(column < 0.0, -1.0, column)
     onehot = jnp.concatenate(
         [
-            (column == key_ref[:, at : at + lanes]).astype(jnp.float32).astype(jnp.bfloat16)
-            for at in range(0, senders * capacity, lanes)
+            (column == key_ref[:, block : block + lanes]).astype(jnp.float32).astype(jnp.bfloat16)
+            for block in range(0, senders * capacity, lanes)
         ],
         axis=1,
     )
@@ -128,24 +121,93 @@
     sums = jnp.dot(onehot, entries, preferred_element_type=jnp.float32)
     count = jnp.dot(onehot, jnp.ones_like(entries), preferred_element_type=jnp.float32)
     mean = sums / jnp.maximum(count, 1.0)
-    out_ref[...] = mean.astype(jnp.bfloat16).reshape(out_ref.shape)
-
-
-def answer(lists, members, axis):
+    return mean.astype(jnp.bfloat16).reshape(len(asking), capacity, lanes)
+
+
+def answer_kernel(lists_ref, out_ref, key_ref):
+    members = out_ref.shape[0]
+    step = math.gcd(members, 8)
+    load_keys(lists_ref, key_ref)
+    first = lax.axis_index("grp") * members
+
+    @pl.loop(0, members, step=step)
+    def _(at):
+        asking = [first + at + k for k in range(step)]
+        out_ref[pl.ds(at, step)] = answer_some(lists_ref, key_ref, asking)
+
+
+def pair_answer_kernel(lists_ref, same_ref, other_ref, key_ref):
+    pairs = same_ref.shape[0]
+    load_keys(lists_ref, key_ref)
+    first = lax.axis_index("grp") * 2 * pairs
+    me = lax.axis_index("mem")
+    half = lax.rem(me, 2)
+    pair = lax.div(me, 2)
+    order = [first + 2 * lax.rem(pair + k, pairs) for k in range(pairs)]
+    asking = [at + half for at in order] + [at + 1 - half for at in order]
+    both = answer_some(lists_ref, key_ref, asking)
+    same_ref[...] = both[:pairs]
+    other_ref[...] = both[pairs:]
+
+
+def answer(lists, members, paired):
     senders, rows, lanes = lists.shape
     capacity = rows - META
     entries = senders * capacity
-    step = math.gcd(members, 8)
-    return pl.pallas_call(
-        functools.partial(answer_kernel, axis, step),
-        grid=(members // step,),
-        out_shape=jax.ShapeDtypeStruct((members, capacity, lanes), jnp.bfloat16),
+    parts = 2 if paired else 1
+    return pl.pallas_call(
+        pair_answer_kernel if paired else answer_kernel,
+        out_shape=[jax.ShapeDtypeStruct((members // parts, capacity, lanes), jnp.bfloat16)] * parts,
         in_specs=[vmem_spec()],
-        out_specs=pl.BlockSpec((step, capacity, lanes), lambda i: (i, 0, 0)),
+        out_specs=[vmem_spec()] * parts,
         scratch_shapes=[pltpu.VMEM((1, entries), jnp.float32)],
         compiler_params=grant(48 * entries * lanes),
         name="answer",
     )(lists)
+
+
+def place_kernel(*refs):
+    *parts, out_ref, sems = refs
+    pairs = out_ref.shape[0] // 2
+    me = lax.axis_index("mem")
+    half = lax.rem(me, 2)
+    pair = lax.div(me, 2)
+    copies = []
+    for k in range(pairs):
+        source = 2 * lax.rem(pair + pairs - k, pairs)
+        two = (parts[0].at[0], parts[1].at[0]) if k == 0 else (parts[k + 1].at[0], parts[k + 1].at[1])
+        for part, at in zip(two, (source + half, source + 1 - half)):
+            copies.append(pltpu.make_async_copy(part, out_ref.at[at], sems.at[len(copies)]))
+    for copy in copies:
+        copy.start()
+    for copy in copies:
+        copy.wait()
+
+
+def place(parts, members):
+    capacity, lanes = parts[0].shape[1:]
+    return pl.pallas_call(
+        place_kernel,
+        out_shape=jax.ShapeDtypeStruct((members, capacity, lanes), jnp.bfloat16),
+        in_specs=[vmem_spec()] * len(parts),
+        out_specs=hbm_spec(),
+        scratch_shapes=[pltpu.SemaphoreType.DMA((members,))],
+        compiler_params=grant(2 * 2**20),
+        name="place",
+    )(*parts)
+
+
+def send_back(lists, members):
+    if members % 2 or members > 8:
+        (back,) = answer(lists, members, False)
+        return lax.all_to_all(back, "mem", split_axis=0, concat_axis=0, tiled=True)
+    same, other = answer(lists, members, True)
+    mine = lax.ppermute(other, "mem", [(i, i ^ 1) for i in range(members)])
+    parts = [same, mine]
+    for k in range(1, members // 2):
+        two = jnp.concatenate([same[k : k + 1], mine[k : k + 1]], axis=0)
+        parts.append(lax.ppermute(two, "mem", [(i, (i + 2 * k) % members) for i in range(members)]))
+    return place(parts, members)
 
 
 def dense_kernel(lists_ref, out_ref, rhs_ref, key_ref):
@@ -200,7 +262,7 @@
         dense_whole_kernel,
         out_shape=jax.ShapeDtypeStruct((BUCKET, lanes), jnp.float32),
         in_specs=[vmem_spec()],
-        out_specs=pl.BlockSpec(memory_space=pltpu.HBM),
+        out_specs=hbm_spec(),
         scratch_shapes=[
             pltpu.VMEM((DIGIT, entries), jnp.bfloat16),
             pltpu.VMEM((entries, lanes), jnp.bfloat16),
@@ -238,10 +300,9 @@
 
 def per_device(groups, values, slots, counts):
     members = values.shape[1]
-    lists = pack(values[0], slots[0], counts, groups)
+    lists = pack(values[0], slots[0], counts[0], groups)
     got = lax.all_to_all(lists, ("grp", "mem"), split_axis=0, concat_axis=0, tiled=True)
-    back = answer(got, members, "grp")
-    returned = lax.all_to_all(back, "mem", split_axis=0, concat_axis=0, tiled=True)
+    returned = send_back(got, members)
     averaged = dense(got)
     return (averaged, returned[None])
 

time: 33.6 us -> 32.5 us (0.967)
  local copies, waits for them, and re-layouts: 2.8 us -> 0.84 us
  other arithmetic: 0 us -> 0.77 us
  starting transfers between devices: 3.35 us -> 4.05 us
  waiting for transfers between devices: 1.65 us -> 1.1 us
    ppermute x0 -> x4, starting transfers between devices: none -> 4.05 us  [the longest x3 3.87 us: send_back(): lax.ppermute(two, 'mem', [(i, (i + 2 * k) % members) for i in range(membe...]
    all_to_all x1 -> x0, starting transfers between devices: 3.35 us -> none  [per_device(): lax.all_to_all(back, 'mem', split_axis=0, concat_axis=0, tiled=True)]
    unnamed x7 -> x2, local copies, waits for them, and re-layouts: 2.8 us -> 0.84 us
    all_to_all x1 -> x0, waiting for transfers between devices: 1.65 us -> none  [per_device(): lax.all_to_all(back, 'mem', split_axis=0, concat_axis=0, tiled=True)]
    ppermute x0 -> x4, waiting for transfers between devices: none -> 1.1 us  [the longest x1 1.09 us: send_back(): mine = lax.ppermute(other, 'mem', [(i, i ^ 1) for i in range(members)])]
    convert_element_type x0 -> x1, other arithmetic: none -> 0.76 us  [pack(): low = jnp.where(live, slots % DIGIT, 0).astype(jnp.float32)]
    pallas_call x1 -> x2, Pallas kernels: 1.28 us -> 1.36 us  [the longest x1 0.71 us: place(): pl.pallas_call(place_kernel, out_shape=jax.ShapeDtypeStruct((members, cap...]
  transfers between devices with their start and end apart: 1 -> 4, of which waited for: 1 -> 1; matrix products, arithmetic and copies ran while one was open for 0% -> 0% of each run, Pallas kernels for 13% -> 13%
where the time goes in v3:
time: 32.5 us; the launch traced here: 32.3 us
  blocking collectives  19.2 us (59%)
  Pallas kernels  5.64 us (17%)
  starting transfers between devices  4.05 us (12%)
  waiting for transfers between devices  1.1 us (3%)
  local copies, waits for them, and re-layouts  0.84 us (3%)
  other arithmetic  0.77 us (2%)
  between operations  0.69 us (2%)
    all_to_all x1, blocking collectives, per_device(): lax.all_to_all(lists, ('grp', 'mem'), split_axis=0, concat_axis=0, tiled=...  19.2 us
    pallas_call x1, Pallas kernels, dense_whole(): pl.pallas_call(dense_whole_kernel, out_shape=jax.ShapeDtypeStruct((BUCKET...  4.19 us
    ppermute x3, starting transfers between devices, send_back(): lax.ppermute(two, 'mem', [(i, (i + 2 * k) % members) for i in range(membe...  3.87 us
    ppermute x1, waiting for transfers between devices, send_back(): mine = lax.ppermute(other, 'mem', [(i, i ^ 1) for i in range(members)])  1.09 us
    unnamed x2, local copies, waits for them, and re-layouts  0.84 us
    convert_element_type x1, other arithmetic, pack(): low = jnp.where(live, slots % DIGIT, 0).astype(jnp.float32)  0.76 us
    pallas_call x1, Pallas kernels, place(): pl.pallas_call(place_kernel, out_shape=jax.ShapeDtypeStruct((members, cap...  0.71 us
    pallas_call x1, Pallas kernels, answer(): pl.pallas_call(pair_answer_kernel if paired else answer_kernel, out_shape...  0.65 us
  transfers between devices with their start and end apart: 4, of which 1 were waited for; matrix products, arithmetic and copies ran while one was open for 0% of the time, Pallas kernels for 13%

profile of v3, /device:TPU:0, one launch (start us, length us, event | category | flops | bytes accessed | tf_op | source)
XLA Modules:
  0.0 32.3 jit_solution(6035318010704151372)
XLA Ops:
  0.6 0.8 %fusion.3 = (f32[8,32]{1,0:T(8,128)S(1)}, f32[8,32]{1,0:T(8,128)S(1)}) fusion(s32[1,8,32]{2,1,0:T(8,128)} %param.4, s32[8]{0:T(128)} %bitcast.31), kind=kLoop, calls=%fused_computation.11 | loop fusion | flops 6144 | bytes 3104 | tf_op jit(solution)/shard_map/convert_element_type | solution.py:45
  1.4 0.0 copy-start
  1.4 0.8 %copy-done = bf16[1,8,32,128]{3,2,1,0:T(8,128)(2,1)S(1)} copy-done((bf16[1,8,32,128]{3,2,1,0:T(8,128)(2,1)S(1)}, bf16[1,8,32,128]{3,2,1,0:T(8,128)(2,1)}, u32[]{:S(2)}) %copy-start) | copy-done | bytes 65560
  2.2 0.1 pack.1
  2.3 19.2 %all_to_all.5.lists_ref = bf16[32,40,128]{2,1,0:T(8,128)(2,1)S(1)} all-to-all(bf16[32,40,128]{2,1,0:T(8,128)(2,1)S(1)} %pack.1), channel_id=1, replica_groups=mesh['grp'=4,'mem'=8] {'grp','mem'}, dimensions={0} | all-to-all | bytes 655360 | tf_op jit(solution)/shard_map/all_to_all | solution.py:304
  21.5 0.7 %answer.1 = (bf16[4,32,128]{2,1,0:T(8,128)(2,1)S(1)}, bf16[4,32,128]{2,1,0:T(8,128)(2,1)S(1)}) custom-call(bf16[32,40,128]{2,1,0:T(8,128)(2,1)S(1)} %all_to_all.5.lists_ref), custom_call_target="tpu_custom_call" | custom-call | tf_op jit(solution)/shard_map/answer/pallas_call | solution.py:158
  22.1 0.2 collective-permute-start
  22.3 1.1 %collective-permute-done.refs_1_ = bf16[4,32,128]{2,1,0:T(8,128)(2,1)S(1)} collective-permute-done((bf16[4,32,128]{2,1,0:T(8,128)(2,1)S(1)}, bf16[4,32,128]{2,1,0:T(8,128)(2,1)S(1)}, u32[]{:S(2)}, u32[]{:S(2)}) %collective-permute-start) | collective-permute-done | bytes 32800 | tf_op jit(solution)/shard_map/ppermute | solution.py:205
  23.4 0.0 collective-permute-start.1
  23.4 1.5 %collective-permute-start.2 = (bf16[2,32,128]{2,1,0:T(8,128)(2,1)S(1)}, bf16[2,32,128]{2,1,0:T(8,128)(2,1)S(1)}, u32[]{:S(2)}, u32[]{:S(2)}) collective-permute-start(bf16[2,32,128]{2,1,0:T(8,128)(2,1)S(1)} %pad_maximum_fusion.1), channel_id=1, source_target_pairs={{0,4},{1,5},{2,6},{3,7},{4,0},{5,1},{6,2},{7,3},{8,12},{9,13},{10,... | collective-permute-start | bytes 49160 | tf_op jit(solution)/shard_map/ppermute | solution.py:209
  24.9 2.4 %collective-permute-start.3 = (bf16[2,32,128]{2,1,0:T(8,128)(2,1)S(1)}, bf16[2,32,128]{2,1,0:T(8,128)(2,1)S(1)}, u32[]{:S(2)}, u32[]{:S(2)}) collective-permute-start(bf16[2,32,128]{2,1,0:T(8,128)(2,1)S(1)} %pad_maximum_fusion.2), channel_id=1, source_target_pairs={{0,6},{1,7},{2,0},{3,1},{4,2},{5,3},{6,4},{7,5},{8,14},{9,15},{10,... | collective-permute-start | bytes 49160 | tf_op jit(solution)/shard_map/ppermute | solution.py:209
  27.3 4.2 %dense_whole.1 = f32[7168,128]{1,0:T(8,128)} custom-call(bf16[32,40,128]{2,1,0:T(8,128)(2,1)S(1)} %all_to_all.5.lists_ref), custom_call_target="tpu_custom_call" | custom-call | flops 1879048192 | bytes 3670016 | tf_op jit(solution)/shard_map/dense_whole/pallas_call | solution.py:261
  31.5 0.0 collective-permute-done.1.refs_2_
  31.5 0.0 collective-permute-done.2.refs_3_
  31.5 0.0 collective-permute-done.3.refs_4_
  31.5 0.7 %place.1 = bf16[8,32,128]{2,1,0:T(8,128)(2,1)} custom-call(bf16[4,32,128]{2,1,0:T(8,128)(2,1)S(1)} %get-tuple-element.4.refs_0_, bf16[4,32,128]{2,1,0:T(8,128)(2,1)S(1)} %collective-permute-done.refs_1_, bf16[2,32,128]{2,1,0:T(8,128)(2,1)S(1)} %collective-permute-done.1.refs_2_, bf16[2,32,128]{2,1,0:T(8,128)(2,1)S(1)} %collective-permute-done.2.refs_3_, ...), custom_call_target="tpu_custom_call" | custom-call | tf_op jit(solution)/shard_map/place/pallas_call | solution.py:189
  (5 shorter events, 0.0 us)
Async XLA Ops:
  1.4 0.8 %copy-start = (bf16[1,8,32,128]{3,2,1,0:T(8,128)(2,1)S(1)}, bf16[1,8,32,128]{3,2,1,0:T(8,128)(2,1)}, u32[]{:S(2)}) copy-start(bf16[1,8,32,128]{3,2,1,0:T(8,128)(2,1)} %param.3) | copy-start | bytes 196612
  22.1 1.3 %collective-permute-start = (bf16[4,32,128]{2,1,0:T(8,128)(2,1)S(1)}, bf16[4,32,128]{2,1,0:T(8,128)(2,1)S(1)}, u32[]{:S(2)}, u32[]{:S(2)}) collective-permute-start(bf16[4,32,128]{2,1,0:T(8,128)(2,1)S(1)} %get-tuple-element.5), channel_id=1, source_target_pairs={{0,1},{1,0},{2,3},{3,2},{4,5},{5,4},{6,7},{7,6},{8,9},{9,8},{10,11... | collective-permute-start | bytes 98312 | tf_op jit(solution)/shard_map/ppermute | solution.py:205
  23.4 8.1 %collective-permute-start.1 = (bf16[2,32,128]{2,1,0:T(8,128)(2,1)S(1)}, bf16[2,32,128]{2,1,0:T(8,128)(2,1)S(1)}, u32[]{:S(2)}, u32[]{:S(2)}) collective-permute-start(bf16[2,32,128]{2,1,0:T(8,128)(2,1)S(1)} %pad_maximum_fusion), channel_id=1, source_target_pairs={{0,2},{1,3},{2,4},{3,5},{4,6},{5,7},{6,0},{7,1},{8,10},{9,11},{10,... | collective-permute-start | bytes 49160 | tf_op jit(solution)/shard_map/ppermute | solution.py:209
  23.4 8.1 %collective-permute-start.2 = (bf16[2,32,128]{2,1,0:T(8,128)(2,1)S(1)}, bf16[2,32,128]{2,1,0:T(8,128)(2,1)S(1)}, u32[]{:S(2)}, u32[]{:S(2)}) collective-permute-start(bf16[2,32,128]{2,1,0:T(8,128)(2,1)S(1)} %pad_maximum_fusion.1), channel_id=1, source_target_pairs={{0,4},{1,5},{2,6},{3,7},{4,0},{5,1},{6,2},{7,3},{8,12},{9,13},{10,... | collective-permute-start | bytes 49160 | tf_op jit(solution)/shard_map/ppermute | solution.py:209
  24.9 6.6 %collective-permute-start.3 = (bf16[2,32,128]{2,1,0:T(8,128)(2,1)S(1)}, bf16[2,32,128]{2,1,0:T(8,128)(2,1)S(1)}, u32[]{:S(2)}, u32[]{:S(2)}) collective-permute-start(bf16[2,32,128]{2,1,0:T(8,128)(2,1)S(1)} %pad_maximum_fusion.2), channel_id=1, source_target_pairs={{0,6},{1,7},{2,0},{3,1},{4,2},{5,3},{6,4},{7,5},{8,14},{9,15},{10,... | collective-permute-start | bytes 49160 | tf_op jit(solution)/shard_map/ppermute | solution.py:209

commit v4 on v3

--- a/solution.py
+++ b/solution.py
@@ -10,6 +10,7 @@
 
 BUCKET = 7168
 DIGIT = 256
+TILE = 512
 META = 8
 
 
@@ -25,11 +26,22 @@
     return pltpu.CompilerParams(vmem_limit_bytes=size)
 
 
-def pack_kernel(groups, values_ref, high_ref, low_ref, out_ref):
+def place_in_list_kernel(out_ref):
+    out_ref[...] = lax.broadcasted_iota(jnp.int32, out_ref.shape, 1).astype(jnp.float32)
+
+
+def pack_kernel(groups, values_ref, slots_ref, counts_ref, place_ref, out_ref):
     members, capacity, lanes = values_ref.shape
+    shape = (members, members)
+    diagonal = lax.broadcasted_iota(jnp.int32, shape, 0) == lax.broadcasted_iota(jnp.int32, shape, 1)
+    count = jnp.sum(jnp.where(diagonal, counts_ref[...].astype(jnp.float32), 0.0), axis=1, keepdims=True)
+    slot = slots_ref[...]
+    live = place_ref[...] < count
+    high = jnp.where(live, (slot // DIGIT).astype(jnp.float32), -1.0)
+    low = jnp.where(live, (slot % DIGIT).astype(jnp.float32), 0.0)
     repeats = lanes // capacity
-    high = jnp.concatenate([high_ref[...]] * repeats, axis=1)
-    low = jnp.concatenate([low_ref[...]] * repeats, axis=1)
+    high = jnp.concatenate([high] * repeats, axis=1)
+    low = jnp.concatenate([low] * repeats, axis=1)
     row = lax.broadcasted_iota(jnp.int32, (members, META, lanes), 1)
     meta = jnp.where(row == 0, high[:, None, :], low[:, None, :]).astype(jnp.bfloat16)
     for group in range(groups):
@@ -40,17 +52,22 @@
 
 def pack(values, slots, counts, groups):
     members, capacity, lanes = values.shape
-    live = lax.broadcasted_iota(jnp.int32, slots.shape, 1) < counts[:, None]
-    high = jnp.where(live, slots // DIGIT, -1).astype(jnp.float32)
-    low = jnp.where(live, slots % DIGIT, 0).astype(jnp.float32)
+    place_in_list = pl.pallas_call(
+        place_in_list_kernel,
+        out_shape=jax.ShapeDtypeStruct(slots.shape, jnp.float32),
+        out_specs=vmem_spec(),
+        cost_estimate=pl.CostEstimate(flops=2 * 10**9, bytes_accessed=16 * 10**6, transcendentals=0),
+        compiler_params=grant(2**20),
+        name="place_in_list",
+    )()
     return pl.pallas_call(
         functools.partial(pack_kernel, groups),
         out_shape=jax.ShapeDtypeStruct((groups * members, capacity + META, lanes), jnp.bfloat16),
-        in_specs=[vmem_spec()] * 3,
+        in_specs=[vmem_spec()] * 4,
         out_specs=vmem_spec(),
         compiler_params=grant(8 * 2**20),
         name="pack",
-    )(values, high, low)
+    )(values, slots, counts, place_in_list)
 
 
 def digits_of(lists_ref, first, senders):
@@ -220,71 +237,97 @@
     out_ref[...] = average(wanted, key_ref, rhs_ref)
 
 
-def dense_whole_kernel(lists_ref, out_ref, same_ref, high_ref, mean_ref, sems):
+def tile_pair(pair, lists_ref, same_ref, tile_ref, inverse_ref, mean_ref, out_ref, sem):
+    senders, rows, lanes = lists_ref.shape
+    capacity = rows - META
+    values = lists_ref[:, pl.ds(0, capacity), :].reshape(senders * capacity, lanes)
+    tile_of = tile_ref[...]
+    zero = jnp.zeros_like(values)
+    picked = jnp.concatenate([jnp.where(tile_of == 2 * pair + k, values, zero) for k in range(2)], axis=1)
+    sums = jnp.dot(same_ref[...], picked, preferred_element_type=jnp.float32)
+    copies = []
+    for k in range(2):
+        tile = 2 * pair + k
+        where = pl.ds(tile * TILE, TILE)
+        part = mean_ref.at[pl.ds(k * TILE, TILE)]
+        part[...] = sums[:, k * lanes : (k + 1) * lanes] * inverse_ref[:, tile : tile + 1]
+        copy = pltpu.make_async_copy(part, out_ref.at[where], sem.at[k])
+        copy.start()
+        copies.append(copy)
+    return copies
+
+
+def dense_prepare_kernel(lists_ref, same_ref, tile_ref, inverse_ref):
     senders, rows, lanes = lists_ref.shape
     capacity = rows - META
     entries = senders * capacity
+    ratio = TILE // DIGIT
     high, low = digits_of(lists_ref, 0, senders)
-    low_row = as_row(low, capacity)
-    wanted = lax.broadcasted_iota(jnp.int32, (DIGIT, lanes), 0).astype(jnp.float32)
+    tile = jnp.floor(high * (1.0 / ratio))
+    low_row = as_row(low + DIGIT * (high - ratio * tile), capacity)
+    wanted = lax.broadcasted_iota(jnp.int32, (TILE, lanes), 0).astype(jnp.float32)
     for at in range(0, entries, lanes):
         same = (wanted == low_row[:, at : at + lanes]).astype(jnp.float32)
         same_ref[:, at : at + lanes] = same.astype(jnp.bfloat16)
-    high_column = as_column(high, capacity)
-    high_ref[...] = high_column.astype(jnp.bfloat16)
+    tile_column = as_column(tile, capacity)
+    tile_ref[...] = tile_column.astype(jnp.bfloat16)
     lane = lax.broadcasted_iota(jnp.int32, (entries, lanes), 1).astype(jnp.float32)
-    in_tile = (high_column == lane).astype(jnp.float32).astype(jnp.bfloat16)
-    count = jnp.dot(same_ref[...], in_tile, preferred_element_type=jnp.float32)
-    inverse = 1.0 / jnp.maximum(count, 1.0)
+    in_tile = (tile_column == lane).astype(jnp.float32).astype(jnp.bfloat16)
+    number = jnp.dot(same_ref[...], in_tile, preferred_element_type=jnp.float32)
+    inverse_ref[...] = 1.0 / jnp.maximum(number, 1.0)
+
+
+def dense_tiles_kernel(lists_ref, same_ref, tile_ref, inverse_ref, out_ref, mean_ref, sems):
     copies = []
-    for pair in range(BUCKET // (2 * DIGIT)):
-        values = lists_ref[:, pl.ds(0, capacity), :].reshape(entries, lanes)
-        tile_of = high_ref[...]
-        zero = jnp.zeros_like(values)
-        picked = jnp.concatenate([jnp.where(tile_of == 2 * pair + k, values, zero) for k in range(2)], axis=1)
-        sums = jnp.dot(same_ref[...], picked, preferred_element_type=jnp.float32)
-        for k in range(2):
-            tile = 2 * pair + k
-            where = pl.ds(tile * DIGIT, DIGIT)
-            mean_ref[where, :] = sums[:, k * lanes : (k + 1) * lanes] * inverse[:, tile : tile + 1]
-        where = pl.ds(2 * pair * DIGIT, 2 * DIGIT)
-        copy = pltpu.make_async_copy(mean_ref.at[where], out_ref.at[where], sems.at[pair])
-        copy.start()
-        copies.append(copy)
+    for pair in range(sems.shape[0]):
+        part = mean_ref.at[pl.ds(2 * pair * TILE, 2 * TILE)]
+        copies += tile_pair(pair, lists_ref, same_ref, tile_ref, inverse_ref, part, out_ref, sems.at[pair])
     for copy in copies:
         copy.wait()
 
 
-def dense_whole(lists):
+def dense_split(lists):
     senders, rows, lanes = lists.shape
     entries = senders * (rows - META)
-    return pl.pallas_call(
-        dense_whole_kernel,
+    same, tile, inverse = pl.pallas_call(
+        dense_prepare_kernel,
+        out_shape=[
+            jax.ShapeDtypeStruct((TILE, entries), jnp.bfloat16),
+            jax.ShapeDtypeStruct((entries, lanes), jnp.bfloat16),
+            jax.ShapeDtypeStruct((TILE, lanes), jnp.float32),
+        ],
+        in_specs=[vmem_spec()],
+        out_specs=[vmem_spec()] * 3,
+        cost_estimate=dense_cost(entries, lanes, TILE / BUCKET),
+        compiler_params=grant(8 * 2**20),
+        name="dense_prepare",
+    )(lists)
+    return pl.pallas_call(
+        dense_tiles_kernel,
         out_shape=jax.ShapeDtypeStruct((BUCKET, lanes), jnp.float32),
-        in_specs=[vmem_spec()],
+        in_specs=[vmem_spec()] * 4,
         out_specs=hbm_spec(),
         scratch_shapes=[
-            pltpu.VMEM((DIGIT, entries), jnp.bfloat16),
-            pltpu.VMEM((entries, lanes), jnp.bfloat16),
             pltpu.VMEM((BUCKET, lanes), jnp.float32),
-            pltpu.SemaphoreType.DMA((BUCKET // (2 * DIGIT),)),
+            pltpu.SemaphoreType.DMA((BUCKET // (2 * TILE), 2)),
         ],
         cost_estimate=dense_cost(entries, lanes),
         compiler_params=grant(16 * 2**20),
-        name="dense_whole",
-    )(lists)
-
-
-def dense_cost(entries, lanes):
-    return pl.CostEstimate(flops=2 * BUCKET * entries * lanes, bytes_accessed=4 * BUCKET * lanes, transcendentals=0)
+        name="dense_tiles",
+    )(lists, same, tile, inverse)
+
+
+def dense_cost(entries, lanes, share=1.0):
+    flops = int(2 * BUCKET * entries * lanes * share)
+    return pl.CostEstimate(flops=flops, bytes_accessed=int(4 * BUCKET * lanes * share), transcendentals=0)
 
 
 def dense(lists):
     senders, rows, lanes = lists.shape
     capacity = rows - META
     entries = senders * capacity
-    if entries <= 1024 and BUCKET % (2 * DIGIT) == 0 and BUCKET // DIGIT <= lanes:
-        return dense_whole(lists)
+    if entries <= 1024 and BUCKET % (2 * TILE) == 0 and BUCKET // TILE <= lanes:
+        return dense_split(lists)
     tile = math.gcd(BUCKET, 512)
     return pl.pallas_call(
         dense_kernel,
@@ -300,7 +343,7 @@
 
 def per_device(groups, values, slots, counts):
     members = values.shape[1]
-    lists = pack(values[0], slots[0], counts[0], groups)
+    lists = pack(values[0], slots[0], counts, groups)
     got = lax.all_to_all(lists, ("grp", "mem"), split_axis=0, concat_axis=0, tiled=True)
     returned = send_back(got, members)
     averaged = dense(got)

time: 32.5 us -> 31 us (0.954)
  other arithmetic: 0.77 us -> 0.01 us
  waiting for transfers between devices: 1.1 us -> 0.42 us
    convert_element_type x1 -> x0, other arithmetic: 0.76 us -> none  [pack(): low = jnp.where(live, slots % DIGIT, 0).astype(jnp.float32)]
    ppermute x1, waiting for transfers between devices: 1.09 us -> 0.42 us  [send_back(): mine = lax.ppermute(other, 'mem', [(i, i ^ 1) for i in range(members)])]
    pallas_call x1 -> x3, Pallas kernels: 4.19 us -> 4.12 us  [the longest x1 3.45 us: dense_split(): pl.pallas_call(dense_tiles_kernel, out_shape=jax.ShapeDtypeStruct((BUCKET...]
    unnamed x2 -> x6, local copies, waits for them, and re-layouts: 0.84 us -> 0.81 us
where the time goes in v4:
time: 31 us; the launch traced here: 30.8 us
  blocking collectives  19.2 us (62%)
  Pallas kernels  5.65 us (18%)
  starting transfers between devices  4.06 us (13%)
  local copies, waits for them, and re-layouts  0.82 us (3%)
  between operations  0.73 us (2%)
  waiting for transfers between devices  0.42 us (1%)
    all_to_all x1, blocking collectives, per_device(): lax.all_to_all(lists, ('grp', 'mem'), split_axis=0, concat_axis=0, tiled=...  19.2 us
    ppermute x3, starting transfers between devices, send_back(): lax.ppermute(two, 'mem', [(i, (i + 2 * k) % members) for i in range(membe...  3.87 us
    pallas_call x1, Pallas kernels, dense_split(): pl.pallas_call(dense_tiles_kernel, out_shape=jax.ShapeDtypeStruct((BUCKET...  3.45 us
    unnamed x6, local copies, waits for them, and re-layouts  0.81 us
    pallas_call x1, Pallas kernels, place(): pl.pallas_call(place_kernel, out_shape=jax.ShapeDtypeStruct((members, cap...  0.71 us
    pallas_call x1, Pallas kernels, dense_split(): pl.pallas_call(dense_prepare_kernel, out_shape=[jax.ShapeDtypeStruct((TIL...  0.66 us
    pallas_call x1, Pallas kernels, answer(): pl.pallas_call(pair_answer_kernel if paired else answer_kernel, out_shape...  0.65 us
  transfers between devices with their start and end apart: 4, of which 1 were waited for; matrix products, arithmetic and copies ran while one was open for 0% of the time, Pallas kernels for 13%

profile of v4, /device:TPU:0, one launch (start us, length us, event | category | flops | bytes accessed | tf_op | source)
XLA Modules:
  0.0 30.8 jit_solution(16339346268993878548)
XLA Ops:
  0.6 0.0 copy-start
  0.6 0.0 copy-start.1
  0.6 0.0 copy-start.2
  0.7 0.8 %copy-done = bf16[1,8,32,128]{3,2,1,0:T(8,128)(2,1)S(1)} copy-done((bf16[1,8,32,128]{3,2,1,0:T(8,128)(2,1)S(1)}, bf16[1,8,32,128]{3,2,1,0:T(8,128)(2,1)}, u32[]{:S(2)}) %copy-start) | copy-done | bytes 65560
  1.5 0.0 copy-done.1
  1.5 0.0 copy-done.2
  1.5 0.2 pack.1
  1.7 19.2 %all_to_all.5.lists_ref = bf16[32,40,128]{2,1,0:T(8,128)(2,1)S(1)} all-to-all(bf16[32,40,128]{2,1,0:T(8,128)(2,1)S(1)} %pack.1), channel_id=1, replica_groups=mesh['grp'=4,'mem'=8] {'grp','mem'}, dimensions={0} | all-to-all | bytes 655360 | tf_op jit(solution)/shard_map/all_to_all | solution.py:347
  20.8 0.7 %answer.1 = (bf16[4,32,128]{2,1,0:T(8,128)(2,1)S(1)}, bf16[4,32,128]{2,1,0:T(8,128)(2,1)S(1)}) custom-call(bf16[32,40,128]{2,1,0:T(8,128)(2,1)S(1)} %all_to_all.5.lists_ref), custom_call_target="tpu_custom_call" | custom-call | tf_op jit(solution)/shard_map/answer/pallas_call | solution.py:175
  21.5 0.2 collective-permute-start
  21.7 0.7 %dense_prepare.1 = (bf16[512,1024]{1,0:T(8,128)(2,1)S(1)}, bf16[1024,128]{1,0:T(8,128)(2,1)S(1)}, f32[512,128]{1,0:T(8,128)S(1)}) custom-call(bf16[32,40,128]{2,1,0:T(8,128)(2,1)S(1)} %all_to_all.5.lists_ref), custom_call_target="tpu_custom_call" | custom-call | flops 134217728 | bytes 262144 | tf_op jit(solution)/shard_map/dense_prepare/pallas_call | solution.py:292
  22.3 0.4 %collective-permute-done.refs_1_ = bf16[4,32,128]{2,1,0:T(8,128)(2,1)S(1)} collective-permute-done((bf16[4,32,128]{2,1,0:T(8,128)(2,1)S(1)}, bf16[4,32,128]{2,1,0:T(8,128)(2,1)S(1)}, u32[]{:S(2)}, u32[]{:S(2)}) %collective-permute-start) | collective-permute-done | bytes 32800 | tf_op jit(solution)/shard_map/ppermute | solution.py:222
  22.7 0.0 collective-permute-start.1
  22.8 1.5 %collective-permute-start.2 = (bf16[2,32,128]{2,1,0:T(8,128)(2,1)S(1)}, bf16[2,32,128]{2,1,0:T(8,128)(2,1)S(1)}, u32[]{:S(2)}, u32[]{:S(2)}) collective-permute-start(bf16[2,32,128]{2,1,0:T(8,128)(2,1)S(1)} %pad_maximum_fusion.1), channel_id=1, source_target_pairs={{0,4},{1,5},{2,6},{3,7},{4,0},{5,1},{6,2},{7,3},{8,12},{9,13},{10,... | collective-permute-start | bytes 49160 | tf_op jit(solution)/shard_map/ppermute | solution.py:226
  24.2 2.4 %collective-permute-start.3 = (bf16[2,32,128]{2,1,0:T(8,128)(2,1)S(1)}, bf16[2,32,128]{2,1,0:T(8,128)(2,1)S(1)}, u32[]{:S(2)}, u32[]{:S(2)}) collective-permute-start(bf16[2,32,128]{2,1,0:T(8,128)(2,1)S(1)} %pad_maximum_fusion.2), channel_id=1, source_target_pairs={{0,6},{1,7},{2,0},{3,1},{4,2},{5,3},{6,4},{7,5},{8,14},{9,15},{10,... | collective-permute-start | bytes 49160 | tf_op jit(solution)/shard_map/ppermute | solution.py:226
  26.6 3.5 %dense_tiles.1 = f32[7168,128]{1,0:T(8,128)} custom-call(bf16[32,40,128]{2,1,0:T(8,128)(2,1)S(1)} %all_to_all.5.lists_ref, bf16[512,1024]{1,0:T(8,128)(2,1)S(1)} %get-tuple-element.7.same_ref, bf16[1024,128]{1,0:T(8,128)(2,1)S(1)} %get-tuple-element.8.tile_ref, f32[512,128]{1,0:T(8,128)S(1)} %get-tuple-element.9.inverse_ref), custom_call_target="tpu_custom_call" | custom-call | flops 1879048192 | bytes 3670016 | tf_op jit(solution)/shard_map/dense_tiles/pallas_call | solution.py:305
  30.1 0.0 collective-permute-done.1.refs_2_
  30.1 0.0 collective-permute-done.2.refs_3_
  30.1 0.0 collective-permute-done.3.refs_4_
  30.1 0.7 %place.1 = bf16[8,32,128]{2,1,0:T(8,128)(2,1)} custom-call(bf16[4,32,128]{2,1,0:T(8,128)(2,1)S(1)} %get-tuple-element.10.refs_0_, bf16[4,32,128]{2,1,0:T(8,128)(2,1)S(1)} %collective-permute-done.refs_1_, bf16[2,32,128]{2,1,0:T(8,128)(2,1)S(1)} %collective-permute-done.1.refs_2_, bf16[2,32,128]{2,1,0:T(8,128)(2,1)S(1)} %collective-permute-done.2.refs_3_, ...), custom_call_target="tpu_custom_call" | custom-call | tf_op jit(solution)/shard_map/place/pallas_call | solution.py:206
  (6 shorter events, 0.0 us)
Async XLA Ops:
  0.6 0.8 %copy-start = (bf16[1,8,32,128]{3,2,1,0:T(8,128)(2,1)S(1)}, bf16[1,8,32,128]{3,2,1,0:T(8,128)(2,1)}, u32[]{:S(2)}) copy-start(bf16[1,8,32,128]{3,2,1,0:T(8,128)(2,1)} %param.3) | copy-start | bytes 196612
  0.6 0.8 %copy-start.1 = (s32[1,8,32]{2,1,0:T(8,128)S(1)}, s32[1,8,32]{2,1,0:T(8,128)}, u32[]{:S(2)}) copy-start(s32[1,8,32]{2,1,0:T(8,128)} %param.4) | copy-start | bytes 3076
  0.6 0.8 %copy-start.2 = (s32[1,8]{1,0:T(1,128)S(1)}, s32[1,8]{1,0:T(1,128)}, u32[]{:S(2)}) copy-start(s32[1,8]{1,0:T(1,128)} %counts_ref.1) | copy-start | bytes 100
  21.5 1.3 %collective-permute-start = (bf16[4,32,128]{2,1,0:T(8,128)(2,1)S(1)}, bf16[4,32,128]{2,1,0:T(8,128)(2,1)S(1)}, u32[]{:S(2)}, u32[]{:S(2)}) collective-permute-start(bf16[4,32,128]{2,1,0:T(8,128)(2,1)S(1)} %get-tuple-element.11), channel_id=1, source_target_pairs={{0,1},{1,0},{2,3},{3,2},{4,5},{5,4},{6,7},{7,6},{8,9},{9,8},{10,11... | collective-permute-start | bytes 98312 | tf_op jit(solution)/shard_map/ppermute | solution.py:222
  22.7 7.4 %collective-permute-start.1 = (bf16[2,32,128]{2,1,0:T(8,128)(2,1)S(1)}, bf16[2,32,128]{2,1,0:T(8,128)(2,1)S(1)}, u32[]{:S(2)}, u32[]{:S(2)}) collective-permute-start(bf16[2,32,128]{2,1,0:T(8,128)(2,1)S(1)} %pad_maximum_fusion), channel_id=1, source_target_pairs={{0,2},{1,3},{2,4},{3,5},{4,6},{5,7},{6,0},{7,1},{8,10},{9,11},{10,... | collective-permute-start | bytes 49160 | tf_op jit(solution)/shard_map/ppermute | solution.py:226
  22.8 7.3 %collective-permute-start.2 = (bf16[2,32,128]{2,1,0:T(8,128)(2,1)S(1)}, bf16[2,32,128]{2,1,0:T(8,128)(2,1)S(1)}, u32[]{:S(2)}, u32[]{:S(2)}) collective-permute-start(bf16[2,32,128]{2,1,0:T(8,128)(2,1)S(1)} %pad_maximum_fusion.1), channel_id=1, source_target_pairs={{0,4},{1,5},{2,6},{3,7},{4,0},{5,1},{6,2},{7,3},{8,12},{9,13},{10,... | collective-permute-start | bytes 49160 | tf_op jit(solution)/shard_map/ppermute | solution.py:226
  24.2 5.9 %collective-permute-start.3 = (bf16[2,32,128]{2,1,0:T(8,128)(2,1)S(1)}, bf16[2,32,128]{2,1,0:T(8,128)(2,1)S(1)}, u32[]{:S(2)}, u32[]{:S(2)}) collective-permute-start(bf16[2,32,128]{2,1,0:T(8,128)(2,1)S(1)} %pad_maximum_fusion.2), channel_id=1, source_target_pairs={{0,6},{1,7},{2,0},{3,1},{4,2},{5,3},{6,4},{7,5},{8,14},{9,15},{10,... | collective-permute-start | bytes 49160 | tf_op jit(solution)/shard_map/ppermute | solution.py:226

commit v5 on v4

v5 whole, which is shorter than its diff:
```python
import functools
import math

import jax
import jax.numpy as jnp
from jax import lax
from jax.experimental import pallas as pl
from jax.experimental.pallas import tpu as pltpu
from jax.sharding import PartitionSpec as P


BUCKET = 7168
DIGIT = 256
TILE = 512
META = 8
MIB = 2**20


def vmem_spec():
    return pl.BlockSpec(memory_space=pltpu.VMEM)


def hbm_spec():
    return pl.BlockSpec(memory_space=pltpu.HBM)


def grant(size):
    return pltpu.CompilerParams(vmem_limit_bytes=size)


def lists_shape(count, capacity, lanes):
    return jax.ShapeDtypeStruct((count, capacity + META, lanes), jnp.bfloat16)


def place_in_list_kernel(out_ref):
    out_ref[...] = lax.broadcasted_iota(jnp.int32, out_ref.shape, 1).astype(jnp.float32)


def meta_rows(slots_ref, counts_ref, place_ref, lanes):
    members, capacity = slots_ref.shape
    shape = (members, members)
    diagonal = lax.broadcasted_iota(jnp.int32, shape, 0) == lax.broadcasted_iota(jnp.int32, shape, 1)
    count = jnp.sum(jnp.where(diagonal, counts_ref[...].astype(jnp.float32), 0.0), axis=1, keepdims=True)
    slot = slots_ref[...]
    live = place_ref[...] < count
    high = jnp.where(live, (slot // DIGIT).astype(jnp.float32), -1.0)
    low = jnp.where(live, (slot % DIGIT).astype(jnp.float32), 0.0)
    repeats = lanes // capacity
    high = jnp.concatenate([high] * repeats, axis=1)
    low = jnp.concatenate([low] * repeats, axis=1)
    row = lax.broadcasted_iota(jnp.int32, (members, META, lanes), 1)
    return jnp.where(row == 0, high[:, None, :], low[:, None, :]).astype(jnp.bfloat16)


def pack_groups_kernel(values_ref, slots_ref, counts_ref, place_ref, out_ref):
    members, capacity, lanes = values_ref.shape
    meta = meta_rows(slots_ref, counts_ref, place_ref, lanes)
    for group in range(out_ref.shape[0] // members):
        rows = pl.ds(group * members, members)
        out_ref[rows, pl.ds(0, capacity), :] = values_ref[...]
        out_ref[rows, pl.ds(capacity, META), :] = meta


def pack_pairs_kernel(values_ref, slots_ref, counts_ref, place_ref, *out_and_scratch):
    *out_refs, meta_ref = out_and_scratch
    capacity, lanes = values_ref.shape[1:]
    meta_ref[...] = meta_rows(slots_ref, counts_ref, place_ref, lanes)
    pair = lax.div(lax.axis_index("mem"), 2)
    for k, out_ref in enumerate(out_refs):
        rows = pl.ds(2 * lax.bitwise_xor(pair, jnp.int32(k)), 2)
        out_ref[:, pl.ds(0, capacity), :] = values_ref[rows]
        out_ref[:, pl.ds(capacity, META), :] = meta_ref[rows]


def pack(values, slots, counts, groups, paired):
    members, capacity, lanes = values.shape
    place_in_list = pl.pallas_call(
        place_in_list_kernel,
        out_shape=jax.ShapeDtypeStruct(slots.shape, jnp.float32),
        out_specs=vmem_spec(),
        cost_estimate=pl.CostEstimate(flops=2 * 10**9, bytes_accessed=16 * 10**6, transcendentals=0),
        compiler_params=grant(MIB),
        name="place_in_list",
    )()
    if paired:
        kernel, out_shape = pack_pairs_kernel, [lists_shape(2, capacity, lanes)] * (members // 2)
        scratch = [pltpu.VMEM((members, META, lanes), jnp.bfloat16)]
    else:
        kernel, out_shape = pack_groups_kernel, [lists_shape(groups * members, capacity, lanes)]
        scratch = []
    return pl.pallas_call(
        kernel,
        out_shape=out_shape,
        in_specs=[vmem_spec()] * 4,
        out_specs=[vmem_spec()] * len(out_shape),
        scratch_shapes=scratch,
        compiler_params=grant(8 * MIB),
        name="pack",
    )(values, slots, counts, place_in_list)


def digits_of(refs):
    capacity = refs[0].shape[1] - META
    meta = [ref[:, pl.ds(capacity, META), :].astype(jnp.float32) for ref in refs]
    return jnp.concatenate([m[:, 0, :] for m in meta], axis=0), jnp.concatenate([m[:, 1, :] for m in meta], axis=0)


def entries_of(refs):
    capacity, lanes = refs[0].shape[1] - META, refs[0].shape[2]
    return jnp.concatenate([ref[:, pl.ds(0, capacity), :].reshape(-1, lanes) for ref in refs], axis=0)


def as_row(digit, capacity):
    lists, lanes = digit.shape
    per_block = lanes // capacity
    part = lax.broadcasted_iota(jnp.int32, (1, lanes), 1) // capacity
    blocks = []
    for block in range(lists // per_block):
        row = digit[block * per_block : block * per_block + 1]
        for k in range(1, per_block):
            at = block * per_block + k
            row = jnp.where(part == k, digit[at : at + 1], row)
        blocks.append(row)
    return jnp.concatenate(blocks, axis=1)


def as_column(digit, capacity):
    lists, lanes = digit.shape
    shape = (lists, capacity, lanes)
    here = lax.broadcasted_iota(jnp.int32, shape, 2) == lax.broadcasted_iota(jnp.int32, shape, 1)
    picked = jnp.where(here, digit[:, None, :], 0.0).astype(jnp.bfloat16).reshape(lists * capacity, lanes)
    return jnp.dot(picked, jnp.ones((lanes, lanes), jnp.bfloat16), preferred_element_type=jnp.float32)


def keys_of(refs):
    high, low = digits_of(refs)
    return as_row(high * DIGIT + low, refs[0].shape[1] - META)


def answer_some(asking, key, entries):
    capacity, lanes = asking[0].shape[1] - META, entries.shape[1]
    high, low = digits_of(asking)
    column = as_column(high, capacity) * DIGIT + as_column(low, capacity)
    column = jnp.where(column < 0.0, -1.0, column)
    onehot = jnp.concatenate(
        [
            (column == key[:, at : at + lanes]).astype(jnp.float32).astype(jnp.bfloat16)
            for at in range(0, entries.shape[0], lanes)
        ],
        axis=1,
    )
    sums = jnp.dot(onehot, entries, preferred_element_type=jnp.float32)
    count = jnp.dot(onehot, jnp.ones_like(entries), preferred_element_type=jnp.float32)
    mean = sums / jnp.maximum(count, 1.0)
    return mean.astype(jnp.bfloat16).reshape(-1, capacity, lanes)


def answer_kernel(lists_ref, out_ref, key_ref):
    members = out_ref.shape[0]
    step = math.gcd(members, 8)
    key_ref[...] = keys_of([lists_ref])
    first = lax.axis_index("grp") * members

    @pl.loop(0, members, step=step)
    def _(at):
        asking = lists_ref.at[pl.ds(first + at, step)]
        out_ref[pl.ds(at, step)] = answer_some([asking], key_ref[...], entries_of([lists_ref]))


def answer(lists, members):
    senders, rows, lanes = lists.shape
    capacity = rows - META
    entries = senders * capacity
    return pl.pallas_call(
        answer_kernel,
        out_shape=jax.ShapeDtypeStruct((members, capacity, lanes), jnp.bfloat16),
        in_specs=[vmem_spec()],
        out_specs=vmem_spec(),
        scratch_shapes=[pltpu.VMEM((1, entries), jnp.float32)],
        compiler_params=grant(48 * entries * lanes),
        name="answer",
    )(lists)


def pair_answer_kernel(count, *refs):
    in_refs, out_refs = refs[:count], refs[count:]
    for bucket in range(2):
        views = [ref.at[bucket] for ref in in_refs]
        mean = answer_some(views[:1], keys_of(views), entries_of(views))
        for k, out_ref in enumerate(out_refs):
            out_ref[bucket] = mean[k]


def pair_answer(parts):
    pairs, rows, lanes = parts[0].shape[1:]
    shape = jax.ShapeDtypeStruct((2, rows - META, lanes), jnp.bfloat16)
    return pl.pallas_call(
        functools.partial(pair_answer_kernel, len(parts)),
        out_shape=[shape] * pairs,
        in_specs=[vmem_spec()] * len(parts),
        out_specs=[vmem_spec()] * pairs,
        compiler_params=grant(8 * MIB),
        name="pair_answer",
    )(*parts)


def place_kernel(*refs):
    *parts, out_ref, sems = refs
    pair = lax.div(lax.axis_index("mem"), 2)
    copies = []
    for k, part in enumerate(parts):
        rows = pl.ds(2 * lax.bitwise_xor(pair, jnp.int32(k)), 2)
        copies.append(pltpu.make_async_copy(part, out_ref.at[rows], sems.at[k]))
    for copy in copies:
        copy.start()
    for copy in copies:
        copy.wait()


def place(parts):
    two, capacity, lanes = parts[0].shape
    return pl.pallas_call(
        place_kernel,
        out_shape=jax.ShapeDtypeStruct((two * len(parts), capacity, lanes), jnp.bfloat16),
        in_specs=[vmem_spec()] * len(parts),
        out_specs=hbm_spec(),
        scratch_shapes=[pltpu.SemaphoreType.DMA((len(parts),))],
        compiler_params=grant(2 * MIB),
        name="place",
    )(*parts)


def dense_cost(entries, lanes, share=1.0):
    flops = int(2 * BUCKET * entries * lanes * share)
    return pl.CostEstimate(flops=flops, bytes_accessed=int(4 * BUCKET * lanes * share), transcendentals=0)


def dense_kernel(lists_ref, out_ref, key_ref):
    @pl.when(pl.program_id(0) == 0)
    def _():
        key_ref[...] = keys_of([lists_ref])

    tile = out_ref.shape[0]
    wanted = (lax.broadcasted_iota(jnp.int32, (tile, 1), 0) + pl.program_id(0) * tile).astype(jnp.float32)
    onehot = (wanted == key_ref[...]).astype(jnp.float32).astype(jnp.bfloat16)
    entries = entries_of([lists_ref])
    sums = jnp.dot(onehot, entries, preferred_element_type=jnp.float32)
    count = jnp.dot(onehot, jnp.ones_like(entries), preferred_element_type=jnp.float32)
    out_ref[...] = sums / jnp.maximum(count, 1.0)


def dense(lists):
    senders, rows, lanes = lists.shape
    entries = senders * (rows - META)
    tile = math.gcd(BUCKET, 512)
    return pl.pallas_call(
        dense_kernel,
        grid=(BUCKET // tile,),
        out_shape=jax.ShapeDtypeStruct((BUCKET, lanes), jnp.float32),
        in_specs=[vmem_spec()],
        out_specs=pl.BlockSpec((tile, lanes), lambda i: (i, 0)),
        scratch_shapes=[pltpu.VMEM((1, entries), jnp.float32)],
        cost_estimate=dense_cost(entries, lanes),
        name="dense",
    )(lists)


def own_bucket(refs):
    return [ref.at[lax.rem(lax.axis_index("mem"), 2)] for ref in refs]


def dense_prepare_kernel(*refs):
    *in_refs, same_ref, tile_ref, inverse_ref = refs
    views = own_bucket(in_refs)
    capacity, lanes = views[0].shape[1] - META, views[0].shape[2]
    entries = same_ref.shape[1]
    ratio = TILE // DIGIT
    high, low = digits_of(views)
    tile = jnp.floor(high * (1.0 / ratio))
    low_row = as_row(low + DIGIT * (high - ratio * tile), capacity)
    wanted = lax.broadcasted_iota(jnp.int32, (TILE, lanes), 0).astype(jnp.float32)
    for at in range(0, entries, lanes):
        same = (wanted == low_row[:, at : at + lanes]).astype(jnp.float32)
        same_ref[:, at : at + lanes] = same.astype(jnp.bfloat16)
    tile_column = as_column(tile, capacity)
    tile_ref[...] = tile_column.astype(jnp.bfloat16)
    lane = lax.broadcasted_iota(jnp.int32, (entries, lanes), 1).astype(jnp.float32)
    in_tile = (tile_column == lane).astype(jnp.float32).astype(jnp.bfloat16)
    number = jnp.dot(same_ref[...], in_tile, preferred_element_type=jnp.float32)
    inverse_ref[...] = 1.0 / jnp.maximum(number, 1.0)


def dense_tiles_kernel(*refs):
    *in_refs, same_ref, tile_ref, inverse_ref, out_ref, mean_ref, sems = refs
    views = own_bucket(in_refs)
    lanes = views[0].shape[2]
    copies = []
    for pair in range(sems.shape[0]):
        values = entries_of(views)
        tile_of = tile_ref[...]
        zero = jnp.zeros_like(values)
        picked = jnp.concatenate([jnp.where(tile_of == 2 * pair + k, values, zero) for k in range(2)], axis=1)
        sums = jnp.dot(same_ref[...], picked, preferred_element_type=jnp.float32)
        for k in range(2):
            tile = 2 * pair + k
            where = pl.ds(tile * TILE, TILE)
            mean_ref[where, :] = sums[:, k * lanes : (k + 1) * lanes] * inverse_ref[:, tile : tile + 1]
            copy = pltpu.make_async_copy(mean_ref.at[where], out_ref.at[where], sems.at[pair, k])
            copy.start()
            copies.append(copy)
    for copy in copies:
        copy.wait()


def pair_dense(parts):
    _, pairs, rows, _ = parts[0].shape
    entries = len(parts) * pairs * (rows - META)
    prepared = dense_prepare(parts, entries)
    return dense_tiles(parts, prepared)


def dense_prepare(parts, entries):
    lanes = parts[0].shape[3]
    return pl.pallas_call(
        dense_prepare_kernel,
        out_shape=[
            jax.ShapeDtypeStruct((TILE, entries), jnp.bfloat16),
            jax.ShapeDtypeStruct((entries, lanes), jnp.bfloat16),
            jax.ShapeDtypeStruct((TILE, lanes), jnp.float32),
        ],
        in_specs=[vmem_spec()] * len(parts),
        out_specs=[vmem_spec()] * 3,
        cost_estimate=dense_cost(entries, lanes, TILE / BUCKET),
        compiler_params=grant(8 * MIB),
        name="dense_prepare",
    )(*parts)


def dense_tiles(parts, prepared):
    entries, lanes = prepared[1].shape
    return pl.pallas_call(
        dense_tiles_kernel,
        out_shape=jax.ShapeDtypeStruct((BUCKET, lanes), jnp.float32),
        in_specs=[vmem_spec()] * (len(parts) + 3),
        out_specs=hbm_spec(),
        scratch_shapes=[
            pltpu.VMEM((BUCKET, lanes), jnp.float32),
            pltpu.SemaphoreType.DMA((BUCKET // (2 * TILE), 2)),
        ],
        cost_estimate=dense_cost(entries, lanes),
        compiler_params=grant(16 * MIB),
        name="dense_tiles",
    )(*parts, *prepared)


def by_pairs(values, slots, counts, groups):
    members = values.shape[0]
    pairs = members // 2

    def swap(array, axis, size, by):
        return lax.ppermute(array, axis, [(i, i ^ by) for i in range(size)])

    sent = pack(values, slots, counts, groups, True)
    mine = [sent[0]] + [swap(sent[k], "mem", members, 2 * k) for k in range(1, pairs)]
    mine = jnp.stack(mine, axis=1)
    parts = [mine] + [swap(mine, "grp", groups, k) for k in range(1, groups)]
    parts = parts + [swap(part, "mem", members, 1) for part in parts]
    answers = pair_answer(parts)
    averaged = pair_dense(parts)
    back = [answers[0]] + [swap(answers[k], "mem", members, 2 * k) for k in range(1, pairs)]
    return averaged, place(back)


def by_all(values, slots, counts, groups):
    members = values.shape[0]
    (lists,) = pack(values, slots, counts, groups, False)
    got = lax.all_to_all(lists, ("grp", "mem"), split_axis=0, concat_axis=0, tiled=True)
    back = answer(got, members)
    returned = lax.all_to_all(back, "mem", split_axis=0, concat_axis=0, tiled=True)
    return dense(got), returned


def per_device(groups, values, slots, counts):
    members, capacity, lanes = values.shape[1:]
    entries = groups * members * capacity
    few = members in (2, 4, 8) and groups in (1, 2, 4, 8) and entries <= 2048
    tiles = BUCKET % (2 * TILE) == 0 and BUCKET // TILE <= lanes
    move = by_pairs if few and tiles else by_all
    averaged, returned = move(values[0], slots[0], counts, groups)
    return (averaged, returned[None])


def one_step(groups, values, slots, counts):
    return per_device(groups, values, slots, counts)


def solution(mesh):
    return jax.shard_map(
        functools.partial(one_step, mesh.shape["grp"]),
        mesh=mesh,
        in_specs=(
            P(("grp", "mem"), None, None, None),
            P(("grp", "mem"), None, None),
            P(("grp", "mem"), None),
        ),
        out_specs=(P("mem", None), P(("grp", "mem"), None, None, None)),
        check_vma=False,
    )
```

time: 31 us -> 31.4 us (1.013)
  blocking collectives: 19.2 us -> 0 us
  waiting for transfers between devices: 0.42 us -> 10.2 us
  starting transfers between devices: 4.06 us -> 13.8 us
    all_to_all x1 -> x0, blocking collectives: 19.2 us -> none  [per_device(): lax.all_to_all(lists, ('grp', 'mem'), split_axis=0, concat_axis=0, tiled=...]
    ppermute x4 -> x13, waiting for transfers between devices: 0.42 us -> 10.2 us  [swap(): return lax.ppermute(array, axis, [(i, i ^ by) for i in range(size)])]
    ppermute x4 -> x13, starting transfers between devices: 4.06 us -> 13.8 us  [swap(): return lax.ppermute(array, axis, [(i, i ^ by) for i in range(size)])]
  transfers between devices with their start and end apart: 4 -> 13, of which waited for: 1 -> 6; matrix products, arithmetic and copies ran while one was open for 0% -> 0% of each run, Pallas kernels for 13% -> 13%
where the time goes in v5:
time: 31.4 us; the launch traced here: 31.2 us
  starting transfers between devices  13.8 us (44%)
  waiting for transfers between devices  10.2 us (32%)
  Pallas kernels  5.68 us (18%)
  local copies, waits for them, and re-layouts  0.81 us (3%)
  between operations  0.74 us (2%)
    ppermute x13, starting transfers between devices, swap(): return lax.ppermute(array, axis, [(i, i ^ by) for i in range(size)])  13.8 us
    ppermute x13, waiting for transfers between devices, swap(): return lax.ppermute(array, axis, [(i, i ^ by) for i in range(size)])  10.2 us
    pallas_call x1, Pallas kernels, dense_tiles(): pl.pallas_call(dense_tiles_kernel, out_shape=jax.ShapeDtypeStruct((BUCKET...  3.46 us
    unnamed x6, local copies, waits for them, and re-layouts  0.81 us
    pallas_call x1, Pallas kernels, pair_answer(): pl.pallas_call(functools.partial(pair_answer_kernel, len(parts)), out_sha...  0.71 us
    pallas_call x1, Pallas kernels, place(): pl.pallas_call(place_kernel, out_shape=jax.ShapeDtypeStruct((two * len(pa...  0.67 us
    pallas_call x1, Pallas kernels, dense_prepare(): pl.pallas_call(dense_prepare_kernel, out_shape=[jax.ShapeDtypeStruct((TIL...  0.66 us
  transfers between devices with their start and end apart: 13, of which 6 were waited for; matrix products, arithmetic and copies ran while one was open for 0% of the time, Pallas kernels for 13%

profile of v5, /device:TPU:0, one launch (start us, length us, event | category | flops | bytes accessed | tf_op | source)
XLA Modules:
  0.0 31.2 jit_solution(9652931352508806170)
XLA Ops:
  0.7 0.8 %copy-done = bf16[1,8,32,128]{3,2,1,0:T(8,128)(2,1)S(1)} copy-done((bf16[1,8,32,128]{3,2,1,0:T(8,128)(2,1)S(1)}, bf16[1,8,32,128]{3,2,1,0:T(8,128)(2,1)}, u32[]{:S(2)}) %copy-start) | copy-done | bytes 65560
  1.5 0.2 pack.1
  1.6 5.1 %collective-permute-start.2 = (bf16[2,40,128]{2,1,0:T(8,128)(2,1)S(1)}, bf16[2,40,128]{2,1,0:T(8,128)(2,1)S(1)}, u32[]{:S(2)}, u32[]{:S(2)}) collective-permute-start(bf16[2,40,128]{2,1,0:T(8,128)(2,1)S(1)} %get-tuple-element.16), channel_id=1, source_target_pairs={{0,6},{1,7},{2,4},{3,5},{4,2},{5,3},{6,0},{7,1},{8,14},{9,15},{10,... | collective-permute-start | bytes 61448 | tf_op jit(solution)/shard_map/ppermute | solution.py:361
  6.8 0.0 collective-permute-start.1
  6.8 0.6 %collective-permute-start = (bf16[2,40,128]{2,1,0:T(8,128)(2,1)S(1)}, bf16[2,40,128]{2,1,0:T(8,128)(2,1)S(1)}, u32[]{:S(2)}, u32[]{:S(2)}) collective-permute-start(bf16[2,40,128]{2,1,0:T(8,128)(2,1)S(1)} %get-tuple-element.14), channel_id=1, source_target_pairs={{0,2},{1,3},{2,0},{3,1},{4,6},{5,7},{6,4},{7,5},{8,10},{9,11},{10,... | collective-permute-start | bytes 61448 | tf_op jit(solution)/shard_map/ppermute | solution.py:361
  7.4 1.1 %collective-permute-done.2 = bf16[2,40,128]{2,1,0:T(8,128)(2,1)S(1)} collective-permute-done((bf16[2,40,128]{2,1,0:T(8,128)(2,1)S(1)}, bf16[2,40,128]{2,1,0:T(8,128)(2,1)S(1)}, u32[]{:S(2)}, u32[]{:S(2)}) %collective-permute-start.2) | collective-permute-done | bytes 20512 | tf_op jit(solution)/shard_map/ppermute | solution.py:361
  8.6 2.9 %collective-permute-done.1 = bf16[2,40,128]{2,1,0:T(8,128)(2,1)S(1)} collective-permute-done((bf16[2,40,128]{2,1,0:T(8,128)(2,1)S(1)}, bf16[2,40,128]{2,1,0:T(8,128)(2,1)S(1)}, u32[]{:S(2)}, u32[]{:S(2)}) %collective-permute-start.1) | collective-permute-done | bytes 20512 | tf_op jit(solution)/shard_map/ppermute | solution.py:361
  11.5 0.0 collective-permute-done
  11.5 1.6 %collective-permute-start.3 = (bf16[2,4,40,128]{3,2,1,0:T(8,128)(2,1)S(1)}, bf16[2,4,40,128]{3,2,1,0:T(8,128)(2,1)S(1)}, u32[]{:S(2)}, u32[]{:S(2)}) collective-permute-start(bf16[2,4,40,128]{3,2,1,0:T(8,128)(2,1)S(1)} %pad_maximum_fusion.refs_0_), channel_id=1, source_target_pairs={{0,8},{8,0},{16,24},{24,16},{1,9},{9,1},{17,25},{25,17},{2,10},{10... | collective-permute-start | bytes 245768 | tf_op jit(solution)/shard_map/ppermute | solution.py:361
  13.1 1.5 %collective-permute-start.4 = (bf16[2,4,40,128]{3,2,1,0:T(8,128)(2,1)S(1)}, bf16[2,4,40,128]{3,2,1,0:T(8,128)(2,1)S(1)}, u32[]{:S(2)}, u32[]{:S(2)}) collective-permute-start(bf16[2,4,40,128]{3,2,1,0:T(8,128)(2,1)S(1)} %pad_maximum_fusion.refs_0_), channel_id=1, source_target_pairs={{0,16},{8,24},{16,0},{24,8},{1,17},{9,25},{17,1},{25,9},{2,18},{10... | collective-permute-start | bytes 245768 | tf_op jit(solution)/shard_map/ppermute | solution.py:361
  14.6 0.5 %collective-permute-start.5 = (bf16[2,4,40,128]{3,2,1,0:T(8,128)(2,1)S(1)}, bf16[2,4,40,128]{3,2,1,0:T(8,128)(2,1)S(1)}, u32[]{:S(2)}, u32[]{:S(2)}) collective-permute-start(bf16[2,4,40,128]{3,2,1,0:T(8,128)(2,1)S(1)} %pad_maximum_fusion.refs_0_), channel_id=1, source_target_pairs={{0,24},{8,16},{16,8},{24,0},{1,25},{9,17},{17,9},{25,1},{2,26},{10... | collective-permute-start | bytes 245768 | tf_op jit(solution)/shard_map/ppermute | solution.py:361
  15.1 0.0 collective-permute-start.6
  15.1 1.7 %collective-permute-done.3.refs_1_ = bf16[2,4,40,128]{3,2,1,0:T(8,128)(2,1)S(1)} collective-permute-done((bf16[2,4,40,128]{3,2,1,0:T(8,128)(2,1)S(1)}, bf16[2,4,40,128]{3,2,1,0:T(8,128)(2,1)S(1)}, u32[]{:S(2)}, u32[]{:S(2)}) %collective-permute-start.3) | collective-permute-done | bytes 81952 | tf_op jit(solution)/shard_map/ppermute | solution.py:361
  16.7 0.0 collective-permute-start.7
  16.7 1.2 %collective-permute-done.4.refs_2_ = bf16[2,4,40,128]{3,2,1,0:T(8,128)(2,1)S(1)} collective-permute-done((bf16[2,4,40,128]{3,2,1,0:T(8,128)(2,1)S(1)}, bf16[2,4,40,128]{3,2,1,0:T(8,128)(2,1)S(1)}, u32[]{:S(2)}, u32[]{:S(2)}) %collective-permute-start.4) | collective-permute-done | bytes 81952 | tf_op jit(solution)/shard_map/ppermute | solution.py:361
  17.9 0.0 collective-permute-start.8
  17.9 2.0 %collective-permute-done.5.refs_3_ = bf16[2,4,40,128]{3,2,1,0:T(8,128)(2,1)S(1)} collective-permute-done((bf16[2,4,40,128]{3,2,1,0:T(8,128)(2,1)S(1)}, bf16[2,4,40,128]{3,2,1,0:T(8,128)(2,1)S(1)}, u32[]{:S(2)}, u32[]{:S(2)}) %collective-permute-start.5) | collective-permute-done | bytes 81952 | tf_op jit(solution)/shard_map/ppermute | solution.py:361
  19.9 0.0 collective-permute-start.9
  19.9 0.0 collective-permute-done.6.refs_4_
  19.9 0.0 collective-permute-done.7.refs_5_
  19.9 0.0 collective-permute-done.8.refs_6_
  19.9 1.3 %collective-permute-done.9.refs_7_ = bf16[2,4,40,128]{3,2,1,0:T(8,128)(2,1)S(1)} collective-permute-done((bf16[2,4,40,128]{3,2,1,0:T(8,128)(2,1)S(1)}, bf16[2,4,40,128]{3,2,1,0:T(8,128)(2,1)S(1)}, u32[]{:S(2)}, u32[]{:S(2)}) %collective-permute-start.9) | collective-permute-done | bytes 81952 | tf_op jit(solution)/shard_map/ppermute | solution.py:361
  21.2 0.7 %pair_answer.1 = (bf16[2,32,128]{2,1,0:T(8,128)(2,1)S(1)}, bf16[2,32,128]{2,1,0:T(8,128)(2,1)S(1)}, bf16[2,32,128]{2,1,0:T(8,128)(2,1)S(1)}, bf16[2,32,128]{2,1,0:T(8,128)(2,1)S(1)}) custom-call(bf16[2,4,40,128]{3,2,1,0:T(8,128)(2,1)S(1)} %pad_maximum_fusion.refs_0_, bf16[2,4,40,128]{3,2,1,0:T(8,128)(2,1)S(1)} %collective-permute-done.3.refs_1_, ...), custom_call_target="tpu_custom_call" | custom-call | tf_op jit(solution)/shard_map/pair_answer/pallas_call | solution.py:197
  21.9 0.1 collective-permute-start.10
  22.0 2.1 %collective-permute-start.11 = (bf16[2,32,128]{2,1,0:T(8,128)(2,1)S(1)}, bf16[2,32,128]{2,1,0:T(8,128)(2,1)S(1)}, u32[]{:S(2)}, u32[]{:S(2)}) collective-permute-start(bf16[2,32,128]{2,1,0:T(8,128)(2,1)S(1)} %get-tuple-element.22), channel_id=1, source_target_pairs={{0,4},{1,5},{2,6},{3,7},{4,0},{5,1},{6,2},{7,3},{8,12},{9,13},{10,... | collective-permute-start | bytes 49160 | tf_op jit(solution)/shard_map/ppermute | solution.py:361
  24.1 2.3 %collective-permute-start.12 = (bf16[2,32,128]{2,1,0:T(8,128)(2,1)S(1)}, bf16[2,32,128]{2,1,0:T(8,128)(2,1)S(1)}, u32[]{:S(2)}, u32[]{:S(2)}) collective-permute-start(bf16[2,32,128]{2,1,0:T(8,128)(2,1)S(1)} %get-tuple-element.23), channel_id=1, source_target_pairs={{0,6},{1,7},{2,4},{3,5},{4,2},{5,3},{6,0},{7,1},{8,14},{9,15},{10,... | collective-permute-start | bytes 49160 | tf_op jit(solution)/shard_map/ppermute | solution.py:361
  26.4 0.7 %dense_prepare.1 = (bf16[512,1024]{1,0:T(8,128)(2,1)S(1)}, bf16[1024,128]{1,0:T(8,128)(2,1)S(1)}, f32[512,128]{1,0:T(8,128)S(1)}) custom-call(bf16[2,4,40,128]{3,2,1,0:T(8,128)(2,1)S(1)} %pad_maximum_fusion.refs_0_, bf16[2,4,40,128]{3,2,1,0:T(8,128)(2,1)S(1)} %collective-permute-done.3.refs_1_, bf16[2,4,40,128]{3,2,1,0:T(8,128)(2,1)S(1)} %collective-permute-done.4.refs_2_, ...), custom_call_target="tpu_custom_call" | custom-call | flops 134217728 | bytes 262144 | tf_op jit(solution)/shard_map/dense_prepare/pallas_call | solution.py:324
  27.0 3.5 %dense_tiles.1 = f32[7168,128]{1,0:T(8,128)} custom-call(bf16[2,4,40,128]{3,2,1,0:T(8,128)(2,1)S(1)} %pad_maximum_fusion.refs_0_, bf16[2,4,40,128]{3,2,1,0:T(8,128)(2,1)S(1)} %collective-permute-done.3.refs_1_, bf16[2,4,40,128]{3,2,1,0:T(8,128)(2,1)S(1)} %collective-permute-done.4.refs_2_, bf16[2,4,40,128]{3,2,1,0:T(8,128)(2,1)S(1)} %collective-permute-done.5.refs_3_, ...), custom_call_target="tpu_custom_call" | custom-call | flops 1879048192 | bytes 3670016 | tf_op jit(solution)/shard_map/dense_tiles/pallas_call | solution.py:341
  30.5 0.0 collective-permute-done.10.refs_1_
  30.5 0.0 collective-permute-done.11.refs_2_
  30.5 0.0 collective-permute-done.12.refs_3_
  30.5 0.7 %place.1 = bf16[8,32,128]{2,1,0:T(8,128)(2,1)} custom-call(bf16[2,32,128]{2,1,0:T(8,128)(2,1)S(1)} %get-tuple-element.20.refs_0_, bf16[2,32,128]{2,1,0:T(8,128)(2,1)S(1)} %collective-permute-done.10.refs_1_, bf16[2,32,128]{2,1,0:T(8,128)(2,1)S(1)} %collective-permute-done.11.refs_2_, bf16[2,32,128]{2,1,0:T(8,128)(2,1)S(1)} %collective-permute-done.12.refs_3_), custom_call_target="tpu_custom_call" | custom-call | tf_op jit(solution)/shard_map/place/pallas_call | solution.py:222
  (7 shorter events, 0.0 us)
Async XLA Ops:
  0.6 0.8 %copy-start = (bf16[1,8,32,128]{3,2,1,0:T(8,128)(2,1)S(1)}, bf16[1,8,32,128]{3,2,1,0:T(8,128)(2,1)}, u32[]{:S(2)}) copy-start(bf16[1,8,32,128]{3,2,1,0:T(8,128)(2,1)} %param.3) | copy-start | bytes 196612
  0.6 0.8 %copy-start.1 = (s32[1,8,32]{2,1,0:T(8,128)S(1)}, s32[1,8,32]{2,1,0:T(8,128)}, u32[]{:S(2)}) copy-start(s32[1,8,32]{2,1,0:T(8,128)} %param.4) | copy-start | bytes 3076
  0.6 0.8 %copy-start.2 = (s32[1,8]{1,0:T(1,128)S(1)}, s32[1,8]{1,0:T(1,128)}, u32[]{:S(2)}) copy-start(s32[1,8]{1,0:T(1,128)} %counts_ref.1) | copy-start | bytes 100
  1.6 6.9 %collective-permute-start.2 = (bf16[2,40,128]{2,1,0:T(8,128)(2,1)S(1)}, bf16[2,40,128]{2,1,0:T(8,128)(2,1)S(1)}, u32[]{:S(2)}, u32[]{:S(2)}) collective-permute-start(bf16[2,40,128]{2,1,0:T(8,128)(2,1)S(1)} %get-tuple-element.16), channel_id=1, source_target_pairs={{0,6},{1,7},{2,4},{3,5},{4,2},{5,3},{6,0},{7,1},{8,14},{9,15},{10,... | collective-permute-start | bytes 61448 | tf_op jit(solution)/shard_map/ppermute | solution.py:361
  6.8 4.7 %collective-permute-start.1 = (bf16[2,40,128]{2,1,0:T(8,128)(2,1)S(1)}, bf16[2,40,128]{2,1,0:T(8,128)(2,1)S(1)}, u32[]{:S(2)}, u32[]{:S(2)}) collective-permute-start(bf16[2,40,128]{2,1,0:T(8,128)(2,1)S(1)} %get-tuple-element.15), channel_id=1, source_target_pairs={{0,4},{1,5},{2,6},{3,7},{4,0},{5,1},{6,2},{7,3},{8,12},{9,13},{10,... | collective-permute-start | bytes 61448 | tf_op jit(solution)/shard_map/ppermute | solution.py:361
  6.8 4.7 %collective-permute-start = (bf16[2,40,128]{2,1,0:T(8,128)(2,1)S(1)}, bf16[2,40,128]{2,1,0:T(8,128)(2,1)S(1)}, u32[]{:S(2)}, u32[]{:S(2)}) collective-permute-start(bf16[2,40,128]{2,1,0:T(8,128)(2,1)S(1)} %get-tuple-element.14), channel_id=1, source_target_pairs={{0,2},{1,3},{2,0},{3,1},{4,6},{5,7},{6,4},{7,5},{8,10},{9,11},{10,... | collective-permute-start | bytes 61448 | tf_op jit(solution)/shard_map/ppermute | solution.py:361
  11.5 5.2 %collective-permute-start.3 = (bf16[2,4,40,128]{3,2,1,0:T(8,128)(2,1)S(1)}, bf16[2,4,40,128]{3,2,1,0:T(8,128)(2,1)S(1)}, u32[]{:S(2)}, u32[]{:S(2)}) collective-permute-start(bf16[2,4,40,128]{3,2,1,0:T(8,128)(2,1)S(1)} %pad_maximum_fusion.refs_0_), channel_id=1, source_target_pairs={{0,8},{8,0},{16,24},{24,16},{1,9},{9,1},{17,25},{25,17},{2,10},{10... | collective-permute-start | bytes 245768 | tf_op jit(solution)/shard_map/ppermute | solution.py:361
  13.1 4.9 %collective-permute-start.4 = (bf16[2,4,40,128]{3,2,1,0:T(8,128)(2,1)S(1)}, bf16[2,4,40,128]{3,2,1,0:T(8,128)(2,1)S(1)}, u32[]{:S(2)}, u32[]{:S(2)}) collective-permute-start(bf16[2,4,40,128]{3,2,1,0:T(8,128)(2,1)S(1)} %pad_maximum_fusion.refs_0_), channel_id=1, source_target_pairs={{0,16},{8,24},{16,0},{24,8},{1,17},{9,25},{17,1},{25,9},{2,18},{10... | collective-permute-start | bytes 245768 | tf_op jit(solution)/shard_map/ppermute | solution.py:361
  14.6 5.3 %collective-permute-start.5 = (bf16[2,4,40,128]{3,2,1,0:T(8,128)(2,1)S(1)}, bf16[2,4,40,128]{3,2,1,0:T(8,128)(2,1)S(1)}, u32[]{:S(2)}, u32[]{:S(2)}) collective-permute-start(bf16[2,4,40,128]{3,2,1,0:T(8,128)(2,1)S(1)} %pad_maximum_fusion.refs_0_), channel_id=1, source_target_pairs={{0,24},{8,16},{16,8},{24,0},{1,25},{9,17},{17,9},{25,1},{2,26},{10... | collective-permute-start | bytes 245768 | tf_op jit(solution)/shard_map/ppermute | solution.py:361
  15.1 4.9 %collective-permute-start.6 = (bf16[2,4,40,128]{3,2,1,0:T(8,128)(2,1)S(1)}, bf16[2,4,40,128]{3,2,1,0:T(8,128)(2,1)S(1)}, u32[]{:S(2)}, u32[]{:S(2)}) collective-permute-start(bf16[2,4,40,128]{3,2,1,0:T(8,128)(2,1)S(1)} %pad_maximum_fusion.refs_0_), channel_id=1, source_target_pairs={{0,1},{1,0},{2,3},{3,2},{4,5},{5,4},{6,7},{7,6},{8,9},{9,8},{10,11... | collective-permute-start | bytes 245768 | tf_op jit(solution)/shard_map/ppermute | solution.py:361
  16.7 3.2 %collective-permute-start.7 = (bf16[2,4,40,128]{3,2,1,0:T(8,128)(2,1)S(1)}, bf16[2,4,40,128]{3,2,1,0:T(8,128)(2,1)S(1)}, u32[]{:S(2)}, u32[]{:S(2)}) collective-permute-start(bf16[2,4,40,128]{3,2,1,0:T(8,128)(2,1)S(1)} %collective-permute-done.3.refs_1_), channel_id=1, source_target_pairs={{0,1},{1,0},{2,3},{3,2},{4,5},{5,4},{6,7},{7,6},{8,9},{9,8},{10,11... | collective-permute-start | bytes 245768 | tf_op jit(solution)/shard_map/ppermute | solution.py:361
  17.9 2.0 %collective-permute-start.8 = (bf16[2,4,40,128]{3,2,1,0:T(8,128)(2,1)S(1)}, bf16[2,4,40,128]{3,2,1,0:T(8,128)(2,1)S(1)}, u32[]{:S(2)}, u32[]{:S(2)}) collective-permute-start(bf16[2,4,40,128]{3,2,1,0:T(8,128)(2,1)S(1)} %collective-permute-done.4.refs_2_), channel_id=1, source_target_pairs={{0,1},{1,0},{2,3},{3,2},{4,5},{5,4},{6,7},{7,6},{8,9},{9,8},{10,11... | collective-permute-start | bytes 245768 | tf_op jit(solution)/shard_map/ppermute | solution.py:361
  19.9 1.3 %collective-permute-start.9 = (bf16[2,4,40,128]{3,2,1,0:T(8,128)(2,1)S(1)}, bf16[2,4,40,128]{3,2,1,0:T(8,128)(2,1)S(1)}, u32[]{:S(2)}, u32[]{:S(2)}) collective-permute-start(bf16[2,4,40,128]{3,2,1,0:T(8,128)(2,1)S(1)} %collective-permute-done.5.refs_3_), channel_id=1, source_target_pairs={{0,1},{1,0},{2,3},{3,2},{4,5},{5,4},{6,7},{7,6},{8,9},{9,8},{10,11... | collective-permute-start | bytes 245768 | tf_op jit(solution)/shard_map/ppermute | solution.py:361
  21.9 8.6 %collective-permute-start.10 = (bf16[2,32,128]{2,1,0:T(8,128)(2,1)S(1)}, bf16[2,32,128]{2,1,0:T(8,128)(2,1)S(1)}, u32[]{:S(2)}, u32[]{:S(2)}) collective-permute-start(bf16[2,32,128]{2,1,0:T(8,128)(2,1)S(1)} %get-tuple-element.21), channel_id=1, source_target_pairs={{0,2},{1,3},{2,0},{3,1},{4,6},{5,7},{6,4},{7,5},{8,10},{9,11},{10,... | collective-permute-start | bytes 49160 | tf_op jit(solution)/shard_map/ppermute | solution.py:361
  22.0 8.5 %collective-permute-start.11 = (bf16[2,32,128]{2,1,0:T(8,128)(2,1)S(1)}, bf16[2,32,128]{2,1,0:T(8,128)(2,1)S(1)}, u32[]{:S(2)}, u32[]{:S(2)}) collective-permute-start(bf16[2,32,128]{2,1,0:T(8,128)(2,1)S(1)} %get-tuple-element.22), channel_id=1, source_target_pairs={{0,4},{1,5},{2,6},{3,7},{4,0},{5,1},{6,2},{7,3},{8,12},{9,13},{10,... | collective-permute-start | bytes 49160 | tf_op jit(solution)/shard_map/ppermute | solution.py:361
  24.1 6.4 %collective-permute-start.12 = (bf16[2,32,128]{2,1,0:T(8,128)(2,1)S(1)}, bf16[2,32,128]{2,1,0:T(8,128)(2,1)S(1)}, u32[]{:S(2)}, u32[]{:S(2)}) collective-permute-start(bf16[2,32,128]{2,1,0:T(8,128)(2,1)S(1)} %get-tuple-element.23), channel_id=1, source_target_pairs={{0,6},{1,7},{2,4},{3,5},{4,2},{5,3},{6,0},{7,1},{8,14},{9,15},{10,... | collective-permute-start | bytes 49160 | tf_op jit(solution)/shard_map/ppermute | solution.py:361

commit v6 on v5

--- a/solution.py
+++ b/solution.py
@@ -137,11 +137,15 @@
     return as_row(high * DIGIT + low, refs[0].shape[1] - META)
 
 
-def answer_some(asking, key, entries):
-    capacity, lanes = asking[0].shape[1] - META, entries.shape[1]
+def asked_column(asking):
+    capacity = asking[0].shape[1] - META
     high, low = digits_of(asking)
     column = as_column(high, capacity) * DIGIT + as_column(low, capacity)
-    column = jnp.where(column < 0.0, -1.0, column)
+    return jnp.where(column < 0.0, -1.0, column)
+
+
+def matching_sums(column, key, entries):
+    lanes = entries.shape[1]
     onehot = jnp.concatenate(
         [
             (column == key[:, at : at + lanes]).astype(jnp.float32).astype(jnp.bfloat16)
@@ -150,9 +154,7 @@
         axis=1,
     )
     sums = jnp.dot(onehot, entries, preferred_element_type=jnp.float32)
-    count = jnp.dot(onehot, jnp.ones_like(entries), preferred_element_type=jnp.float32)
-    mean = sums / jnp.maximum(count, 1.0)
-    return mean.astype(jnp.bfloat16).reshape(-1, capacity, lanes)
+    return sums, jnp.dot(onehot, jnp.ones_like(entries), preferred_element_type=jnp.float32)
 
 
 def answer_kernel(lists_ref, out_ref, key_ref):
@@ -164,7 +166,9 @@
     @pl.loop(0, members, step=step)
     def _(at):
         asking = lists_ref.at[pl.ds(first + at, step)]
-        out_ref[pl.ds(at, step)] = answer_some([asking], key_ref[...], entries_of([lists_ref]))
+        sums, count = matching_sums(asked_column([asking]), key_ref[...], entries_of([lists_ref]))
+        mean = sums / jnp.maximum(count, 1.0)
+        out_ref[pl.ds(at, step)] = mean.astype(jnp.bfloat16).reshape(step, *out_ref.shape[1:])
 
 
 def answer(lists, members):
@@ -182,26 +186,52 @@
     )(lists)
 
 
-def pair_answer_kernel(count, *refs):
-    in_refs, out_refs = refs[:count], refs[count:]
+def begin_answer_kernel(*refs):
+    *in_refs, column_ref, sums_ref, count_ref = refs
     for bucket in range(2):
         views = [ref.at[bucket] for ref in in_refs]
-        mean = answer_some(views[:1], keys_of(views), entries_of(views))
+        column = asked_column(views[:1])
+        sums, count = matching_sums(column, keys_of(views), entries_of(views))
+        column_ref[bucket] = column
+        sums_ref[bucket] = sums
+        count_ref[bucket] = count
+
+
+def finish_answer_kernel(count, *refs):
+    in_refs, (column_ref, sums_ref, count_ref), out_refs = refs[:count], refs[count : count + 3], refs[count + 3 :]
+    for bucket in range(2):
+        views = [ref.at[bucket] for ref in in_refs]
+        sums, number = matching_sums(column_ref[bucket], keys_of(views), entries_of(views))
+        mean = (sums_ref[bucket] + sums) / jnp.maximum(count_ref[bucket] + number, 1.0)
+        mean = mean.astype(jnp.bfloat16).reshape(len(out_refs), *out_refs[0].shape[1:])
         for k, out_ref in enumerate(out_refs):
             out_ref[bucket] = mean[k]
 
 
-def pair_answer(parts):
+def begin_answer(parts):
+    pairs, rows, lanes = parts[0].shape[1:]
+    partial = jax.ShapeDtypeStruct((2, pairs * (rows - META), lanes), jnp.float32)
+    return pl.pallas_call(
+        begin_answer_kernel,
+        out_shape=[partial] * 3,
+        in_specs=[vmem_spec()] * len(parts),
+        out_specs=[vmem_spec()] * 3,
+        compiler_params=grant(8 * MIB),
+        name="begin_answer",
+    )(*parts)
+
+
+def finish_answer(parts, begun):
     pairs, rows, lanes = parts[0].shape[1:]
     shape = jax.ShapeDtypeStruct((2, rows - META, lanes), jnp.bfloat16)
     return pl.pallas_call(
-        functools.partial(pair_answer_kernel, len(parts)),
+        functools.partial(finish_answer_kernel, len(parts)),
         out_shape=[shape] * pairs,
-        in_specs=[vmem_spec()] * len(parts),
+        in_specs=[vmem_spec()] * (len(parts) + 3),
         out_specs=[vmem_spec()] * pairs,
         compiler_params=grant(8 * MIB),
-        name="pair_answer",
-    )(*parts)
+        name="finish_answer",
+    )(*parts, *begun)
 
 
 def place_kernel(*refs):
@@ -270,7 +300,7 @@
 
 
 def dense_prepare_kernel(*refs):
-    *in_refs, same_ref, tile_ref, inverse_ref = refs
+    *in_refs, same_ref, tile_ref, number_ref = refs
     views = own_bucket(in_refs)
     capacity, lanes = views[0].shape[1] - META, views[0].shape[2]
     entries = same_ref.shape[1]
@@ -286,21 +316,40 @@
     tile_ref[...] = tile_column.astype(jnp.bfloat16)
     lane = lax.broadcasted_iota(jnp.int32, (entries, lanes), 1).astype(jnp.float32)
     in_tile = (tile_column == lane).astype(jnp.float32).astype(jnp.bfloat16)
-    number = jnp.dot(same_ref[...], in_tile, preferred_element_type=jnp.float32)
-    inverse_ref[...] = 1.0 / jnp.maximum(number, 1.0)
-
-
-def dense_tiles_kernel(*refs):
-    *in_refs, same_ref, tile_ref, inverse_ref, out_ref, mean_ref, sems = refs
+    number_ref[...] = jnp.dot(same_ref[...], in_tile, preferred_element_type=jnp.float32)
+
+
+def dense_prepare(parts):
+    pairs, rows, lanes = parts[0].shape[1:]
+    entries = len(parts) * pairs * (rows - META)
+    return pl.pallas_call(
+        dense_prepare_kernel,
+        out_shape=[
+            jax.ShapeDtypeStruct((TILE, entries), jnp.bfloat16),
+            jax.ShapeDtypeStruct((entries, lanes), jnp.bfloat16),
+            jax.ShapeDtypeStruct((TILE, lanes), jnp.float32),
+        ],
+        in_specs=[vmem_spec()] * len(parts),
+        out_specs=[vmem_spec()] * 3,
+        compiler_params=grant(8 * MIB),
+        name="dense_prepare",
+    )(*parts)
+
+
+def dense_tiles_kernel(count, *refs):
+    in_refs, prepared = refs[:count], refs[count : count + 6]
+    out_ref, mean_ref, inverse_ref, sems = refs[count + 6 :]
     views = own_bucket(in_refs)
     lanes = views[0].shape[2]
+    inverse_ref[...] = 1.0 / jnp.maximum(prepared[2][...] + prepared[5][...], 1.0)
     copies = []
     for pair in range(sems.shape[0]):
         values = entries_of(views)
-        tile_of = tile_ref[...]
+        tile_of = jnp.concatenate([prepared[1][...], prepared[4][...]], axis=0)
+        same = jnp.concatenate([prepared[0][...], prepared[3][...]], axis=1)
         zero = jnp.zeros_like(values)
         picked = jnp.concatenate([jnp.where(tile_of == 2 * pair + k, values, zero) for k in range(2)], axis=1)
-        sums = jnp.dot(same_ref[...], picked, preferred_element_type=jnp.float32)
+        sums = jnp.dot(same, picked, preferred_element_type=jnp.float32)
         for k in range(2):
             tile = 2 * pair + k
             where = pl.ds(tile * TILE, TILE)
@@ -312,39 +361,17 @@
         copy.wait()
 
 
-def pair_dense(parts):
-    _, pairs, rows, _ = parts[0].shape
+def dense_tiles(parts, prepared):
+    pairs, rows, lanes = parts[0].shape[1:]
     entries = len(parts) * pairs * (rows - META)
-    prepared = dense_prepare(parts, entries)
-    return dense_tiles(parts, prepared)
-
-
-def dense_prepare(parts, entries):
-    lanes = parts[0].shape[3]
-    return pl.pallas_call(
-        dense_prepare_kernel,
-        out_shape=[
-            jax.ShapeDtypeStruct((TILE, entries), jnp.bfloat16),
-            jax.ShapeDtypeStruct((entries, lanes), jnp.bfloat16),
-            jax.ShapeDtypeStruct((TILE, lanes), jnp.float32),
-        ],
-        in_specs=[vmem_spec()] * len(parts),
-        out_specs=[vmem_spec()] * 3,
-        cost_estimate=dense_cost(entries, lanes, TILE / BUCKET),
-        compiler_params=grant(8 * MIB),
-        name="dense_prepare",
-    )(*parts)
-
-
-def dense_tiles(parts, prepared):
-    entries, lanes = prepared[1].shape
-    return pl.pallas_call(
-        dense_tiles_kernel,
+    return pl.pallas_call(
+        functools.partial(dense_tiles_kernel, len(parts)),
         out_shape=jax.ShapeDtypeStruct((BUCKET, lanes), jnp.float32),
-        in_specs=[vmem_spec()] * (len(parts) + 3),
+        in_specs=[vmem_spec()] * (len(parts) + len(prepared)),
         out_specs=hbm_spec(),
         scratch_shapes=[
             pltpu.VMEM((BUCKET, lanes), jnp.float32),
+            pltpu.VMEM((TILE, lanes), jnp.float32),
             pltpu.SemaphoreType.DMA((BUCKET // (2 * TILE), 2)),
         ],
         cost_estimate=dense_cost(entries, lanes),
@@ -363,10 +390,13 @@
     sent = pack(values, slots, counts, groups, True)
     mine = [sent[0]] + [swap(sent[k], "mem", members, 2 * k) for k in range(1, pairs)]
     mine = jnp.stack(mine, axis=1)
-    parts = [mine] + [swap(mine, "grp", groups, k) for k in range(1, groups)]
-    parts = parts + [swap(part, "mem", members, 1) for part in parts]
-    answers = pair_answer(parts)
-    averaged = pair_dense(parts)
+    same = [mine] + [swap(mine, "grp", groups, k) for k in range(1, groups)]
+    other = [swap(part, "mem", members, 1) for part in same]
+    begun = begin_answer(same)
+    prepared = dense_prepare(same)
+    answers = finish_answer(other, begun)
+    prepared += dense_prepare(other)
+    averaged = dense_tiles(same + other, prepared)
     back = [answers[0]] + [swap(answers[k], "mem", members, 2 * k) for k in range(1, pairs)]
     return averaged, place(back)
 

time: 31.4 us -> 30.7 us (0.978)
  waiting for transfers between devices: 10.2 us -> 9.12 us
  Pallas kernels: 5.68 us -> 6.05 us
    ppermute x13, waiting for transfers between devices: 10.2 us -> 9.12 us  [swap(): return lax.ppermute(array, axis, [(i, i ^ by) for i in range(size)])]
    pallas_call x1 -> x2, Pallas kernels: 0.66 us -> 0.92 us  [dense_prepare(): pl.pallas_call(dense_prepare_kernel, out_shape=[jax.ShapeDtypeStruct((TIL...]
    pallas_call x2 -> x3, Pallas kernels: 4.17 us -> 4.3 us  [the longest x1 3.42 us: dense_tiles(): pl.pallas_call(functools.partial(dense_tiles_kernel, len(parts)), out_sha...]
  transfers between devices with their start and end apart: 13 -> 13, of which waited for: 6 -> 6; matrix products, arithmetic and copies ran while one was open for 0% -> 0% of each run, Pallas kernels for 13% -> 16%
where the time goes in v6:
time: 30.7 us; the launch traced here: 30.6 us
  starting transfers between devices  13.8 us (45%)
  waiting for transfers between devices  9.12 us (30%)
  Pallas kernels  6.05 us (20%)
  local copies, waits for them, and re-layouts  0.81 us (3%)
  between operations  0.77 us (3%)
    ppermute x13, starting transfers between devices, swap(): return lax.ppermute(array, axis, [(i, i ^ by) for i in range(size)])  13.8 us
    ppermute x13, waiting for transfers between devices, swap(): return lax.ppermute(array, axis, [(i, i ^ by) for i in range(size)])  9.12 us
    pallas_call x1, Pallas kernels, dense_tiles(): pl.pallas_call(functools.partial(dense_tiles_kernel, len(parts)), out_sha...  3.42 us
    pallas_call x2, Pallas kernels, dense_prepare(): pl.pallas_call(dense_prepare_kernel, out_shape=[jax.ShapeDtypeStruct((TIL...  0.92 us
    unnamed x6, local copies, waits for them, and re-layouts  0.81 us
    pallas_call x1, Pallas kernels, place(): pl.pallas_call(place_kernel, out_shape=jax.ShapeDtypeStruct((two * len(pa...  0.67 us
  transfers between devices with their start and end apart: 13, of which 6 were waited for; matrix products, arithmetic and copies ran while one was open for 0% of the time, Pallas kernels for 16%

profile of v6, /device:TPU:0, one launch (start us, length us, event | category | flops | bytes accessed | tf_op | source)
XLA Modules:
  0.0 30.6 jit_solution(7644197625066521104)
XLA Ops:
  0.7 0.8 %copy-done = bf16[1,8,32,128]{3,2,1,0:T(8,128)(2,1)S(1)} copy-done((bf16[1,8,32,128]{3,2,1,0:T(8,128)(2,1)S(1)}, bf16[1,8,32,128]{3,2,1,0:T(8,128)(2,1)}, u32[]{:S(2)}) %copy-start) | copy-done | bytes 65560
  1.5 0.2 pack.1
  1.6 5.1 %collective-permute-start.2 = (bf16[2,40,128]{2,1,0:T(8,128)(2,1)S(1)}, bf16[2,40,128]{2,1,0:T(8,128)(2,1)S(1)}, u32[]{:S(2)}, u32[]{:S(2)}) collective-permute-start(bf16[2,40,128]{2,1,0:T(8,128)(2,1)S(1)} %get-tuple-element.22), channel_id=1, source_target_pairs={{0,6},{1,7},{2,4},{3,5},{4,2},{5,3},{6,0},{7,1},{8,14},{9,15},{10,... | collective-permute-start | bytes 61448 | tf_op jit(solution)/shard_map/ppermute | solution.py:388
  6.8 0.0 collective-permute-start.1
  6.8 0.6 %collective-permute-start = (bf16[2,40,128]{2,1,0:T(8,128)(2,1)S(1)}, bf16[2,40,128]{2,1,0:T(8,128)(2,1)S(1)}, u32[]{:S(2)}, u32[]{:S(2)}) collective-permute-start(bf16[2,40,128]{2,1,0:T(8,128)(2,1)S(1)} %get-tuple-element.20), channel_id=1, source_target_pairs={{0,2},{1,3},{2,0},{3,1},{4,6},{5,7},{6,4},{7,5},{8,10},{9,11},{10,... | collective-permute-start | bytes 61448 | tf_op jit(solution)/shard_map/ppermute | solution.py:388
  7.4 1.1 %collective-permute-done.2 = bf16[2,40,128]{2,1,0:T(8,128)(2,1)S(1)} collective-permute-done((bf16[2,40,128]{2,1,0:T(8,128)(2,1)S(1)}, bf16[2,40,128]{2,1,0:T(8,128)(2,1)S(1)}, u32[]{:S(2)}, u32[]{:S(2)}) %collective-permute-start.2) | collective-permute-done | bytes 20512 | tf_op jit(solution)/shard_map/ppermute | solution.py:388
  8.6 2.9 %collective-permute-done.1 = bf16[2,40,128]{2,1,0:T(8,128)(2,1)S(1)} collective-permute-done((bf16[2,40,128]{2,1,0:T(8,128)(2,1)S(1)}, bf16[2,40,128]{2,1,0:T(8,128)(2,1)S(1)}, u32[]{:S(2)}, u32[]{:S(2)}) %collective-permute-start.1) | collective-permute-done | bytes 20512 | tf_op jit(solution)/shard_map/ppermute | solution.py:388
  11.5 0.0 collective-permute-done
  11.5 1.6 %collective-permute-start.3 = (bf16[2,4,40,128]{3,2,1,0:T(8,128)(2,1)S(1)}, bf16[2,4,40,128]{3,2,1,0:T(8,128)(2,1)S(1)}, u32[]{:S(2)}, u32[]{:S(2)}) collective-permute-start(bf16[2,4,40,128]{3,2,1,0:T(8,128)(2,1)S(1)} %pad_maximum_fusion.refs_0_), channel_id=1, source_target_pairs={{0,8},{8,0},{16,24},{24,16},{1,9},{9,1},{17,25},{25,17},{2,10},{10... | collective-permute-start | bytes 245768 | tf_op jit(solution)/shard_map/ppermute | solution.py:388
  13.1 1.5 %collective-permute-start.4 = (bf16[2,4,40,128]{3,2,1,0:T(8,128)(2,1)S(1)}, bf16[2,4,40,128]{3,2,1,0:T(8,128)(2,1)S(1)}, u32[]{:S(2)}, u32[]{:S(2)}) collective-permute-start(bf16[2,4,40,128]{3,2,1,0:T(8,128)(2,1)S(1)} %pad_maximum_fusion.refs_0_), channel_id=1, source_target_pairs={{0,16},{8,24},{16,0},{24,8},{1,17},{9,25},{17,1},{25,9},{2,18},{10... | collective-permute-start | bytes 245768 | tf_op jit(solution)/shard_map/ppermute | solution.py:388
  14.6 0.5 %collective-permute-start.5 = (bf16[2,4,40,128]{3,2,1,0:T(8,128)(2,1)S(1)}, bf16[2,4,40,128]{3,2,1,0:T(8,128)(2,1)S(1)}, u32[]{:S(2)}, u32[]{:S(2)}) collective-permute-start(bf16[2,4,40,128]{3,2,1,0:T(8,128)(2,1)S(1)} %pad_maximum_fusion.refs_0_), channel_id=1, source_target_pairs={{0,24},{8,16},{16,8},{24,0},{1,25},{9,17},{17,9},{25,1},{2,26},{10... | collective-permute-start | bytes 245768 | tf_op jit(solution)/shard_map/ppermute | solution.py:388
  15.1 0.0 collective-permute-start.6
  15.1 1.7 %collective-permute-done.3.refs_1_ = bf16[2,4,40,128]{3,2,1,0:T(8,128)(2,1)S(1)} collective-permute-done((bf16[2,4,40,128]{3,2,1,0:T(8,128)(2,1)S(1)}, bf16[2,4,40,128]{3,2,1,0:T(8,128)(2,1)S(1)}, u32[]{:S(2)}, u32[]{:S(2)}) %collective-permute-start.3) | collective-permute-done | bytes 81952 | tf_op jit(solution)/shard_map/ppermute | solution.py:388
  16.7 0.0 collective-permute-start.7
  16.7 1.2 %collective-permute-done.4.refs_2_ = bf16[2,4,40,128]{3,2,1,0:T(8,128)(2,1)S(1)} collective-permute-done((bf16[2,4,40,128]{3,2,1,0:T(8,128)(2,1)S(1)}, bf16[2,4,40,128]{3,2,1,0:T(8,128)(2,1)S(1)}, u32[]{:S(2)}, u32[]{:S(2)}) %collective-permute-start.4) | collective-permute-done | bytes 81952 | tf_op jit(solution)/shard_map/ppermute | solution.py:388
  17.9 0.0 collective-permute-start.8
  17.9 2.0 %collective-permute-done.5.refs_3_ = bf16[2,4,40,128]{3,2,1,0:T(8,128)(2,1)S(1)} collective-permute-done((bf16[2,4,40,128]{3,2,1,0:T(8,128)(2,1)S(1)}, bf16[2,4,40,128]{3,2,1,0:T(8,128)(2,1)S(1)}, u32[]{:S(2)}, u32[]{:S(2)}) %collective-permute-start.5) | collective-permute-done | bytes 81952 | tf_op jit(solution)/shard_map/ppermute | solution.py:388
  19.9 0.0 collective-permute-start.9
  19.9 0.5 %dense_prepare.2 = (bf16[512,512]{1,0:T(8,128)(2,1)S(1)}, bf16[512,128]{1,0:T(8,128)(2,1)S(1)}, f32[512,128]{1,0:T(8,128)S(1)}) custom-call(bf16[2,4,40,128]{3,2,1,0:T(8,128)(2,1)S(1)} %pad_maximum_fusion.refs_0_, bf16[2,4,40,128]{3,2,1,0:T(8,128)(2,1)S(1)} %collective-permute-done.3.refs_1_, bf16[2,4,40,128]{3,2,1,0:T(8,128)(2,1)S(1)} %collective-permute-done.4.refs_2_, ...), custom_call_target="tpu_custom_call" | custom-call | tf_op jit(solution)/shard_map/dense_prepare/pallas_call | solution.py:325
  20.4 0.6 %begin_answer.1 = (f32[2,128,128]{2,1,0:T(8,128)S(1)}, f32[2,128,128]{2,1,0:T(8,128)S(1)}, f32[2,128,128]{2,1,0:T(8,128)S(1)}) custom-call(bf16[2,4,40,128]{3,2,1,0:T(8,128)(2,1)S(1)} %pad_maximum_fusion.refs_0_, bf16[2,4,40,128]{3,2,1,0:T(8,128)(2,1)S(1)} %collective-permute-done.3.refs_1_, bf16[2,4,40,128]{3,2,1,0:T(8,128)(2,1)S(1)} %collective-permute-done.4.refs_2_, ...), custom_call_target="tpu_custom_call" | custom-call | tf_op jit(solution)/shard_map/begin_answer/pallas_call | solution.py:214
  21.0 0.0 collective-permute-done.6.refs_0_.refs_4_
  21.0 0.0 collective-permute-done.7.refs_1_.refs_5_
  21.0 0.0 collective-permute-done.8.refs_2_.refs_6_
  21.0 0.2 collective-permute-done.9.refs_3_.refs_7_
  21.2 0.3 %finish_answer.1 = (bf16[2,32,128]{2,1,0:T(8,128)(2,1)S(1)}, bf16[2,32,128]{2,1,0:T(8,128)(2,1)S(1)}, bf16[2,32,128]{2,1,0:T(8,128)(2,1)S(1)}, bf16[2,32,128]{2,1,0:T(8,128)(2,1)S(1)}) custom-call(bf16[2,4,40,128]{3,2,1,0:T(8,128)(2,1)S(1)} %collective-permute-done.6.refs_0_.refs_4_, bf16[2,4,40,128]{3,2,1,0:T(8,128)(2,1)S(1)} %collective-permute-done.7.refs_1_.refs_5_, ...), custom_call_target="tpu_custom_call" | custom-call | tf_op jit(solution)/shard_map/finish_answer/pallas_call | solution.py:227
  21.5 0.1 collective-permute-start.10
  21.6 2.1 %collective-permute-start.11 = (bf16[2,32,128]{2,1,0:T(8,128)(2,1)S(1)}, bf16[2,32,128]{2,1,0:T(8,128)(2,1)S(1)}, u32[]{:S(2)}, u32[]{:S(2)}) collective-permute-start(bf16[2,32,128]{2,1,0:T(8,128)(2,1)S(1)} %get-tuple-element.34), channel_id=1, source_target_pairs={{0,4},{1,5},{2,6},{3,7},{4,0},{5,1},{6,2},{7,3},{8,12},{9,13},{10,... | collective-permute-start | bytes 49160 | tf_op jit(solution)/shard_map/ppermute | solution.py:388
  23.7 2.3 %collective-permute-start.12 = (bf16[2,32,128]{2,1,0:T(8,128)(2,1)S(1)}, bf16[2,32,128]{2,1,0:T(8,128)(2,1)S(1)}, u32[]{:S(2)}, u32[]{:S(2)}) collective-permute-start(bf16[2,32,128]{2,1,0:T(8,128)(2,1)S(1)} %get-tuple-element.35), channel_id=1, source_target_pairs={{0,6},{1,7},{2,4},{3,5},{4,2},{5,3},{6,0},{7,1},{8,14},{9,15},{10,... | collective-permute-start | bytes 49160 | tf_op jit(solution)/shard_map/ppermute | solution.py:388
  26.0 0.5 %dense_prepare.3 = (bf16[512,512]{1,0:T(8,128)(2,1)S(1)}, bf16[512,128]{1,0:T(8,128)(2,1)S(1)}, f32[512,128]{1,0:T(8,128)S(1)}) custom-call(bf16[2,4,40,128]{3,2,1,0:T(8,128)(2,1)S(1)} %collective-permute-done.6.refs_0_.refs_4_, bf16[2,4,40,128]{3,2,1,0:T(8,128)(2,1)S(1)} %collective-permute-done.7.refs_1_.refs_5_, ...), custom_call_target="tpu_custom_call" | custom-call | tf_op jit(solution)/shard_map/dense_prepare/pallas_call | solution.py:325
  26.4 3.4 %dense_tiles.1 = f32[7168,128]{1,0:T(8,128)} custom-call(bf16[2,4,40,128]{3,2,1,0:T(8,128)(2,1)S(1)} %pad_maximum_fusion.refs_0_, bf16[2,4,40,128]{3,2,1,0:T(8,128)(2,1)S(1)} %collective-permute-done.3.refs_1_, bf16[2,4,40,128]{3,2,1,0:T(8,128)(2,1)S(1)} %collective-permute-done.4.refs_2_, bf16[2,4,40,128]{3,2,1,0:T(8,128)(2,1)S(1)} %collective-permute-done.5.refs_3_, ...), custom_call_target="tpu_custom_call" | custom-call | flops 1879048192 | bytes 3670016 | tf_op jit(solution)/shard_map/dense_tiles/pallas_call | solution.py:367
  29.9 0.0 collective-permute-done.11.refs_2_
  29.9 0.7 %place.1 = bf16[8,32,128]{2,1,0:T(8,128)(2,1)} custom-call(bf16[2,32,128]{2,1,0:T(8,128)(2,1)S(1)} %get-tuple-element.32.refs_0_, bf16[2,32,128]{2,1,0:T(8,128)(2,1)S(1)} %collective-permute-done.10.refs_1_, bf16[2,32,128]{2,1,0:T(8,128)(2,1)S(1)} %collective-permute-done.11.refs_2_, bf16[2,32,128]{2,1,0:T(8,128)(2,1)S(1)} %collective-permute-done.12.refs_3_), custom_call_target="tpu_custom_call" | custom-call | tf_op jit(solution)/shard_map/place/pallas_call | solution.py:252
  (9 shorter events, 0.0 us)
Async XLA Ops:
  0.6 0.8 %copy-start = (bf16[1,8,32,128]{3,2,1,0:T(8,128)(2,1)S(1)}, bf16[1,8,32,128]{3,2,1,0:T(8,128)(2,1)}, u32[]{:S(2)}) copy-start(bf16[1,8,32,128]{3,2,1,0:T(8,128)(2,1)} %param.3) | copy-start | bytes 196612
  0.6 0.8 %copy-start.1 = (s32[1,8,32]{2,1,0:T(8,128)S(1)}, s32[1,8,32]{2,1,0:T(8,128)}, u32[]{:S(2)}) copy-start(s32[1,8,32]{2,1,0:T(8,128)} %param.4) | copy-start | bytes 3076
  0.6 0.8 %copy-start.2 = (s32[1,8]{1,0:T(1,128)S(1)}, s32[1,8]{1,0:T(1,128)}, u32[]{:S(2)}) copy-start(s32[1,8]{1,0:T(1,128)} %counts_ref.1) | copy-start | bytes 100
  1.6 6.9 %collective-permute-start.2 = (bf16[2,40,128]{2,1,0:T(8,128)(2,1)S(1)}, bf16[2,40,128]{2,1,0:T(8,128)(2,1)S(1)}, u32[]{:S(2)}, u32[]{:S(2)}) collective-permute-start(bf16[2,40,128]{2,1,0:T(8,128)(2,1)S(1)} %get-tuple-element.22), channel_id=1, source_target_pairs={{0,6},{1,7},{2,4},{3,5},{4,2},{5,3},{6,0},{7,1},{8,14},{9,15},{10,... | collective-permute-start | bytes 61448 | tf_op jit(solution)/shard_map/ppermute | solution.py:388
  6.8 4.7 %collective-permute-start.1 = (bf16[2,40,128]{2,1,0:T(8,128)(2,1)S(1)}, bf16[2,40,128]{2,1,0:T(8,128)(2,1)S(1)}, u32[]{:S(2)}, u32[]{:S(2)}) collective-permute-start(bf16[2,40,128]{2,1,0:T(8,128)(2,1)S(1)} %get-tuple-element.21), channel_id=1, source_target_pairs={{0,4},{1,5},{2,6},{3,7},{4,0},{5,1},{6,2},{7,3},{8,12},{9,13},{10,... | collective-permute-start | bytes 61448 | tf_op jit(solution)/shard_map/ppermute | solution.py:388
  6.8 4.7 %collective-permute-start = (bf16[2,40,128]{2,1,0:T(8,128)(2,1)S(1)}, bf16[2,40,128]{2,1,0:T(8,128)(2,1)S(1)}, u32[]{:S(2)}, u32[]{:S(2)}) collective-permute-start(bf16[2,40,128]{2,1,0:T(8,128)(2,1)S(1)} %get-tuple-element.20), channel_id=1, source_target_pairs={{0,2},{1,3},{2,0},{3,1},{4,6},{5,7},{6,4},{7,5},{8,10},{9,11},{10,... | collective-permute-start | bytes 61448 | tf_op jit(solution)/shard_map/ppermute | solution.py:388
  11.5 5.2 %collective-permute-start.3 = (bf16[2,4,40,128]{3,2,1,0:T(8,128)(2,1)S(1)}, bf16[2,4,40,128]{3,2,1,0:T(8,128)(2,1)S(1)}, u32[]{:S(2)}, u32[]{:S(2)}) collective-permute-start(bf16[2,4,40,128]{3,2,1,0:T(8,128)(2,1)S(1)} %pad_maximum_fusion.refs_0_), channel_id=1, source_target_pairs={{0,8},{8,0},{16,24},{24,16},{1,9},{9,1},{17,25},{25,17},{2,10},{10... | collective-permute-start | bytes 245768 | tf_op jit(solution)/shard_map/ppermute | solution.py:388
  13.1 4.9 %collective-permute-start.4 = (bf16[2,4,40,128]{3,2,1,0:T(8,128)(2,1)S(1)}, bf16[2,4,40,128]{3,2,1,0:T(8,128)(2,1)S(1)}, u32[]{:S(2)}, u32[]{:S(2)}) collective-permute-start(bf16[2,4,40,128]{3,2,1,0:T(8,128)(2,1)S(1)} %pad_maximum_fusion.refs_0_), channel_id=1, source_target_pairs={{0,16},{8,24},{16,0},{24,8},{1,17},{9,25},{17,1},{25,9},{2,18},{10... | collective-permute-start | bytes 245768 | tf_op jit(solution)/shard_map/ppermute | solution.py:388
  14.6 5.3 %collective-permute-start.5 = (bf16[2,4,40,128]{3,2,1,0:T(8,128)(2,1)S(1)}, bf16[2,4,40,128]{3,2,1,0:T(8,128)(2,1)S(1)}, u32[]{:S(2)}, u32[]{:S(2)}) collective-permute-start(bf16[2,4,40,128]{3,2,1,0:T(8,128)(2,1)S(1)} %pad_maximum_fusion.refs_0_), channel_id=1, source_target_pairs={{0,24},{8,16},{16,8},{24,0},{1,25},{9,17},{17,9},{25,1},{2,26},{10... | collective-permute-start | bytes 245768 | tf_op jit(solution)/shard_map/ppermute | solution.py:388
  15.1 5.9 %collective-permute-start.6 = (bf16[2,4,40,128]{3,2,1,0:T(8,128)(2,1)S(1)}, bf16[2,4,40,128]{3,2,1,0:T(8,128)(2,1)S(1)}, u32[]{:S(2)}, u32[]{:S(2)}) collective-permute-start(bf16[2,4,40,128]{3,2,1,0:T(8,128)(2,1)S(1)} %pad_maximum_fusion.refs_0_), channel_id=1, source_target_pairs={{0,1},{1,0},{2,3},{3,2},{4,5},{5,4},{6,7},{7,6},{8,9},{9,8},{10,11... | collective-permute-start | bytes 245768 | tf_op jit(solution)/shard_map/ppermute | solution.py:388
  16.7 4.3 %collective-permute-start.7 = (bf16[2,4,40,128]{3,2,1,0:T(8,128)(2,1)S(1)}, bf16[2,4,40,128]{3,2,1,0:T(8,128)(2,1)S(1)}, u32[]{:S(2)}, u32[]{:S(2)}) collective-permute-start(bf16[2,4,40,128]{3,2,1,0:T(8,128)(2,1)S(1)} %collective-permute-done.3.refs_1_), channel_id=1, source_target_pairs={{0,1},{1,0},{2,3},{3,2},{4,5},{5,4},{6,7},{7,6},{8,9},{9,8},{10,11... | collective-permute-start | bytes 245768 | tf_op jit(solution)/shard_map/ppermute | solution.py:388
  17.9 3.0 %collective-permute-start.8 = (bf16[2,4,40,128]{3,2,1,0:T(8,128)(2,1)S(1)}, bf16[2,4,40,128]{3,2,1,0:T(8,128)(2,1)S(1)}, u32[]{:S(2)}, u32[]{:S(2)}) collective-permute-start(bf16[2,4,40,128]{3,2,1,0:T(8,128)(2,1)S(1)} %collective-permute-done.4.refs_2_), channel_id=1, source_target_pairs={{0,1},{1,0},{2,3},{3,2},{4,5},{5,4},{6,7},{7,6},{8,9},{9,8},{10,11... | collective-permute-start | bytes 245768 | tf_op jit(solution)/shard_map/ppermute | solution.py:388
  19.9 1.3 %collective-permute-start.9 = (bf16[2,4,40,128]{3,2,1,0:T(8,128)(2,1)S(1)}, bf16[2,4,40,128]{3,2,1,0:T(8,128)(2,1)S(1)}, u32[]{:S(2)}, u32[]{:S(2)}) collective-permute-start(bf16[2,4,40,128]{3,2,1,0:T(8,128)(2,1)S(1)} %collective-permute-done.5.refs_3_), channel_id=1, source_target_pairs={{0,1},{1,0},{2,3},{3,2},{4,5},{5,4},{6,7},{7,6},{8,9},{9,8},{10,11... | collective-permute-start | bytes 245768 | tf_op jit(solution)/shard_map/ppermute | solution.py:388
  21.5 8.4 %collective-permute-start.10 = (bf16[2,32,128]{2,1,0:T(8,128)(2,1)S(1)}, bf16[2,32,128]{2,1,0:T(8,128)(2,1)S(1)}, u32[]{:S(2)}, u32[]{:S(2)}) collective-permute-start(bf16[2,32,128]{2,1,0:T(8,128)(2,1)S(1)} %get-tuple-element.33), channel_id=1, source_target_pairs={{0,2},{1,3},{2,0},{3,1},{4,6},{5,7},{6,4},{7,5},{8,10},{9,11},{10,... | collective-permute-start | bytes 49160 | tf_op jit(solution)/shard_map/ppermute | solution.py:388
  21.6 8.3 %collective-permute-start.11 = (bf16[2,32,128]{2,1,0:T(8,128)(2,1)S(1)}, bf16[2,32,128]{2,1,0:T(8,128)(2,1)S(1)}, u32[]{:S(2)}, u32[]{:S(2)}) collective-permute-start(bf16[2,32,128]{2,1,0:T(8,128)(2,1)S(1)} %get-tuple-element.34), channel_id=1, source_target_pairs={{0,4},{1,5},{2,6},{3,7},{4,0},{5,1},{6,2},{7,3},{8,12},{9,13},{10,... | collective-permute-start | bytes 49160 | tf_op jit(solution)/shard_map/ppermute | solution.py:388
  23.7 6.2 %collective-permute-start.12 = (bf16[2,32,128]{2,1,0:T(8,128)(2,1)S(1)}, bf16[2,32,128]{2,1,0:T(8,128)(2,1)S(1)}, u32[]{:S(2)}, u32[]{:S(2)}) collective-permute-start(bf16[2,32,128]{2,1,0:T(8,128)(2,1)S(1)} %get-tuple-element.35), channel_id=1, source_target_pairs={{0,6},{1,7},{2,4},{3,5},{4,2},{5,3},{6,0},{7,1},{8,14},{9,15},{10,... | collective-permute-start | bytes 49160 | tf_op jit(solution)/shard_map/ppermute | solution.py:388

commit v7 on v6

--- a/solution.py
+++ b/solution.py
@@ -186,52 +186,62 @@
     )(lists)
 
 
+def partial_answer(refs, bucket, column_ref):
+    views = [ref.at[bucket] for ref in refs]
+    return matching_sums(column_ref[bucket], keys_of(views), entries_of(views))
+
+
 def begin_answer_kernel(*refs):
     *in_refs, column_ref, sums_ref, count_ref = refs
     for bucket in range(2):
-        views = [ref.at[bucket] for ref in in_refs]
-        column = asked_column(views[:1])
-        sums, count = matching_sums(column, keys_of(views), entries_of(views))
-        column_ref[bucket] = column
-        sums_ref[bucket] = sums
-        count_ref[bucket] = count
+        column_ref[bucket] = asked_column([in_refs[0].at[bucket]])
+        sums_ref[bucket], count_ref[bucket] = partial_answer(in_refs, bucket, column_ref)
+
+
+def more_answer_kernel(*refs):
+    *in_refs, column_ref, sums_ref, count_ref, new_sums_ref, new_count_ref = refs
+    for bucket in range(2):
+        sums, number = partial_answer(in_refs, bucket, column_ref)
+        new_sums_ref[bucket] = sums_ref[bucket] + sums
+        new_count_ref[bucket] = count_ref[bucket] + number
 
 
 def finish_answer_kernel(count, *refs):
     in_refs, (column_ref, sums_ref, count_ref), out_refs = refs[:count], refs[count : count + 3], refs[count + 3 :]
     for bucket in range(2):
-        views = [ref.at[bucket] for ref in in_refs]
-        sums, number = matching_sums(column_ref[bucket], keys_of(views), entries_of(views))
+        sums, number = partial_answer(in_refs, bucket, column_ref)
         mean = (sums_ref[bucket] + sums) / jnp.maximum(count_ref[bucket] + number, 1.0)
         mean = mean.astype(jnp.bfloat16).reshape(len(out_refs), *out_refs[0].shape[1:])
         for k, out_ref in enumerate(out_refs):
             out_ref[bucket] = mean[k]
 
 
+def run_answer(kernel, out_shape, operands):
+    return pl.pallas_call(
+        kernel,
+        out_shape=out_shape,
+        in_specs=[vmem_spec()] * len(operands),
+        out_specs=[vmem_spec()] * len(out_shape),
+        compiler_params=grant(8 * MIB),
+    )(*operands)
+
+
 def begin_answer(parts):
     pairs, rows, lanes = parts[0].shape[1:]
     partial = jax.ShapeDtypeStruct((2, pairs * (rows - META), lanes), jnp.float32)
-    return pl.pallas_call(
-        begin_answer_kernel,
-        out_shape=[partial] * 3,
-        in_specs=[vmem_spec()] * len(parts),
-        out_specs=[vmem_spec()] * 3,
-        compiler_params=grant(8 * MIB),
-        name="begin_answer",
-    )(*parts)
+    return run_answer(begin_answer_kernel, [partial] * 3, parts)
+
+
+def more_answer(parts, begun):
+    partial = jax.ShapeDtypeStruct(begun[0].shape, jnp.float32)
+    return [begun[0], *run_answer(more_answer_kernel, [partial] * 2, [*parts, *begun])]
 
 
 def finish_answer(parts, begun):
     pairs, rows, lanes = parts[0].shape[1:]
     shape = jax.ShapeDtypeStruct((2, rows - META, lanes), jnp.bfloat16)
-    return pl.pallas_call(
-        functools.partial(finish_answer_kernel, len(parts)),
-        out_shape=[shape] * pairs,
-        in_specs=[vmem_spec()] * (len(parts) + 3),
-        out_specs=[vmem_spec()] * pairs,
-        compiler_params=grant(8 * MIB),
-        name="finish_answer",
-    )(*parts, *begun)
+    kernel = functools.partial(finish_answer_kernel, len(parts))
+    return run_answer(kernel, [shape] * pairs, [*parts, *begun])
 
 
 def place_kernel(*refs):
@@ -299,9 +309,7 @@
     return [ref.at[lax.rem(lax.axis_index("mem"), 2)] for ref in refs]
 
 
-def dense_prepare_kernel(*refs):
-    *in_refs, same_ref, tile_ref, number_ref = refs
-    views = own_bucket(in_refs)
+def prepare_tiles(views, same_ref, tile_ref, number_ref):
     capacity, lanes = views[0].shape[1] - META, views[0].shape[2]
     entries = same_ref.shape[1]
     ratio = TILE // DIGIT
@@ -319,6 +327,11 @@
     number_ref[...] = jnp.dot(same_ref[...], in_tile, preferred_element_type=jnp.float32)
 
 
+def dense_prepare_kernel(*refs):
+    *in_refs, same_ref, tile_ref, number_ref = refs
+    prepare_tiles(own_bucket(in_refs), same_ref, tile_ref, number_ref)
+
+
 def dense_prepare(parts):
     pairs, rows, lanes = parts[0].shape[1:]
     entries = len(parts) * pairs * (rows - META)
@@ -336,24 +349,53 @@
     )(*parts)
 
 
-def dense_tiles_kernel(count, *refs):
-    in_refs, prepared = refs[:count], refs[count : count + 6]
-    out_ref, mean_ref, inverse_ref, sems = refs[count + 6 :]
+def pair_sums(pair, views, same_refs, tile_refs):
+    values = entries_of(views)
+    tile_of = jnp.concatenate([ref[...] for ref in tile_refs], axis=0)
+    same = jnp.concatenate([ref[...] for ref in same_refs], axis=1)
+    zero = jnp.zeros_like(values)
+    picked = jnp.concatenate([jnp.where(tile_of == 2 * pair + k, values, zero) for k in range(2)], axis=1)
+    return jnp.dot(same, picked, preferred_element_type=jnp.float32)
+
+
+def begin_tiles_kernel(*refs):
+    *in_refs, same_ref, tile_ref, out_ref = refs
     views = own_bucket(in_refs)
+    lanes = out_ref.shape[1]
+    for pair in range(BUCKET // (2 * TILE)):
+        sums = pair_sums(pair, views, [same_ref], [tile_ref])
+        for k in range(2):
+            out_ref[pl.ds((2 * pair + k) * TILE, TILE), :] = sums[:, k * lanes : (k + 1) * lanes]
+
+
+def begin_tiles(parts, prepared):
+    lanes = parts[0].shape[3]
+    return pl.pallas_call(
+        begin_tiles_kernel,
+        out_shape=jax.ShapeDtypeStruct((BUCKET, lanes), jnp.float32),
+        in_specs=[vmem_spec()] * (len(parts) + 2),
+        out_specs=vmem_spec(),
+        compiler_params=grant(8 * MIB),
+        name="begin_tiles",
+    )(*parts, *prepared[:2])
+
+
+def finish_tiles_kernel(count, *refs):
+    same_parts, other_parts = refs[:count], refs[count : 2 * count]
+    begun_ref, number_ref, *middle = refs[2 * count : 2 * count + 5]
+    out_ref, mean_ref, inverse_ref, same_ref, tile_ref, last_ref, sems = refs[2 * count + 5 :]
+    prepare_tiles(own_bucket(other_parts), same_ref, tile_ref, last_ref)
+    views = own_bucket(same_parts + other_parts)
     lanes = views[0].shape[2]
-    inverse_ref[...] = 1.0 / jnp.maximum(prepared[2][...] + prepared[5][...], 1.0)
+    inverse_ref[...] = 1.0 / jnp.maximum(number_ref[...] + middle[2][...] + last_ref[...], 1.0)
     copies = []
     for pair in range(sems.shape[0]):
-        values = entries_of(views)
-        tile_of = jnp.concatenate([prepared[1][...], prepared[4][...]], axis=0)
-        same = jnp.concatenate([prepared[0][...], prepared[3][...]], axis=1)
-        zero = jnp.zeros_like(values)
-        picked = jnp.concatenate([jnp.where(tile_of == 2 * pair + k, values, zero) for k in range(2)], axis=1)
-        sums = jnp.dot(same, picked, preferred_element_type=jnp.float32)
+        sums = pair_sums(pair, views, [middle[0], same_ref], [middle[1], tile_ref])
         for k in range(2):
             tile = 2 * pair + k
             where = pl.ds(tile * TILE, TILE)
-            mean_ref[where, :] = sums[:, k * lanes : (k + 1) * lanes] * inverse_ref[:, tile : tile + 1]
+            total = begun_ref[where, :] + sums[:, k * lanes : (k + 1) * lanes]
+            mean_ref[where, :] = total * inverse_ref[:, tile : tile + 1]
             copy = pltpu.make_async_copy(mean_ref.at[where], out_ref.at[where], sems.at[pair, k])
             copy.start()
             copies.append(copy)
@@ -361,23 +403,26 @@
         copy.wait()
 
 
-def dense_tiles(parts, prepared):
-    pairs, rows, lanes = parts[0].shape[1:]
-    entries = len(parts) * pairs * (rows - META)
-    return pl.pallas_call(
-        functools.partial(dense_tiles_kernel, len(parts)),
+def finish_tiles(same_parts, other_parts, begun, number, middle):
+    pairs, rows, lanes = other_parts[0].shape[1:]
+    entries = len(other_parts) * pairs * (rows - META)
+    return pl.pallas_call(
+        functools.partial(finish_tiles_kernel, len(other_parts)),
         out_shape=jax.ShapeDtypeStruct((BUCKET, lanes), jnp.float32),
-        in_specs=[vmem_spec()] * (len(parts) + len(prepared)),
+        in_specs=[vmem_spec()] * (2 * len(other_parts) + 5),
         out_specs=hbm_spec(),
         scratch_shapes=[
             pltpu.VMEM((BUCKET, lanes), jnp.float32),
             pltpu.VMEM((TILE, lanes), jnp.float32),
+            pltpu.VMEM((TILE, entries), jnp.bfloat16),
+            pltpu.VMEM((entries, lanes), jnp.bfloat16),
+            pltpu.VMEM((TILE, lanes), jnp.float32),
             pltpu.SemaphoreType.DMA((BUCKET // (2 * TILE), 2)),
         ],
-        cost_estimate=dense_cost(entries, lanes),
+        cost_estimate=dense_cost(entries, lanes, 2.0),
         compiler_params=grant(16 * MIB),
-        name="dense_tiles",
-    )(*parts, *prepared)
+        name="finish_tiles",
+    )(*same_parts, *other_parts, begun, number, *middle)
 
 
 def by_pairs(values, slots, counts, groups):
@@ -392,11 +437,14 @@
     mine = jnp.stack(mine, axis=1)
     same = [mine] + [swap(mine, "grp", groups, k) for k in range(1, groups)]
     other = [swap(part, "mem", members, 1) for part in same]
-    begun = begin_answer(same)
-    prepared = dense_prepare(same)
-    answers = finish_answer(other, begun)
-    prepared += dense_prepare(other)
-    averaged = dense_tiles(same + other, prepared)
+    first = [same[0], other[0]]
+    begun = begin_answer(first)
+    early = dense_prepare(first)
+    sums = begin_tiles(first, early)
+    begun = more_answer(same[1:], begun)
+    prepared = dense_prepare(same[1:])
+    answers = finish_answer(other[1:], begun)
+    averaged = finish_tiles(same[1:], other[1:], sums, early[2], prepared)
     back = [answers[0]] + [swap(answers[k], "mem", members, 2 * k) for k in range(1, pairs)]
     return averaged, place(back)
 
@@ -413,7 +461,7 @@
 def per_device(groups, values, slots, counts):
     members, capacity, lanes = values.shape[1:]
     entries = groups * members * capacity
-    few = members in (2, 4, 8) and groups in (1, 2, 4, 8) and entries <= 2048
+    few = members == 8 and groups in (2, 4, 8) and entries <= 2048 and 4 * capacity == lanes
     tiles = BUCKET % (2 * TILE) == 0 and BUCKET // TILE <= lanes
     move = by_pairs if few and tiles else by_all
     averaged, returned = move(values[0], slots[0], counts, groups)

time: 30.7 us -> 31.5 us (1.026)
  Pallas kernels: 6.05 us -> 6.47 us
  waiting for transfers between devices: 9.12 us -> 9.49 us
    pallas_call x3 -> x5, Pallas kernels: 4.3 us -> 4.83 us  [the longest x1 3.15 us: finish_tiles(): pl.pallas_call(functools.partial(finish_tiles_kernel, len(other_parts)),...]
    ppermute x13, waiting for transfers between devices: 9.12 us -> 9.49 us  [swap(): return lax.ppermute(array, axis, [(i, i ^ by) for i in range(size)])]
  transfers between devices with their start and end apart: 13 -> 13, of which waited for: 6 -> 5; matrix products, arithmetic and copies ran while one was open for 0% -> 0% of each run, Pallas kernels for 16% -> 17%
where the time goes in v7:
time: 31.5 us; the launch traced here: 31.3 us
  starting transfers between devices  13.7 us (43%)
  waiting for transfers between devices  9.49 us (30%)
  Pallas kernels  6.47 us (21%)
  local copies, waits for them, and re-layouts  0.84 us (3%)
  between operations  0.77 us (2%)
    ppermute x13, starting transfers between devices, swap(): return lax.ppermute(array, axis, [(i, i ^ by) for i in range(size)])  13.7 us
    ppermute x13, waiting for transfers between devices, swap(): return lax.ppermute(array, axis, [(i, i ^ by) for i in range(size)])  9.49 us
    pallas_call x1, Pallas kernels, finish_tiles(): pl.pallas_call(functools.partial(finish_tiles_kernel, len(other_parts)),...  3.15 us
    pallas_call x3, Pallas kernels, run_answer(): pl.pallas_call(kernel, out_shape=out_shape, in_specs=[vmem_spec()] * len(...  1.02 us
    unnamed x6, local copies, waits for them, and re-layouts  0.84 us
    pallas_call x2, Pallas kernels, dense_prepare(): pl.pallas_call(dense_prepare_kernel, out_shape=[jax.ShapeDtypeStruct((TIL...  0.8 us
    pallas_call x1, Pallas kernels, begin_tiles(): pl.pallas_call(begin_tiles_kernel, out_shape=jax.ShapeDtypeStruct((BUCKET...  0.67 us
    pallas_call x1, Pallas kernels, place(): pl.pallas_call(place_kernel, out_shape=jax.ShapeDtypeStruct((two * len(pa...  0.67 us
  transfers between devices with their start and end apart: 13, of which 5 were waited for; matrix products, arithmetic and copies ran while one was open for 0% of the time, Pallas kernels for 17%

profile of v7, /device:TPU:0, one launch (start us, length us, event | category | flops | bytes accessed | tf_op | source)
XLA Modules:
  0.0 31.3 jit_solution(10385136594976259091)
XLA Ops:
  0.7 0.6 %copy-done.2 = s32[1,8]{1,0:T(1,128)S(1)} copy-done((s32[1,8]{1,0:T(1,128)S(1)}, s32[1,8]{1,0:T(1,128)}, u32[]{:S(2)}) %copy-start.2) | copy-done | bytes 56
  1.3 0.0 copy-done.1
  1.3 0.2 copy-done
  1.5 0.2 pack.1
  1.7 3.1 %collective-permute-start = (bf16[2,40,128]{2,1,0:T(8,128)(2,1)S(1)}, bf16[2,40,128]{2,1,0:T(8,128)(2,1)S(1)}, u32[]{:S(2)}, u32[]{:S(2)}) collective-permute-start(bf16[2,40,128]{2,1,0:T(8,128)(2,1)S(1)} %get-tuple-element.22), channel_id=1, source_target_pairs={{0,2},{1,3},{2,0},{3,1},{4,6},{5,7},{6,4},{7,5},{8,10},{9,11},{10,... | collective-permute-start | bytes 61448 | tf_op jit(solution)/shard_map/ppermute | solution.py:433
  4.8 2.6 %collective-permute-start.1 = (bf16[2,40,128]{2,1,0:T(8,128)(2,1)S(1)}, bf16[2,40,128]{2,1,0:T(8,128)(2,1)S(1)}, u32[]{:S(2)}, u32[]{:S(2)}) collective-permute-start(bf16[2,40,128]{2,1,0:T(8,128)(2,1)S(1)} %get-tuple-element.23), channel_id=1, source_target_pairs={{0,4},{1,5},{2,6},{3,7},{4,0},{5,1},{6,2},{7,3},{8,12},{9,13},{10,... | collective-permute-start | bytes 61448 | tf_op jit(solution)/shard_map/ppermute | solution.py:433
  7.4 0.0 collective-permute-start.2
  7.4 0.0 collective-permute-done
  7.4 2.3 %collective-permute-done.1 = bf16[2,40,128]{2,1,0:T(8,128)(2,1)S(1)} collective-permute-done((bf16[2,40,128]{2,1,0:T(8,128)(2,1)S(1)}, bf16[2,40,128]{2,1,0:T(8,128)(2,1)S(1)}, u32[]{:S(2)}, u32[]{:S(2)}) %collective-permute-start.1) | collective-permute-done | bytes 20512 | tf_op jit(solution)/shard_map/ppermute | solution.py:433
  9.7 3.3 %collective-permute-done.2 = bf16[2,40,128]{2,1,0:T(8,128)(2,1)S(1)} collective-permute-done((bf16[2,40,128]{2,1,0:T(8,128)(2,1)S(1)}, bf16[2,40,128]{2,1,0:T(8,128)(2,1)S(1)}, u32[]{:S(2)}, u32[]{:S(2)}) %collective-permute-start.2) | collective-permute-done | bytes 20512 | tf_op jit(solution)/shard_map/ppermute | solution.py:433
  13.0 2.5 %collective-permute-start.5 = (bf16[2,4,40,128]{3,2,1,0:T(8,128)(2,1)S(1)}, bf16[2,4,40,128]{3,2,1,0:T(8,128)(2,1)S(1)}, u32[]{:S(2)}, u32[]{:S(2)}) collective-permute-start(bf16[2,4,40,128]{3,2,1,0:T(8,128)(2,1)S(1)} %pad_maximum_fusion.refs_0_), channel_id=1, source_target_pairs={{0,24},{8,16},{16,8},{24,0},{1,25},{9,17},{17,9},{25,1},{2,26},{10... | collective-permute-start | bytes 245768 | tf_op jit(solution)/shard_map/ppermute | solution.py:433
  15.5 0.5 %collective-permute-start.4 = (bf16[2,4,40,128]{3,2,1,0:T(8,128)(2,1)S(1)}, bf16[2,4,40,128]{3,2,1,0:T(8,128)(2,1)S(1)}, u32[]{:S(2)}, u32[]{:S(2)}) collective-permute-start(bf16[2,4,40,128]{3,2,1,0:T(8,128)(2,1)S(1)} %pad_maximum_fusion.refs_0_), channel_id=1, source_target_pairs={{0,16},{8,24},{16,0},{24,8},{1,17},{9,25},{17,1},{25,9},{2,18},{10... | collective-permute-start | bytes 245768 | tf_op jit(solution)/shard_map/ppermute | solution.py:433
  16.0 0.5 %collective-permute-start.3 = (bf16[2,4,40,128]{3,2,1,0:T(8,128)(2,1)S(1)}, bf16[2,4,40,128]{3,2,1,0:T(8,128)(2,1)S(1)}, u32[]{:S(2)}, u32[]{:S(2)}) collective-permute-start(bf16[2,4,40,128]{3,2,1,0:T(8,128)(2,1)S(1)} %pad_maximum_fusion.refs_0_), channel_id=1, source_target_pairs={{0,8},{8,0},{16,24},{24,16},{1,9},{9,1},{17,25},{25,17},{2,10},{10... | collective-permute-start | bytes 245768 | tf_op jit(solution)/shard_map/ppermute | solution.py:433
  16.5 0.0 collective-permute-start.9
  16.5 2.3 %collective-permute-done.5.refs_2_ = bf16[2,4,40,128]{3,2,1,0:T(8,128)(2,1)S(1)} collective-permute-done((bf16[2,4,40,128]{3,2,1,0:T(8,128)(2,1)S(1)}, bf16[2,4,40,128]{3,2,1,0:T(8,128)(2,1)S(1)}, u32[]{:S(2)}, u32[]{:S(2)}) %collective-permute-start.5) | collective-permute-done | bytes 81952 | tf_op jit(solution)/shard_map/ppermute | solution.py:433
  18.9 0.0 collective-permute-start.8
  18.9 1.1 %collective-permute-done.4.refs_1_ = bf16[2,4,40,128]{3,2,1,0:T(8,128)(2,1)S(1)} collective-permute-done((bf16[2,4,40,128]{3,2,1,0:T(8,128)(2,1)S(1)}, bf16[2,4,40,128]{3,2,1,0:T(8,128)(2,1)S(1)}, u32[]{:S(2)}, u32[]{:S(2)}) %collective-permute-start.4) | collective-permute-done | bytes 81952 | tf_op jit(solution)/shard_map/ppermute | solution.py:433
  19.9 0.0 collective-permute-start.7
  19.9 0.5 %collective-permute-done.3.refs_0_ = bf16[2,4,40,128]{3,2,1,0:T(8,128)(2,1)S(1)} collective-permute-done((bf16[2,4,40,128]{3,2,1,0:T(8,128)(2,1)S(1)}, bf16[2,4,40,128]{3,2,1,0:T(8,128)(2,1)S(1)}, u32[]{:S(2)}, u32[]{:S(2)}) %collective-permute-start.3) | collective-permute-done | bytes 81952 | tf_op jit(solution)/shard_map/ppermute | solution.py:433
  20.4 0.0 collective-permute-start.6
  20.4 0.0 collective-permute-done.9.refs_1_
  20.5 0.5 %shard_map.50 = (f32[2,128,128]{2,1,0:T(8,128)S(1)}, f32[2,128,128]{2,1,0:T(8,128)S(1)}, f32[2,128,128]{2,1,0:T(8,128)S(1)}) custom-call(bf16[2,4,40,128]{3,2,1,0:T(8,128)(2,1)S(1)} %pad_maximum_fusion.refs_0_, bf16[2,4,40,128]{3,2,1,0:T(8,128)(2,1)S(1)} %collective-permute-done.9.refs_1_), custom_call_target="tpu_custom_call" | custom-call | tf_op jit(solution)/shard_map/pallas_call | solution.py:220
  20.9 0.4 %dense_prepare.2 = (bf16[512,256]{1,0:T(8,128)(2,1)S(1)}, bf16[256,128]{1,0:T(8,128)(2,1)S(1)}, f32[512,128]{1,0:T(8,128)S(1)}) custom-call(bf16[2,4,40,128]{3,2,1,0:T(8,128)(2,1)S(1)} %pad_maximum_fusion.refs_0_, bf16[2,4,40,128]{3,2,1,0:T(8,128)(2,1)S(1)} %collective-permute-done.9.refs_1_), custom_call_target="tpu_custom_call" | custom-call | tf_op jit(solution)/shard_map/dense_prepare/pallas_call | solution.py:338
  21.3 0.4 %dense_prepare.3 = (bf16[512,384]{1,0:T(8,128)(2,1)S(1)}, bf16[384,128]{1,0:T(8,128)(2,1)S(1)}, f32[512,128]{1,0:T(8,128)S(1)}) custom-call(bf16[2,4,40,128]{3,2,1,0:T(8,128)(2,1)S(1)} %collective-permute-done.3.refs_0_, bf16[2,4,40,128]{3,2,1,0:T(8,128)(2,1)S(1)} %collective-permute-done.4.refs_1_, bf16[2,4,40,128]{3,2,1,0:T(8,128)(2,1)S(1)} %collective-permute-done.5.refs_2_), custom_call_target="tpu_custom_call" | custom-call | tf_op jit(solution)/shard_map/dense_prepare/pallas_call | solution.py:338
  21.7 0.7 %begin_tiles.1.refs_6_ = f32[7168,128]{1,0:T(8,128)S(1)} custom-call(bf16[2,4,40,128]{3,2,1,0:T(8,128)(2,1)S(1)} %pad_maximum_fusion.refs_0_, bf16[2,4,40,128]{3,2,1,0:T(8,128)(2,1)S(1)} %collective-permute-done.9.refs_1_, bf16[512,256]{1,0:T(8,128)(2,1)S(1)} %get-tuple-element.25.refs_2_, bf16[256,128]{1,0:T(8,128)(2,1)S(1)} %get-tuple-element.26.refs_3_), custom_call_target="tpu_custom_call" | custom-call | tf_op jit(solution)/shard_map/begin_tiles/pallas_call | solution.py:373
  22.4 0.3 shard_map.51
  22.7 0.3 shard_map.52
  23.0 0.1 collective-permute-start.10
  23.1 0.9 %collective-permute-start.11 = (bf16[2,32,128]{2,1,0:T(8,128)(2,1)S(1)}, bf16[2,32,128]{2,1,0:T(8,128)(2,1)S(1)}, u32[]{:S(2)}, u32[]{:S(2)}) collective-permute-start(bf16[2,32,128]{2,1,0:T(8,128)(2,1)S(1)} %get-tuple-element.38), channel_id=1, source_target_pairs={{0,4},{1,5},{2,6},{3,7},{4,0},{5,1},{6,2},{7,3},{8,12},{9,13},{10,... | collective-permute-start | bytes 49160 | tf_op jit(solution)/shard_map/ppermute | solution.py:433
  23.9 3.5 %collective-permute-start.12 = (bf16[2,32,128]{2,1,0:T(8,128)(2,1)S(1)}, bf16[2,32,128]{2,1,0:T(8,128)(2,1)S(1)}, u32[]{:S(2)}, u32[]{:S(2)}) collective-permute-start(bf16[2,32,128]{2,1,0:T(8,128)(2,1)S(1)} %get-tuple-element.39), channel_id=1, source_target_pairs={{0,6},{1,7},{2,4},{3,5},{4,2},{5,3},{6,0},{7,1},{8,14},{9,15},{10,... | collective-permute-start | bytes 49160 | tf_op jit(solution)/shard_map/ppermute | solution.py:433
  27.4 3.1 %finish_tiles.1 = f32[7168,128]{1,0:T(8,128)} custom-call(bf16[2,4,40,128]{3,2,1,0:T(8,128)(2,1)S(1)} %collective-permute-done.3.refs_0_, bf16[2,4,40,128]{3,2,1,0:T(8,128)(2,1)S(1)} %collective-permute-done.4.refs_1_, bf16[2,4,40,128]{3,2,1,0:T(8,128)(2,1)S(1)} %collective-permute-done.5.refs_2_, ...), custom_call_target="tpu_custom_call" | custom-call | flops 1409286144 | bytes 7340032 | tf_op jit(solution)/shard_map/finish_tiles/pallas_call | solution.py:409
  30.6 0.7 %place.1 = bf16[8,32,128]{2,1,0:T(8,128)(2,1)} custom-call(bf16[2,32,128]{2,1,0:T(8,128)(2,1)S(1)} %get-tuple-element.36.refs_0_, bf16[2,32,128]{2,1,0:T(8,128)(2,1)S(1)} %collective-permute-done.10.refs_1_, bf16[2,32,128]{2,1,0:T(8,128)(2,1)S(1)} %collective-permute-done.11.refs_2_, bf16[2,32,128]{2,1,0:T(8,128)(2,1)S(1)} %collective-permute-done.12.refs_3_), custom_call_target="tpu_custom_call" | custom-call | tf_op jit(solution)/shard_map/place/pallas_call | solution.py:262
  (11 shorter events, 0.0 us)
Async XLA Ops:
  0.6 0.7 %copy-start.2 = (s32[1,8]{1,0:T(1,128)S(1)}, s32[1,8]{1,0:T(1,128)}, u32[]{:S(2)}) copy-start(s32[1,8]{1,0:T(1,128)} %counts_ref.1) | copy-start | bytes 100
  0.6 0.7 %copy-start.1 = (s32[1,8,32]{2,1,0:T(8,128)S(1)}, s32[1,8,32]{2,1,0:T(8,128)}, u32[]{:S(2)}) copy-start(s32[1,8,32]{2,1,0:T(8,128)} %param.4) | copy-start | bytes 3076
  0.6 0.9 %copy-start = (bf16[1,8,32,128]{3,2,1,0:T(8,128)(2,1)S(1)}, bf16[1,8,32,128]{3,2,1,0:T(8,128)(2,1)}, u32[]{:S(2)}) copy-start(bf16[1,8,32,128]{3,2,1,0:T(8,128)(2,1)} %param.3) | copy-start | bytes 196612
  1.7 5.7 %collective-permute-start = (bf16[2,40,128]{2,1,0:T(8,128)(2,1)S(1)}, bf16[2,40,128]{2,1,0:T(8,128)(2,1)S(1)}, u32[]{:S(2)}, u32[]{:S(2)}) collective-permute-start(bf16[2,40,128]{2,1,0:T(8,128)(2,1)S(1)} %get-tuple-element.22), channel_id=1, source_target_pairs={{0,2},{1,3},{2,0},{3,1},{4,6},{5,7},{6,4},{7,5},{8,10},{9,11},{10,... | collective-permute-start | bytes 61448 | tf_op jit(solution)/shard_map/ppermute | solution.py:433
  4.8 4.9 %collective-permute-start.1 = (bf16[2,40,128]{2,1,0:T(8,128)(2,1)S(1)}, bf16[2,40,128]{2,1,0:T(8,128)(2,1)S(1)}, u32[]{:S(2)}, u32[]{:S(2)}) collective-permute-start(bf16[2,40,128]{2,1,0:T(8,128)(2,1)S(1)} %get-tuple-element.23), channel_id=1, source_target_pairs={{0,4},{1,5},{2,6},{3,7},{4,0},{5,1},{6,2},{7,3},{8,12},{9,13},{10,... | collective-permute-start | bytes 61448 | tf_op jit(solution)/shard_map/ppermute | solution.py:433
  7.4 5.6 %collective-permute-start.2 = (bf16[2,40,128]{2,1,0:T(8,128)(2,1)S(1)}, bf16[2,40,128]{2,1,0:T(8,128)(2,1)S(1)}, u32[]{:S(2)}, u32[]{:S(2)}) collective-permute-start(bf16[2,40,128]{2,1,0:T(8,128)(2,1)S(1)} %get-tuple-element.24), channel_id=1, source_target_pairs={{0,6},{1,7},{2,4},{3,5},{4,2},{5,3},{6,0},{7,1},{8,14},{9,15},{10,... | collective-permute-start | bytes 61448 | tf_op jit(solution)/shard_map/ppermute | solution.py:433
  13.0 5.9 %collective-permute-start.5 = (bf16[2,4,40,128]{3,2,1,0:T(8,128)(2,1)S(1)}, bf16[2,4,40,128]{3,2,1,0:T(8,128)(2,1)S(1)}, u32[]{:S(2)}, u32[]{:S(2)}) collective-permute-start(bf16[2,4,40,128]{3,2,1,0:T(8,128)(2,1)S(1)} %pad_maximum_fusion.refs_0_), channel_id=1, source_target_pairs={{0,24},{8,16},{16,8},{24,0},{1,25},{9,17},{17,9},{25,1},{2,26},{10... | collective-permute-start | bytes 245768 | tf_op jit(solution)/shard_map/ppermute | solution.py:433
  15.5 4.4 %collective-permute-start.4 = (bf16[2,4,40,128]{3,2,1,0:T(8,128)(2,1)S(1)}, bf16[2,4,40,128]{3,2,1,0:T(8,128)(2,1)S(1)}, u32[]{:S(2)}, u32[]{:S(2)}) collective-permute-start(bf16[2,4,40,128]{3,2,1,0:T(8,128)(2,1)S(1)} %pad_maximum_fusion.refs_0_), channel_id=1, source_target_pairs={{0,16},{8,24},{16,0},{24,8},{1,17},{9,25},{17,1},{25,9},{2,18},{10... | collective-permute-start | bytes 245768 | tf_op jit(solution)/shard_map/ppermute | solution.py:433
  16.0 4.4 %collective-permute-start.3 = (bf16[2,4,40,128]{3,2,1,0:T(8,128)(2,1)S(1)}, bf16[2,4,40,128]{3,2,1,0:T(8,128)(2,1)S(1)}, u32[]{:S(2)}, u32[]{:S(2)}) collective-permute-start(bf16[2,4,40,128]{3,2,1,0:T(8,128)(2,1)S(1)} %pad_maximum_fusion.refs_0_), channel_id=1, source_target_pairs={{0,8},{8,0},{16,24},{24,16},{1,9},{9,1},{17,25},{25,17},{2,10},{10... | collective-permute-start | bytes 245768 | tf_op jit(solution)/shard_map/ppermute | solution.py:433
  16.5 3.9 %collective-permute-start.9 = (bf16[2,4,40,128]{3,2,1,0:T(8,128)(2,1)S(1)}, bf16[2,4,40,128]{3,2,1,0:T(8,128)(2,1)S(1)}, u32[]{:S(2)}, u32[]{:S(2)}) collective-permute-start(bf16[2,4,40,128]{3,2,1,0:T(8,128)(2,1)S(1)} %pad_maximum_fusion.refs_0_), channel_id=1, source_target_pairs={{0,1},{1,0},{2,3},{3,2},{4,5},{5,4},{6,7},{7,6},{8,9},{9,8},{10,11... | collective-permute-start | bytes 245768 | tf_op jit(solution)/shard_map/ppermute | solution.py:433
  18.9 3.8 %collective-permute-start.8 = (bf16[2,4,40,128]{3,2,1,0:T(8,128)(2,1)S(1)}, bf16[2,4,40,128]{3,2,1,0:T(8,128)(2,1)S(1)}, u32[]{:S(2)}, u32[]{:S(2)}) collective-permute-start(bf16[2,4,40,128]{3,2,1,0:T(8,128)(2,1)S(1)} %collective-permute-done.5.refs_2_), channel_id=1, source_target_pairs={{0,1},{1,0},{2,3},{3,2},{4,5},{5,4},{6,7},{7,6},{8,9},{9,8},{10,11... | collective-permute-start | bytes 245768 | tf_op jit(solution)/shard_map/ppermute | solution.py:433
  19.9 2.8 %collective-permute-start.7 = (bf16[2,4,40,128]{3,2,1,0:T(8,128)(2,1)S(1)}, bf16[2,4,40,128]{3,2,1,0:T(8,128)(2,1)S(1)}, u32[]{:S(2)}, u32[]{:S(2)}) collective-permute-start(bf16[2,4,40,128]{3,2,1,0:T(8,128)(2,1)S(1)} %collective-permute-done.4.refs_1_), channel_id=1, source_target_pairs={{0,1},{1,0},{2,3},{3,2},{4,5},{5,4},{6,7},{7,6},{8,9},{9,8},{10,11... | collective-permute-start | bytes 245768 | tf_op jit(solution)/shard_map/ppermute | solution.py:433
  20.4 2.3 %collective-permute-start.6 = (bf16[2,4,40,128]{3,2,1,0:T(8,128)(2,1)S(1)}, bf16[2,4,40,128]{3,2,1,0:T(8,128)(2,1)S(1)}, u32[]{:S(2)}, u32[]{:S(2)}) collective-permute-start(bf16[2,4,40,128]{3,2,1,0:T(8,128)(2,1)S(1)} %collective-permute-done.3.refs_0_), channel_id=1, source_target_pairs={{0,1},{1,0},{2,3},{3,2},{4,5},{5,4},{6,7},{7,6},{8,9},{9,8},{10,11... | collective-permute-start | bytes 245768 | tf_op jit(solution)/shard_map/ppermute | solution.py:433
  23.0 7.6 %collective-permute-start.10 = (bf16[2,32,128]{2,1,0:T(8,128)(2,1)S(1)}, bf16[2,32,128]{2,1,0:T(8,128)(2,1)S(1)}, u32[]{:S(2)}, u32[]{:S(2)}) collective-permute-start(bf16[2,32,128]{2,1,0:T(8,128)(2,1)S(1)} %get-tuple-element.37), channel_id=1, source_target_pairs={{0,2},{1,3},{2,0},{3,1},{4,6},{5,7},{6,4},{7,5},{8,10},{9,11},{10,... | collective-permute-start | bytes 49160 | tf_op jit(solution)/shard_map/ppermute | solution.py:433
  23.1 7.5 %collective-permute-start.11 = (bf16[2,32,128]{2,1,0:T(8,128)(2,1)S(1)}, bf16[2,32,128]{2,1,0:T(8,128)(2,1)S(1)}, u32[]{:S(2)}, u32[]{:S(2)}) collective-permute-start(bf16[2,32,128]{2,1,0:T(8,128)(2,1)S(1)} %get-tuple-element.38), channel_id=1, source_target_pairs={{0,4},{1,5},{2,6},{3,7},{4,0},{5,1},{6,2},{7,3},{8,12},{9,13},{10,... | collective-permute-start | bytes 49160 | tf_op jit(solution)/shard_map/ppermute | solution.py:433
  23.9 6.7 %collective-permute-start.12 = (bf16[2,32,128]{2,1,0:T(8,128)(2,1)S(1)}, bf16[2,32,128]{2,1,0:T(8,128)(2,1)S(1)}, u32[]{:S(2)}, u32[]{:S(2)}) collective-permute-start(bf16[2,32,128]{2,1,0:T(8,128)(2,1)S(1)} %get-tuple-element.39), channel_id=1, source_target_pairs={{0,6},{1,7},{2,4},{3,5},{4,2},{5,3},{6,0},{7,1},{8,14},{9,15},{10,... | collective-permute-start | bytes 49160 | tf_op jit(solution)/shard_map/ppermute | solution.py:433

commit v8 on v7

--- a/solution.py
+++ b/solution.py
@@ -28,15 +28,11 @@
     return pltpu.CompilerParams(vmem_limit_bytes=size)
 
 
-def lists_shape(count, capacity, lanes):
-    return jax.ShapeDtypeStruct((count, capacity + META, lanes), jnp.bfloat16)
-
-
 def place_in_list_kernel(out_ref):
     out_ref[...] = lax.broadcasted_iota(jnp.int32, out_ref.shape, 1).astype(jnp.float32)
 
 
-def meta_rows(slots_ref, counts_ref, place_ref, lanes):
+def meta_rows(slots_ref, counts_ref, place_ref, lanes, buckets):
     members, capacity = slots_ref.shape
     shape = (members, members)
     diagonal = lax.broadcasted_iota(jnp.int32, shape, 0) == lax.broadcasted_iota(jnp.int32, shape, 1)
@@ -49,12 +45,14 @@
     high = jnp.concatenate([high] * repeats, axis=1)
     low = jnp.concatenate([low] * repeats, axis=1)
     row = lax.broadcasted_iota(jnp.int32, (members, META, lanes), 1)
-    return jnp.where(row == 0, high[:, None, :], low[:, None, :]).astype(jnp.bfloat16)
+    row = row - 2 * lax.rem(lax.broadcasted_iota(jnp.int32, row.shape, 0), buckets)
+    meta = jnp.where(row == 0, high[:, None, :], jnp.where(row == 1, low[:, None, :], 0.0))
+    return meta.astype(jnp.bfloat16)
 
 
 def pack_groups_kernel(values_ref, slots_ref, counts_ref, place_ref, out_ref):
     members, capacity, lanes = values_ref.shape
-    meta = meta_rows(slots_ref, counts_ref, place_ref, lanes)
+    meta = meta_rows(slots_ref, counts_ref, place_ref, lanes, 1)
     for group in range(out_ref.shape[0] // members):
         rows = pl.ds(group * members, members)
         out_ref[rows, pl.ds(0, capacity), :] = values_ref[...]
@@ -64,12 +62,13 @@
 def pack_pairs_kernel(values_ref, slots_ref, counts_ref, place_ref, *out_and_scratch):
     *out_refs, meta_ref = out_and_scratch
     capacity, lanes = values_ref.shape[1:]
-    meta_ref[...] = meta_rows(slots_ref, counts_ref, place_ref, lanes)
+    meta_ref[...] = meta_rows(slots_ref, counts_ref, place_ref, lanes, 2)
     pair = lax.div(lax.axis_index("mem"), 2)
     for k, out_ref in enumerate(out_refs):
-        rows = pl.ds(2 * lax.bitwise_xor(pair, jnp.int32(k)), 2)
-        out_ref[:, pl.ds(0, capacity), :] = values_ref[rows]
-        out_ref[:, pl.ds(capacity, META), :] = meta_ref[rows]
+        first = 2 * lax.bitwise_xor(pair, jnp.int32(k))
+        for bucket in range(2):
+            out_ref[pl.ds(bucket * capacity, capacity), :] = values_ref[first + bucket]
+        out_ref[pl.ds(2 * capacity, META), :] = meta_ref[first] + meta_ref[first + 1]
 
 
 def pack(values, slots, counts, groups, paired):
@@ -83,10 +82,12 @@
         name="place_in_list",
     )()
     if paired:
-        kernel, out_shape = pack_pairs_kernel, [lists_shape(2, capacity, lanes)] * (members // 2)
+        shape = jax.ShapeDtypeStruct((2 * capacity + META, lanes), jnp.bfloat16)
+        kernel, out_shape = pack_pairs_kernel, [shape] * (members // 2)
         scratch = [pltpu.VMEM((members, META, lanes), jnp.bfloat16)]
     else:
-        kernel, out_shape = pack_groups_kernel, [lists_shape(groups * members, capacity, lanes)]
+        shape = jax.ShapeDtypeStruct((groups * members, capacity + META, lanes), jnp.bfloat16)
+        kernel, out_shape = pack_groups_kernel, [shape]
         scratch = []
     return pl.pallas_call(
         kernel,
@@ -99,15 +100,35 @@
     )(values, slots, counts, place_in_list)
 
 
-def digits_of(refs):
-    capacity = refs[0].shape[1] - META
-    meta = [ref[:, pl.ds(capacity, META), :].astype(jnp.float32) for ref in refs]
-    return jnp.concatenate([m[:, 0, :] for m in meta], axis=0), jnp.concatenate([m[:, 1, :] for m in meta], axis=0)
-
-
-def entries_of(refs):
-    capacity, lanes = refs[0].shape[1] - META, refs[0].shape[2]
-    return jnp.concatenate([ref[:, pl.ds(0, capacity), :].reshape(-1, lanes) for ref in refs], axis=0)
+def capacity_of(view):
+    ref, bucket = view
+    rows = ref.shape[1] - META
+    return rows if bucket is None else rows // 2
+
+
+def digits_of(views):
+    high, low = [], []
+    for ref, bucket in views:
+        meta = ref[:, pl.ds(ref.shape[1] - META, META), :].astype(jnp.float32)
+        if bucket is None or isinstance(bucket, int):
+            at = 2 * (bucket or 0)
+            high.append(meta[:, at, :])
+            low.append(meta[:, at + 1, :])
+        else:
+            high.append(jnp.where(bucket == 0, meta[:, 0, :], meta[:, 2, :]))
+            low.append(jnp.where(bucket == 0, meta[:, 1, :], meta[:, 3, :]))
+    return jnp.concatenate(high, axis=0), jnp.concatenate(low, axis=0)
+
+
+def entries_of(views):
+    capacity, lanes = capacity_of(views[0]), views[0][0].shape[2]
+
+    def rows(bucket):
+        if bucket is None or isinstance(bucket, int):
+            return pl.ds((bucket or 0) * capacity, capacity)
+        return pl.ds(pl.multiple_of(bucket * capacity, capacity), capacity)
+
+    return jnp.concatenate([ref[:, rows(bucket), :].reshape(-1, lanes) for ref, bucket in views], axis=0)
 
 
 def as_row(digit, capacity):
@@ -132,13 +153,13 @@
     return jnp.dot(picked, jnp.ones((lanes, lanes), jnp.bfloat16), preferred_element_type=jnp.float32)
 
 
-def keys_of(refs):
-    high, low = digits_of(refs)
-    return as_row(high * DIGIT + low, refs[0].shape[1] - META)
+def keys_of(views):
+    high, low = digits_of(views)
+    return as_row(high * DIGIT + low, capacity_of(views[0]))
 
 
 def asked_column(asking):
-    capacity = asking[0].shape[1] - META
+    capacity = capacity_of(asking[0])
     high, low = digits_of(asking)
     column = as_column(high, capacity) * DIGIT + as_column(low, capacity)
     return jnp.where(column < 0.0, -1.0, column)
@@ -160,13 +181,13 @@
 def answer_kernel(lists_ref, out_ref, key_ref):
     members = out_ref.shape[0]
     step = math.gcd(members, 8)
-    key_ref[...] = keys_of([lists_ref])
+    key_ref[...] = keys_of([(lists_ref, None)])
     first = lax.axis_index("grp") * members
 
     @pl.loop(0, members, step=step)
     def _(at):
-        asking = lists_ref.at[pl.ds(first + at, step)]
-        sums, count = matching_sums(asked_column([asking]), key_ref[...], entries_of([lists_ref]))
+        asking = (lists_ref.at[pl.ds(first + at, step)], None)
+        sums, count = matching_sums(asked_column([asking]), key_ref[...], entries_of([(lists_ref, None)]))
         mean = sums / jnp.maximum(count, 1.0)
         out_ref[pl.ds(at, step)] = mean.astype(jnp.bfloat16).reshape(step, *out_ref.shape[1:])
 
@@ -187,14 +208,14 @@
 
 
 def partial_answer(refs, bucket, column_ref):
-    views = [ref.at[bucket] for ref in refs]
+    views = [(ref, bucket) for ref in refs]
     return matching_sums(column_ref[bucket], keys_of(views), entries_of(views))
 
 
 def begin_answer_kernel(*refs):
     *in_refs, column_ref, sums_ref, count_ref = refs
     for bucket in range(2):
-        column_ref[bucket] = asked_column([in_refs[0].at[bucket]])
+        column_ref[bucket] = asked_column([(in_refs[0], bucket)])
         sums_ref[bucket], count_ref[bucket] = partial_answer(in_refs, bucket, column_ref)
 
 
@@ -227,8 +248,8 @@
 
 
 def begin_answer(parts):
-    pairs, rows, lanes = parts[0].shape[1:]
-    partial = jax.ShapeDtypeStruct((2, pairs * (rows - META), lanes), jnp.float32)
+    pairs, rows, lanes = parts[0].shape
+    partial = jax.ShapeDtypeStruct((2, pairs * (rows - META) // 2, lanes), jnp.float32)
     return run_answer(begin_answer_kernel, [partial] * 3, parts)
 
 
@@ -238,8 +259,8 @@
 
 
 def finish_answer(parts, begun):
-    pairs, rows, lanes = parts[0].shape[1:]
-    shape = jax.ShapeDtypeStruct((2, rows - META, lanes), jnp.bfloat16)
+    pairs, rows, lanes = parts[0].shape
+    shape = jax.ShapeDtypeStruct((2, (rows - META) // 2, lanes), jnp.bfloat16)
     kernel = functools.partial(finish_answer_kernel, len(parts))
     return run_answer(kernel, [shape] * pairs, [*parts, *begun])
 
@@ -278,12 +299,12 @@
 def dense_kernel(lists_ref, out_ref, key_ref):
     @pl.when(pl.program_id(0) == 0)
     def _():
-        key_ref[...] = keys_of([lists_ref])
+        key_ref[...] = keys_of([(lists_ref, None)])
 
     tile = out_ref.shape[0]
     wanted = (lax.broadcasted_iota(jnp.int32, (tile, 1), 0) + pl.program_id(0) * tile).astype(jnp.float32)
     onehot = (wanted == key_ref[...]).astype(jnp.float32).astype(jnp.bfloat16)
-    entries = entries_of([lists_ref])
+    entries = entries_of([(lists_ref, None)])
     sums = jnp.dot(onehot, entries, preferred_element_type=jnp.float32)
     count = jnp.dot(onehot, jnp.ones_like(entries), preferred_element_type=jnp.float32)
     out_ref[...] = sums / jnp.maximum(count, 1.0)
@@ -306,11 +327,12 @@
 
 
 def own_bucket(refs):
-    return [ref.at[lax.rem(lax.axis_index("mem"), 2)] for ref in refs]
+    bucket = lax.rem(lax.axis_index("mem"), 2)
+    return [(ref, bucket) for ref in refs]
 
 
 def prepare_tiles(views, same_ref, tile_ref, number_ref):
-    capacity, lanes = views[0].shape[1] - META, views[0].shape[2]
+    capacity, lanes = capacity_of(views[0]), tile_ref.shape[1]
     entries = same_ref.shape[1]
     ratio = TILE // DIGIT
     high, low = digits_of(views)
@@ -333,8 +355,8 @@
 
 
 def dense_prepare(parts):
-    pairs, rows, lanes = parts[0].shape[1:]
-    entries = len(parts) * pairs * (rows - META)
+    pairs, rows, lanes = parts[0].shape
+    entries = len(parts) * pairs * (rows - META) // 2
     return pl.pallas_call(
         dense_prepare_kernel,
         out_shape=[
@@ -369,7 +391,7 @@
 
 
 def begin_tiles(parts, prepared):
-    lanes = parts[0].shape[3]
+    lanes = parts[0].shape[2]
     return pl.pallas_call(
         begin_tiles_kernel,
         out_shape=jax.ShapeDtypeStruct((BUCKET, lanes), jnp.float32),
@@ -386,7 +408,7 @@
     out_ref, mean_ref, inverse_ref, same_ref, tile_ref, last_ref, sems = refs[2 * count + 5 :]
     prepare_tiles(own_bucket(other_parts), same_ref, tile_ref, last_ref)
     views = own_bucket(same_parts + other_parts)
-    lanes = views[0].shape[2]
+    lanes = mean_ref.shape[1]
     inverse_ref[...] = 1.0 / jnp.maximum(number_ref[...] + middle[2][...] + last_ref[...], 1.0)
     copies = []
     for pair in range(sems.shape[0]):
@@ -404,8 +426,8 @@
 
 
 def finish_tiles(same_parts, other_parts, begun, number, middle):
-    pairs, rows, lanes = other_parts[0].shape[1:]
-    entries = len(other_parts) * pairs * (rows - META)
+    pairs, rows, lanes = other_parts[0].shape
+    entries = len(other_parts) * pairs * (rows - META) // 2
     return pl.pallas_call(
         functools.partial(finish_tiles_kernel, len(other_parts)),
         out_shape=jax.ShapeDtypeStruct((BUCKET, lanes), jnp.float32),
@@ -434,7 +456,7 @@
 
     sent = pack(values, slots, counts, groups, True)
     mine = [sent[0]] + [swap(sent[k], "mem", members, 2 * k) for k in range(1, pairs)]
-    mine = jnp.stack(mine, axis=1)
+    mine = jnp.stack(mine, axis=0)
     same = [mine] + [swap(mine, "grp", groups, k) for k in range(1, groups)]
     other = [swap(part, "mem", members, 1) for part in same]
     first = [same[0], other[0]]

time: 31.5 us -> 31.5 us (level)
  no operation moved by 1% of the time
where the time goes in v8:
time: 31.5 us; the launch traced here: 31.3 us
  starting transfers between devices  13.7 us (43%)
  waiting for transfers between devices  9.38 us (30%)
  Pallas kernels  6.59 us (21%)
  local copies, waits for them, and re-layouts  0.84 us (3%)
  between operations  0.77 us (2%)
    ppermute x13, starting transfers between devices, swap(): return lax.ppermute(array, axis, [(i, i ^ by) for i in range(size)])  13.7 us
    ppermute x13, waiting for transfers between devices, swap(): return lax.ppermute(array, axis, [(i, i ^ by) for i in range(size)])  9.38 us
    pallas_call x1, Pallas kernels, finish_tiles(): pl.pallas_call(functools.partial(finish_tiles_kernel, len(other_parts)),...  3.26 us
    pallas_call x3, Pallas kernels, run_answer(): pl.pallas_call(kernel, out_shape=out_shape, in_specs=[vmem_spec()] * len(...  1.01 us
    unnamed x6, local copies, waits for them, and re-layouts  0.84 us
    pallas_call x2, Pallas kernels, dense_prepare(): pl.pallas_call(dense_prepare_kernel, out_shape=[jax.ShapeDtypeStruct((TIL...  0.8 us
    pallas_call x1, Pallas kernels, begin_tiles(): pl.pallas_call(begin_tiles_kernel, out_shape=jax.ShapeDtypeStruct((BUCKET...  0.67 us
    pallas_call x1, Pallas kernels, place(): pl.pallas_call(place_kernel, out_shape=jax.ShapeDtypeStruct((two * len(pa...  0.67 us
  transfers between devices with their start and end apart: 13, of which 5 were waited for; matrix products, arithmetic and copies ran while one was open for 0% of the time, Pallas kernels for 17%

profile of v8, /device:TPU:0, one launch (start us, length us, event | category | flops | bytes accessed | tf_op | source)
XLA Modules:
  0.0 31.3 jit_solution(592834810030797240)
XLA Ops:
  0.7 0.6 %copy-done.2 = s32[1,8]{1,0:T(1,128)S(1)} copy-done((s32[1,8]{1,0:T(1,128)S(1)}, s32[1,8]{1,0:T(1,128)}, u32[]{:S(2)}) %copy-start.2) | copy-done | bytes 56
  1.3 0.0 copy-done.1
  1.3 0.2 copy-done
  1.5 0.2 pack.1
  1.7 3.1 %collective-permute-start = (bf16[72,128]{1,0:T(8,128)(2,1)S(1)}, bf16[72,128]{1,0:T(8,128)(2,1)S(1)}, u32[]{:S(2)}, u32[]{:S(2)}) collective-permute-start(bf16[72,128]{1,0:T(8,128)(2,1)S(1)} %get-tuple-element.22), channel_id=1, source_target_pairs={{0,2},{1,3},{2,0},{3,1},{4,6},{5,7},{6,4},{7,5},{8,10},{9,11},{10,... | collective-permute-start | bytes 55304 | tf_op jit(solution)/shard_map/ppermute | solution.py:455
  4.8 2.6 %collective-permute-start.1 = (bf16[72,128]{1,0:T(8,128)(2,1)S(1)}, bf16[72,128]{1,0:T(8,128)(2,1)S(1)}, u32[]{:S(2)}, u32[]{:S(2)}) collective-permute-start(bf16[72,128]{1,0:T(8,128)(2,1)S(1)} %get-tuple-element.23), channel_id=1, source_target_pairs={{0,4},{1,5},{2,6},{3,7},{4,0},{5,1},{6,2},{7,3},{8,12},{9,13},{10,... | collective-permute-start | bytes 55304 | tf_op jit(solution)/shard_map/ppermute | solution.py:455
  7.4 2.2 %collective-permute-done.1 = bf16[72,128]{1,0:T(8,128)(2,1)S(1)} collective-permute-done((bf16[72,128]{1,0:T(8,128)(2,1)S(1)}, bf16[72,128]{1,0:T(8,128)(2,1)S(1)}, u32[]{:S(2)}, u32[]{:S(2)}) %collective-permute-start.1) | collective-permute-done | bytes 18464 | tf_op jit(solution)/shard_map/ppermute | solution.py:455
  9.6 3.3 %collective-permute-done.2 = bf16[72,128]{1,0:T(8,128)(2,1)S(1)} collective-permute-done((bf16[72,128]{1,0:T(8,128)(2,1)S(1)}, bf16[72,128]{1,0:T(8,128)(2,1)S(1)}, u32[]{:S(2)}, u32[]{:S(2)}) %collective-permute-start.2) | collective-permute-done | bytes 18464 | tf_op jit(solution)/shard_map/ppermute | solution.py:455
  13.0 2.5 %collective-permute-start.5 = (bf16[4,72,128]{2,1,0:T(8,128)(2,1)S(1)}, bf16[4,72,128]{2,1,0:T(8,128)(2,1)S(1)}, u32[]{:S(2)}, u32[]{:S(2)}) collective-permute-start(bf16[4,72,128]{2,1,0:T(8,128)(2,1)S(1)} %pad_maximum_fusion.refs_0_), channel_id=1, source_target_pairs={{0,24},{8,16},{16,8},{24,0},{1,25},{9,17},{17,9},{25,1},{2,26},{10... | collective-permute-start | bytes 221192 | tf_op jit(solution)/shard_map/ppermute | solution.py:455
  15.5 0.5 %collective-permute-start.4 = (bf16[4,72,128]{2,1,0:T(8,128)(2,1)S(1)}, bf16[4,72,128]{2,1,0:T(8,128)(2,1)S(1)}, u32[]{:S(2)}, u32[]{:S(2)}) collective-permute-start(bf16[4,72,128]{2,1,0:T(8,128)(2,1)S(1)} %pad_maximum_fusion.refs_0_), channel_id=1, source_target_pairs={{0,16},{8,24},{16,0},{24,8},{1,17},{9,25},{17,1},{25,9},{2,18},{10... | collective-permute-start | bytes 221192 | tf_op jit(solution)/shard_map/ppermute | solution.py:455
  16.0 0.5 %collective-permute-start.3 = (bf16[4,72,128]{2,1,0:T(8,128)(2,1)S(1)}, bf16[4,72,128]{2,1,0:T(8,128)(2,1)S(1)}, u32[]{:S(2)}, u32[]{:S(2)}) collective-permute-start(bf16[4,72,128]{2,1,0:T(8,128)(2,1)S(1)} %pad_maximum_fusion.refs_0_), channel_id=1, source_target_pairs={{0,8},{8,0},{16,24},{24,16},{1,9},{9,1},{17,25},{25,17},{2,10},{10... | collective-permute-start | bytes 221192 | tf_op jit(solution)/shard_map/ppermute | solution.py:455
  16.5 0.0 collective-permute-start.9
  16.5 2.2 %collective-permute-done.5.refs_2_ = bf16[4,72,128]{2,1,0:T(8,128)(2,1)S(1)} collective-permute-done((bf16[4,72,128]{2,1,0:T(8,128)(2,1)S(1)}, bf16[4,72,128]{2,1,0:T(8,128)(2,1)S(1)}, u32[]{:S(2)}, u32[]{:S(2)}) %collective-permute-start.5) | collective-permute-done | bytes 73760 | tf_op jit(solution)/shard_map/ppermute | solution.py:455
  18.7 1.1 %collective-permute-done.4.refs_1_ = bf16[4,72,128]{2,1,0:T(8,128)(2,1)S(1)} collective-permute-done((bf16[4,72,128]{2,1,0:T(8,128)(2,1)S(1)}, bf16[4,72,128]{2,1,0:T(8,128)(2,1)S(1)}, u32[]{:S(2)}, u32[]{:S(2)}) %collective-permute-start.4) | collective-permute-done | bytes 73760 | tf_op jit(solution)/shard_map/ppermute | solution.py:455
  19.8 0.0 collective-permute-start.7
  19.8 0.5 %collective-permute-done.3.refs_0_ = bf16[4,72,128]{2,1,0:T(8,128)(2,1)S(1)} collective-permute-done((bf16[4,72,128]{2,1,0:T(8,128)(2,1)S(1)}, bf16[4,72,128]{2,1,0:T(8,128)(2,1)S(1)}, u32[]{:S(2)}, u32[]{:S(2)}) %collective-permute-start.3) | collective-permute-done | bytes 73760 | tf_op jit(solution)/shard_map/ppermute | solution.py:455
  20.3 0.0 collective-permute-start.6
  20.3 0.5 %shard_map.50 = (f32[2,128,128]{2,1,0:T(8,128)S(1)}, f32[2,128,128]{2,1,0:T(8,128)S(1)}, f32[2,128,128]{2,1,0:T(8,128)S(1)}) custom-call(bf16[4,72,128]{2,1,0:T(8,128)(2,1)S(1)} %pad_maximum_fusion.refs_0_, bf16[4,72,128]{2,1,0:T(8,128)(2,1)S(1)} %collective-permute-done.9.refs_1_), custom_call_target="tpu_custom_call" | custom-call | tf_op jit(solution)/shard_map/pallas_call | solution.py:241
  20.8 0.4 %dense_prepare.2 = (bf16[512,256]{1,0:T(8,128)(2,1)S(1)}, bf16[256,128]{1,0:T(8,128)(2,1)S(1)}, f32[512,128]{1,0:T(8,128)S(1)}) custom-call(bf16[4,72,128]{2,1,0:T(8,128)(2,1)S(1)} %pad_maximum_fusion.refs_0_, bf16[4,72,128]{2,1,0:T(8,128)(2,1)S(1)} %collective-permute-done.9.refs_1_), custom_call_target="tpu_custom_call" | custom-call | tf_op jit(solution)/shard_map/dense_prepare/pallas_call | solution.py:360
  21.2 0.4 %dense_prepare.3 = (bf16[512,384]{1,0:T(8,128)(2,1)S(1)}, bf16[384,128]{1,0:T(8,128)(2,1)S(1)}, f32[512,128]{1,0:T(8,128)S(1)}) custom-call(bf16[4,72,128]{2,1,0:T(8,128)(2,1)S(1)} %collective-permute-done.3.refs_0_, bf16[4,72,128]{2,1,0:T(8,128)(2,1)S(1)} %collective-permute-done.4.refs_1_, bf16[4,72,128]{2,1,0:T(8,128)(2,1)S(1)} %collective-permute-done.5.refs_2_), custom_call_target="tpu_custom_call" | custom-call | tf_op jit(solution)/shard_map/dense_prepare/pallas_call | solution.py:360
  21.6 0.7 %begin_tiles.1.refs_6_ = f32[7168,128]{1,0:T(8,128)S(1)} custom-call(bf16[4,72,128]{2,1,0:T(8,128)(2,1)S(1)} %pad_maximum_fusion.refs_0_, bf16[4,72,128]{2,1,0:T(8,128)(2,1)S(1)} %collective-permute-done.9.refs_1_, bf16[512,256]{1,0:T(8,128)(2,1)S(1)} %get-tuple-element.25.refs_2_, bf16[256,128]{1,0:T(8,128)(2,1)S(1)} %get-tuple-element.26.refs_3_), custom_call_target="tpu_custom_call" | custom-call | tf_op jit(solution)/shard_map/begin_tiles/pallas_call | solution.py:395
  22.3 0.3 shard_map.51
  22.6 0.0 collective-permute-done.8.refs_5_.refs_2_
  22.6 0.0 collective-permute-done.6.refs_3_.refs_0_
  22.6 0.3 shard_map.52
  22.9 0.1 collective-permute-start.10
  23.0 0.8 %collective-permute-start.11 = (bf16[2,32,128]{2,1,0:T(8,128)(2,1)S(1)}, bf16[2,32,128]{2,1,0:T(8,128)(2,1)S(1)}, u32[]{:S(2)}, u32[]{:S(2)}) collective-permute-start(bf16[2,32,128]{2,1,0:T(8,128)(2,1)S(1)} %get-tuple-element.38), channel_id=1, source_target_pairs={{0,4},{1,5},{2,6},{3,7},{4,0},{5,1},{6,2},{7,3},{8,12},{9,13},{10,... | collective-permute-start | bytes 49160 | tf_op jit(solution)/shard_map/ppermute | solution.py:455
  23.7 3.6 %collective-permute-start.12 = (bf16[2,32,128]{2,1,0:T(8,128)(2,1)S(1)}, bf16[2,32,128]{2,1,0:T(8,128)(2,1)S(1)}, u32[]{:S(2)}, u32[]{:S(2)}) collective-permute-start(bf16[2,32,128]{2,1,0:T(8,128)(2,1)S(1)} %get-tuple-element.39), channel_id=1, source_target_pairs={{0,6},{1,7},{2,4},{3,5},{4,2},{5,3},{6,0},{7,1},{8,14},{9,15},{10,... | collective-permute-start | bytes 49160 | tf_op jit(solution)/shard_map/ppermute | solution.py:455
  27.3 3.3 %finish_tiles.1 = f32[7168,128]{1,0:T(8,128)} custom-call(bf16[4,72,128]{2,1,0:T(8,128)(2,1)S(1)} %collective-permute-done.3.refs_0_, bf16[4,72,128]{2,1,0:T(8,128)(2,1)S(1)} %collective-permute-done.4.refs_1_, bf16[4,72,128]{2,1,0:T(8,128)(2,1)S(1)} %collective-permute-done.5.refs_2_, bf16[4,72,128]{2,1,0:T(8,128)(2,1)S(1)} %collective-permute-done.6.refs_3_.refs_0_, ...), custom_call_target="tpu_custom_call" | custom-call | flops 1409286144 | bytes 7340032 | tf_op jit(solution)/shard_map/finish_tiles/pallas_call | solution.py:431
  30.6 0.0 collective-permute-done.10.refs_1_
  30.6 0.0 collective-permute-done.11.refs_2_
  30.6 0.7 %place.1 = bf16[8,32,128]{2,1,0:T(8,128)(2,1)} custom-call(bf16[2,32,128]{2,1,0:T(8,128)(2,1)S(1)} %get-tuple-element.36.refs_0_, bf16[2,32,128]{2,1,0:T(8,128)(2,1)S(1)} %collective-permute-done.10.refs_1_, bf16[2,32,128]{2,1,0:T(8,128)(2,1)S(1)} %collective-permute-done.11.refs_2_, bf16[2,32,128]{2,1,0:T(8,128)(2,1)S(1)} %collective-permute-done.12.refs_3_), custom_call_target="tpu_custom_call" | custom-call | tf_op jit(solution)/shard_map/place/pallas_call | solution.py:283
  (11 shorter events, 0.0 us)
Async XLA Ops:
  0.6 0.7 %copy-start.2 = (s32[1,8]{1,0:T(1,128)S(1)}, s32[1,8]{1,0:T(1,128)}, u32[]{:S(2)}) copy-start(s32[1,8]{1,0:T(1,128)} %counts_ref.1) | copy-start | bytes 100
  0.6 0.7 %copy-start.1 = (s32[1,8,32]{2,1,0:T(8,128)S(1)}, s32[1,8,32]{2,1,0:T(8,128)}, u32[]{:S(2)}) copy-start(s32[1,8,32]{2,1,0:T(8,128)} %param.4) | copy-start | bytes 3076
  0.6 0.9 %copy-start = (bf16[1,8,32,128]{3,2,1,0:T(8,128)(2,1)S(1)}, bf16[1,8,32,128]{3,2,1,0:T(8,128)(2,1)}, u32[]{:S(2)}) copy-start(bf16[1,8,32,128]{3,2,1,0:T(8,128)(2,1)} %param.3) | copy-start | bytes 196612
  1.7 5.7 %collective-permute-start = (bf16[72,128]{1,0:T(8,128)(2,1)S(1)}, bf16[72,128]{1,0:T(8,128)(2,1)S(1)}, u32[]{:S(2)}, u32[]{:S(2)}) collective-permute-start(bf16[72,128]{1,0:T(8,128)(2,1)S(1)} %get-tuple-element.22), channel_id=1, source_target_pairs={{0,2},{1,3},{2,0},{3,1},{4,6},{5,7},{6,4},{7,5},{8,10},{9,11},{10,... | collective-permute-start | bytes 55304 | tf_op jit(solution)/shard_map/ppermute | solution.py:455
  4.8 4.8 %collective-permute-start.1 = (bf16[72,128]{1,0:T(8,128)(2,1)S(1)}, bf16[72,128]{1,0:T(8,128)(2,1)S(1)}, u32[]{:S(2)}, u32[]{:S(2)}) collective-permute-start(bf16[72,128]{1,0:T(8,128)(2,1)S(1)} %get-tuple-element.23), channel_id=1, source_target_pairs={{0,4},{1,5},{2,6},{3,7},{4,0},{5,1},{6,2},{7,3},{8,12},{9,13},{10,... | collective-permute-start | bytes 55304 | tf_op jit(solution)/shard_map/ppermute | solution.py:455
  7.4 5.6 %collective-permute-start.2 = (bf16[72,128]{1,0:T(8,128)(2,1)S(1)}, bf16[72,128]{1,0:T(8,128)(2,1)S(1)}, u32[]{:S(2)}, u32[]{:S(2)}) collective-permute-start(bf16[72,128]{1,0:T(8,128)(2,1)S(1)} %get-tuple-element.24), channel_id=1, source_target_pairs={{0,6},{1,7},{2,4},{3,5},{4,2},{5,3},{6,0},{7,1},{8,14},{9,15},{10,... | collective-permute-start | bytes 55304 | tf_op jit(solution)/shard_map/ppermute | solution.py:455
  13.0 5.7 %collective-permute-start.5 = (bf16[4,72,128]{2,1,0:T(8,128)(2,1)S(1)}, bf16[4,72,128]{2,1,0:T(8,128)(2,1)S(1)}, u32[]{:S(2)}, u32[]{:S(2)}) collective-permute-start(bf16[4,72,128]{2,1,0:T(8,128)(2,1)S(1)} %pad_maximum_fusion.refs_0_), channel_id=1, source_target_pairs={{0,24},{8,16},{16,8},{24,0},{1,25},{9,17},{17,9},{25,1},{2,26},{10... | collective-permute-start | bytes 221192 | tf_op jit(solution)/shard_map/ppermute | solution.py:455
  15.5 4.4 %collective-permute-start.4 = (bf16[4,72,128]{2,1,0:T(8,128)(2,1)S(1)}, bf16[4,72,128]{2,1,0:T(8,128)(2,1)S(1)}, u32[]{:S(2)}, u32[]{:S(2)}) collective-permute-start(bf16[4,72,128]{2,1,0:T(8,128)(2,1)S(1)} %pad_maximum_fusion.refs_0_), channel_id=1, source_target_pairs={{0,16},{8,24},{16,0},{24,8},{1,17},{9,25},{17,1},{25,9},{2,18},{10... | collective-permute-start | bytes 221192 | tf_op jit(solution)/shard_map/ppermute | solution.py:455
  16.0 4.4 %collective-permute-start.3 = (bf16[4,72,128]{2,1,0:T(8,128)(2,1)S(1)}, bf16[4,72,128]{2,1,0:T(8,128)(2,1)S(1)}, u32[]{:S(2)}, u32[]{:S(2)}) collective-permute-start(bf16[4,72,128]{2,1,0:T(8,128)(2,1)S(1)} %pad_maximum_fusion.refs_0_), channel_id=1, source_target_pairs={{0,8},{8,0},{16,24},{24,16},{1,9},{9,1},{17,25},{25,17},{2,10},{10... | collective-permute-start | bytes 221192 | tf_op jit(solution)/shard_map/ppermute | solution.py:455
  16.5 3.8 %collective-permute-start.9 = (bf16[4,72,128]{2,1,0:T(8,128)(2,1)S(1)}, bf16[4,72,128]{2,1,0:T(8,128)(2,1)S(1)}, u32[]{:S(2)}, u32[]{:S(2)}) collective-permute-start(bf16[4,72,128]{2,1,0:T(8,128)(2,1)S(1)} %pad_maximum_fusion.refs_0_), channel_id=1, source_target_pairs={{0,1},{1,0},{2,3},{3,2},{4,5},{5,4},{6,7},{7,6},{8,9},{9,8},{10,11... | collective-permute-start | bytes 221192 | tf_op jit(solution)/shard_map/ppermute | solution.py:455
  18.7 3.9 %collective-permute-start.8 = (bf16[4,72,128]{2,1,0:T(8,128)(2,1)S(1)}, bf16[4,72,128]{2,1,0:T(8,128)(2,1)S(1)}, u32[]{:S(2)}, u32[]{:S(2)}) collective-permute-start(bf16[4,72,128]{2,1,0:T(8,128)(2,1)S(1)} %collective-permute-done.5.refs_2_), channel_id=1, source_target_pairs={{0,1},{1,0},{2,3},{3,2},{4,5},{5,4},{6,7},{7,6},{8,9},{9,8},{10,11... | collective-permute-start | bytes 221192 | tf_op jit(solution)/shard_map/ppermute | solution.py:455
  19.8 2.8 %collective-permute-start.7 = (bf16[4,72,128]{2,1,0:T(8,128)(2,1)S(1)}, bf16[4,72,128]{2,1,0:T(8,128)(2,1)S(1)}, u32[]{:S(2)}, u32[]{:S(2)}) collective-permute-start(bf16[4,72,128]{2,1,0:T(8,128)(2,1)S(1)} %collective-permute-done.4.refs_1_), channel_id=1, source_target_pairs={{0,1},{1,0},{2,3},{3,2},{4,5},{5,4},{6,7},{7,6},{8,9},{9,8},{10,11... | collective-permute-start | bytes 221192 | tf_op jit(solution)/shard_map/ppermute | solution.py:455
  20.3 2.3 %collective-permute-start.6 = (bf16[4,72,128]{2,1,0:T(8,128)(2,1)S(1)}, bf16[4,72,128]{2,1,0:T(8,128)(2,1)S(1)}, u32[]{:S(2)}, u32[]{:S(2)}) collective-permute-start(bf16[4,72,128]{2,1,0:T(8,128)(2,1)S(1)} %collective-permute-done.3.refs_0_), channel_id=1, source_target_pairs={{0,1},{1,0},{2,3},{3,2},{4,5},{5,4},{6,7},{7,6},{8,9},{9,8},{10,11... | collective-permute-start | bytes 221192 | tf_op jit(solution)/shard_map/ppermute | solution.py:455
  22.9 7.7 %collective-permute-start.10 = (bf16[2,32,128]{2,1,0:T(8,128)(2,1)S(1)}, bf16[2,32,128]{2,1,0:T(8,128)(2,1)S(1)}, u32[]{:S(2)}, u32[]{:S(2)}) collective-permute-start(bf16[2,32,128]{2,1,0:T(8,128)(2,1)S(1)} %get-tuple-element.37), channel_id=1, source_target_pairs={{0,2},{1,3},{2,0},{3,1},{4,6},{5,7},{6,4},{7,5},{8,10},{9,11},{10,... | collective-permute-start | bytes 49160 | tf_op jit(solution)/shard_map/ppermute | solution.py:455
  23.0 7.7 %collective-permute-start.11 = (bf16[2,32,128]{2,1,0:T(8,128)(2,1)S(1)}, bf16[2,32,128]{2,1,0:T(8,128)(2,1)S(1)}, u32[]{:S(2)}, u32[]{:S(2)}) collective-permute-start(bf16[2,32,128]{2,1,0:T(8,128)(2,1)S(1)} %get-tuple-element.38), channel_id=1, source_target_pairs={{0,4},{1,5},{2,6},{3,7},{4,0},{5,1},{6,2},{7,3},{8,12},{9,13},{10,... | collective-permute-start | bytes 49160 | tf_op jit(solution)/shard_map/ppermute | solution.py:455
  23.7 6.9 %collective-permute-start.12 = (bf16[2,32,128]{2,1,0:T(8,128)(2,1)S(1)}, bf16[2,32,128]{2,1,0:T(8,128)(2,1)S(1)}, u32[]{:S(2)}, u32[]{:S(2)}) collective-permute-start(bf16[2,32,128]{2,1,0:T(8,128)(2,1)S(1)} %get-tuple-element.39), channel_id=1, source_target_pairs={{0,6},{1,7},{2,4},{3,5},{4,2},{5,3},{6,0},{7,1},{8,14},{9,15},{10,... | collective-permute-start | bytes 49160 | tf_op jit(solution)/shard_map/ppermute | solution.py:455

commit v9 on v8

--- a/solution.py
+++ b/solution.py
@@ -442,7 +442,7 @@
             pltpu.SemaphoreType.DMA((BUCKET // (2 * TILE), 2)),
         ],
         cost_estimate=dense_cost(entries, lanes, 2.0),
-        compiler_params=grant(16 * MIB),
+        compiler_params=pltpu.CompilerParams(vmem_limit_bytes=16 * MIB),
         name="finish_tiles",
     )(*same_parts, *other_parts, begun, number, *middle)
 
@@ -465,7 +465,8 @@
     sums = begin_tiles(first, early)
     begun = more_answer(same[1:], begun)
     prepared = dense_prepare(same[1:])
-    answers = finish_answer(other[1:], begun)
+    begun = more_answer(other[2:], begun)
+    answers = finish_answer(other[1:2], begun)
     averaged = finish_tiles(same[1:], other[1:], sums, early[2], prepared)
     back = [answers[0]] + [swap(answers[k], "mem", members, 2 * k) for k in range(1, pairs)]
     return averaged, place(back)
@@ -483,7 +484,7 @@
 def per_device(groups, values, slots, counts):
     members, capacity, lanes = values.shape[1:]
     entries = groups * members * capacity
-    few = members == 8 and groups in (2, 4, 8) and entries <= 2048 and 4 * capacity == lanes
+    few = members == 8 and groups in (4, 8) and entries <= 2048 and 4 * capacity == lanes
     tiles = BUCKET % (2 * TILE) == 0 and BUCKET // TILE <= lanes
     move = by_pairs if few and tiles else by_all
     averaged, returned = move(values[0], slots[0], counts, groups)

time: 31.5 us -> 31.6 us (level)
    pallas_call x3 -> x4, Pallas kernels: 1.01 us -> 1.14 us  [run_answer(): pl.pallas_call(kernel, out_shape=out_shape, in_specs=[vmem_spec()] * len(...]
  transfers between devices with their start and end apart: 13 -> 13, of which waited for: 5 -> 5; matrix products, arithmetic and copies ran while one was open for 0% -> 0% of each run, Pallas kernels for 17% -> 18%
where the time goes in v9:
time: 31.6 us; the launch traced here: 31.5 us
  starting transfers between devices  13.7 us (43%)
  waiting for transfers between devices  9.38 us (30%)
  Pallas kernels  6.72 us (21%)
  local copies, waits for them, and re-layouts  0.84 us (3%)
  between operations  0.78 us (2%)
    ppermute x13, starting transfers between devices, swap(): return lax.ppermute(array, axis, [(i, i ^ by) for i in range(size)])  13.7 us
    ppermute x13, waiting for transfers between devices, swap(): return lax.ppermute(array, axis, [(i, i ^ by) for i in range(size)])  9.38 us
    pallas_call x1, Pallas kernels, finish_tiles(): pl.pallas_call(functools.partial(finish_tiles_kernel, len(other_parts)),...  3.26 us
    pallas_call x4, Pallas kernels, run_answer(): pl.pallas_call(kernel, out_shape=out_shape, in_specs=[vmem_spec()] * len(...  1.14 us
    unnamed x6, local copies, waits for them, and re-layouts  0.84 us
    pallas_call x2, Pallas kernels, dense_prepare(): pl.pallas_call(dense_prepare_kernel, out_shape=[jax.ShapeDtypeStruct((TIL...  0.8 us
    pallas_call x1, Pallas kernels, begin_tiles(): pl.pallas_call(begin_tiles_kernel, out_shape=jax.ShapeDtypeStruct((BUCKET...  0.67 us
    pallas_call x1, Pallas kernels, place(): pl.pallas_call(place_kernel, out_shape=jax.ShapeDtypeStruct((two * len(pa...  0.67 us
  transfers between devices with their start and end apart: 13, of which 5 were waited for; matrix products, arithmetic and copies ran while one was open for 0% of the time, Pallas kernels for 18%

profile of v9, /device:TPU:0, one launch (start us, length us, event | category | flops | bytes accessed | tf_op | source)
XLA Modules:
  0.0 31.5 jit_solution(2192957008685449243)
XLA Ops:
  0.7 0.6 %copy-done.2 = s32[1,8]{1,0:T(1,128)S(1)} copy-done((s32[1,8]{1,0:T(1,128)S(1)}, s32[1,8]{1,0:T(1,128)}, u32[]{:S(2)}) %copy-start.2) | copy-done | bytes 56
  1.3 0.0 copy-done.1
  1.3 0.2 copy-done
  1.5 0.2 pack.1
  1.7 3.1 %collective-permute-start = (bf16[72,128]{1,0:T(8,128)(2,1)S(1)}, bf16[72,128]{1,0:T(8,128)(2,1)S(1)}, u32[]{:S(2)}, u32[]{:S(2)}) collective-permute-start(bf16[72,128]{1,0:T(8,128)(2,1)S(1)} %get-tuple-element.24), channel_id=1, source_target_pairs={{0,2},{1,3},{2,0},{3,1},{4,6},{5,7},{6,4},{7,5},{8,10},{9,11},{10,... | collective-permute-start | bytes 55304 | tf_op jit(solution)/shard_map/ppermute | solution.py:455
  4.8 2.6 %collective-permute-start.1 = (bf16[72,128]{1,0:T(8,128)(2,1)S(1)}, bf16[72,128]{1,0:T(8,128)(2,1)S(1)}, u32[]{:S(2)}, u32[]{:S(2)}) collective-permute-start(bf16[72,128]{1,0:T(8,128)(2,1)S(1)} %get-tuple-element.25), channel_id=1, source_target_pairs={{0,4},{1,5},{2,6},{3,7},{4,0},{5,1},{6,2},{7,3},{8,12},{9,13},{10,... | collective-permute-start | bytes 55304 | tf_op jit(solution)/shard_map/ppermute | solution.py:455
  7.4 2.2 %collective-permute-done.1 = bf16[72,128]{1,0:T(8,128)(2,1)S(1)} collective-permute-done((bf16[72,128]{1,0:T(8,128)(2,1)S(1)}, bf16[72,128]{1,0:T(8,128)(2,1)S(1)}, u32[]{:S(2)}, u32[]{:S(2)}) %collective-permute-start.1) | collective-permute-done | bytes 18464 | tf_op jit(solution)/shard_map/ppermute | solution.py:455
  9.6 3.3 %collective-permute-done.2 = bf16[72,128]{1,0:T(8,128)(2,1)S(1)} collective-permute-done((bf16[72,128]{1,0:T(8,128)(2,1)S(1)}, bf16[72,128]{1,0:T(8,128)(2,1)S(1)}, u32[]{:S(2)}, u32[]{:S(2)}) %collective-permute-start.2) | collective-permute-done | bytes 18464 | tf_op jit(solution)/shard_map/ppermute | solution.py:455
  13.0 2.5 %collective-permute-start.5 = (bf16[4,72,128]{2,1,0:T(8,128)(2,1)S(1)}, bf16[4,72,128]{2,1,0:T(8,128)(2,1)S(1)}, u32[]{:S(2)}, u32[]{:S(2)}) collective-permute-start(bf16[4,72,128]{2,1,0:T(8,128)(2,1)S(1)} %pad_maximum_fusion.refs_0_), channel_id=1, source_target_pairs={{0,24},{8,16},{16,8},{24,0},{1,25},{9,17},{17,9},{25,1},{2,26},{10... | collective-permute-start | bytes 221192 | tf_op jit(solution)/shard_map/ppermute | solution.py:455
  15.5 0.5 %collective-permute-start.4 = (bf16[4,72,128]{2,1,0:T(8,128)(2,1)S(1)}, bf16[4,72,128]{2,1,0:T(8,128)(2,1)S(1)}, u32[]{:S(2)}, u32[]{:S(2)}) collective-permute-start(bf16[4,72,128]{2,1,0:T(8,128)(2,1)S(1)} %pad_maximum_fusion.refs_0_), channel_id=1, source_target_pairs={{0,16},{8,24},{16,0},{24,8},{1,17},{9,25},{17,1},{25,9},{2,18},{10... | collective-permute-start | bytes 221192 | tf_op jit(solution)/shard_map/ppermute | solution.py:455
  16.0 0.5 %collective-permute-start.3 = (bf16[4,72,128]{2,1,0:T(8,128)(2,1)S(1)}, bf16[4,72,128]{2,1,0:T(8,128)(2,1)S(1)}, u32[]{:S(2)}, u32[]{:S(2)}) collective-permute-start(bf16[4,72,128]{2,1,0:T(8,128)(2,1)S(1)} %pad_maximum_fusion.refs_0_), channel_id=1, source_target_pairs={{0,8},{8,0},{16,24},{24,16},{1,9},{9,1},{17,25},{25,17},{2,10},{10... | collective-permute-start | bytes 221192 | tf_op jit(solution)/shard_map/ppermute | solution.py:455
  16.5 0.0 collective-permute-start.9
  16.5 2.2 %collective-permute-done.5.refs_2_ = bf16[4,72,128]{2,1,0:T(8,128)(2,1)S(1)} collective-permute-done((bf16[4,72,128]{2,1,0:T(8,128)(2,1)S(1)}, bf16[4,72,128]{2,1,0:T(8,128)(2,1)S(1)}, u32[]{:S(2)}, u32[]{:S(2)}) %collective-permute-start.5) | collective-permute-done | bytes 73760 | tf_op jit(solution)/shard_map/ppermute | solution.py:455
  18.7 1.1 %collective-permute-done.4.refs_1_ = bf16[4,72,128]{2,1,0:T(8,128)(2,1)S(1)} collective-permute-done((bf16[4,72,128]{2,1,0:T(8,128)(2,1)S(1)}, bf16[4,72,128]{2,1,0:T(8,128)(2,1)S(1)}, u32[]{:S(2)}, u32[]{:S(2)}) %collective-permute-start.4) | collective-permute-done | bytes 73760 | tf_op jit(solution)/shard_map/ppermute | solution.py:455
  19.8 0.0 collective-permute-start.7
  19.8 0.5 %collective-permute-done.3.refs_0_ = bf16[4,72,128]{2,1,0:T(8,128)(2,1)S(1)} collective-permute-done((bf16[4,72,128]{2,1,0:T(8,128)(2,1)S(1)}, bf16[4,72,128]{2,1,0:T(8,128)(2,1)S(1)}, u32[]{:S(2)}, u32[]{:S(2)}) %collective-permute-start.3) | collective-permute-done | bytes 73760 | tf_op jit(solution)/shard_map/ppermute | solution.py:455
  20.3 0.0 collective-permute-start.6
  20.3 0.5 %shard_map.50 = (f32[2,128,128]{2,1,0:T(8,128)S(1)}, f32[2,128,128]{2,1,0:T(8,128)S(1)}, f32[2,128,128]{2,1,0:T(8,128)S(1)}) custom-call(bf16[4,72,128]{2,1,0:T(8,128)(2,1)S(1)} %pad_maximum_fusion.refs_0_, bf16[4,72,128]{2,1,0:T(8,128)(2,1)S(1)} %collective-permute-done.9.refs_1_), custom_call_target="tpu_custom_call" | custom-call | tf_op jit(solution)/shard_map/pallas_call | solution.py:241
  20.8 0.4 %dense_prepare.2 = (bf16[512,256]{1,0:T(8,128)(2,1)S(1)}, bf16[256,128]{1,0:T(8,128)(2,1)S(1)}, f32[512,128]{1,0:T(8,128)S(1)}) custom-call(bf16[4,72,128]{2,1,0:T(8,128)(2,1)S(1)} %pad_maximum_fusion.refs_0_, bf16[4,72,128]{2,1,0:T(8,128)(2,1)S(1)} %collective-permute-done.9.refs_1_), custom_call_target="tpu_custom_call" | custom-call | tf_op jit(solution)/shard_map/dense_prepare/pallas_call | solution.py:360
  21.2 0.4 %dense_prepare.3 = (bf16[512,384]{1,0:T(8,128)(2,1)S(1)}, bf16[384,128]{1,0:T(8,128)(2,1)S(1)}, f32[512,128]{1,0:T(8,128)S(1)}) custom-call(bf16[4,72,128]{2,1,0:T(8,128)(2,1)S(1)} %collective-permute-done.3.refs_0_, bf16[4,72,128]{2,1,0:T(8,128)(2,1)S(1)} %collective-permute-done.4.refs_1_, bf16[4,72,128]{2,1,0:T(8,128)(2,1)S(1)} %collective-permute-done.5.refs_2_), custom_call_target="tpu_custom_call" | custom-call | tf_op jit(solution)/shard_map/dense_prepare/pallas_call | solution.py:360
  21.6 0.7 %begin_tiles.1.refs_6_ = f32[7168,128]{1,0:T(8,128)S(1)} custom-call(bf16[4,72,128]{2,1,0:T(8,128)(2,1)S(1)} %pad_maximum_fusion.refs_0_, bf16[4,72,128]{2,1,0:T(8,128)(2,1)S(1)} %collective-permute-done.9.refs_1_, bf16[512,256]{1,0:T(8,128)(2,1)S(1)} %get-tuple-element.27.refs_2_, bf16[256,128]{1,0:T(8,128)(2,1)S(1)} %get-tuple-element.28.refs_3_), custom_call_target="tpu_custom_call" | custom-call | tf_op jit(solution)/shard_map/begin_tiles/pallas_call | solution.py:395
  22.3 0.3 shard_map.51
  22.6 0.0 collective-permute-done.8.refs_5_.refs_1_
  22.6 0.2 shard_map.52
  22.8 0.0 collective-permute-done.6.refs_3_.refs_0_
  22.8 0.2 shard_map.53
  23.0 0.1 collective-permute-start.10
  23.1 0.8 %collective-permute-start.11 = (bf16[2,32,128]{2,1,0:T(8,128)(2,1)S(1)}, bf16[2,32,128]{2,1,0:T(8,128)(2,1)S(1)}, u32[]{:S(2)}, u32[]{:S(2)}) collective-permute-start(bf16[2,32,128]{2,1,0:T(8,128)(2,1)S(1)} %get-tuple-element.42), channel_id=1, source_target_pairs={{0,4},{1,5},{2,6},{3,7},{4,0},{5,1},{6,2},{7,3},{8,12},{9,13},{10,... | collective-permute-start | bytes 49160 | tf_op jit(solution)/shard_map/ppermute | solution.py:455
  23.9 3.6 %collective-permute-start.12 = (bf16[2,32,128]{2,1,0:T(8,128)(2,1)S(1)}, bf16[2,32,128]{2,1,0:T(8,128)(2,1)S(1)}, u32[]{:S(2)}, u32[]{:S(2)}) collective-permute-start(bf16[2,32,128]{2,1,0:T(8,128)(2,1)S(1)} %get-tuple-element.43), channel_id=1, source_target_pairs={{0,6},{1,7},{2,4},{3,5},{4,2},{5,3},{6,0},{7,1},{8,14},{9,15},{10,... | collective-permute-start | bytes 49160 | tf_op jit(solution)/shard_map/ppermute | solution.py:455
  27.5 3.3 %finish_tiles.1 = f32[7168,128]{1,0:T(8,128)} custom-call(bf16[4,72,128]{2,1,0:T(8,128)(2,1)S(1)} %collective-permute-done.3.refs_0_, bf16[4,72,128]{2,1,0:T(8,128)(2,1)S(1)} %collective-permute-done.4.refs_1_, bf16[4,72,128]{2,1,0:T(8,128)(2,1)S(1)} %collective-permute-done.5.refs_2_, bf16[4,72,128]{2,1,0:T(8,128)(2,1)S(1)} %collective-permute-done.6.refs_3_.refs_0_, ...), custom_call_target="tpu_custom_call" | custom-call | flops 1409286144 | bytes 7340032 | tf_op jit(solution)/shard_map/finish_tiles/pallas_call | solution.py:431
  30.8 0.0 collective-permute-done.11.refs_2_
  30.8 0.7 %place.1 = bf16[8,32,128]{2,1,0:T(8,128)(2,1)} custom-call(bf16[2,32,128]{2,1,0:T(8,128)(2,1)S(1)} %get-tuple-element.40.refs_0_, bf16[2,32,128]{2,1,0:T(8,128)(2,1)S(1)} %collective-permute-done.10.refs_1_, bf16[2,32,128]{2,1,0:T(8,128)(2,1)S(1)} %collective-permute-done.11.refs_2_, bf16[2,32,128]{2,1,0:T(8,128)(2,1)S(1)} %collective-permute-done.12.refs_3_), custom_call_target="tpu_custom_call" | custom-call | tf_op jit(solution)/shard_map/place/pallas_call | solution.py:283
  (12 shorter events, 0.0 us)
Async XLA Ops:
  0.6 0.7 %copy-start.2 = (s32[1,8]{1,0:T(1,128)S(1)}, s32[1,8]{1,0:T(1,128)}, u32[]{:S(2)}) copy-start(s32[1,8]{1,0:T(1,128)} %counts_ref.1) | copy-start | bytes 100
  0.6 0.7 %copy-start.1 = (s32[1,8,32]{2,1,0:T(8,128)S(1)}, s32[1,8,32]{2,1,0:T(8,128)}, u32[]{:S(2)}) copy-start(s32[1,8,32]{2,1,0:T(8,128)} %param.4) | copy-start | bytes 3076
  0.6 0.9 %copy-start = (bf16[1,8,32,128]{3,2,1,0:T(8,128)(2,1)S(1)}, bf16[1,8,32,128]{3,2,1,0:T(8,128)(2,1)}, u32[]{:S(2)}) copy-start(bf16[1,8,32,128]{3,2,1,0:T(8,128)(2,1)} %param.3) | copy-start | bytes 196612
  1.7 5.7 %collective-permute-start = (bf16[72,128]{1,0:T(8,128)(2,1)S(1)}, bf16[72,128]{1,0:T(8,128)(2,1)S(1)}, u32[]{:S(2)}, u32[]{:S(2)}) collective-permute-start(bf16[72,128]{1,0:T(8,128)(2,1)S(1)} %get-tuple-element.24), channel_id=1, source_target_pairs={{0,2},{1,3},{2,0},{3,1},{4,6},{5,7},{6,4},{7,5},{8,10},{9,11},{10,... | collective-permute-start | bytes 55304 | tf_op jit(solution)/shard_map/ppermute | solution.py:455
  4.8 4.8 %collective-permute-start.1 = (bf16[72,128]{1,0:T(8,128)(2,1)S(1)}, bf16[72,128]{1,0:T(8,128)(2,1)S(1)}, u32[]{:S(2)}, u32[]{:S(2)}) collective-permute-start(bf16[72,128]{1,0:T(8,128)(2,1)S(1)} %get-tuple-element.25), channel_id=1, source_target_pairs={{0,4},{1,5},{2,6},{3,7},{4,0},{5,1},{6,2},{7,3},{8,12},{9,13},{10,... | collective-permute-start | bytes 55304 | tf_op jit(solution)/shard_map/ppermute | solution.py:455
  7.4 5.6 %collective-permute-start.2 = (bf16[72,128]{1,0:T(8,128)(2,1)S(1)}, bf16[72,128]{1,0:T(8,128)(2,1)S(1)}, u32[]{:S(2)}, u32[]{:S(2)}) collective-permute-start(bf16[72,128]{1,0:T(8,128)(2,1)S(1)} %get-tuple-element.26), channel_id=1, source_target_pairs={{0,6},{1,7},{2,4},{3,5},{4,2},{5,3},{6,0},{7,1},{8,14},{9,15},{10,... | collective-permute-start | bytes 55304 | tf_op jit(solution)/shard_map/ppermute | solution.py:455
  13.0 5.7 %collective-permute-start.5 = (bf16[4,72,128]{2,1,0:T(8,128)(2,1)S(1)}, bf16[4,72,128]{2,1,0:T(8,128)(2,1)S(1)}, u32[]{:S(2)}, u32[]{:S(2)}) collective-permute-start(bf16[4,72,128]{2,1,0:T(8,128)(2,1)S(1)} %pad_maximum_fusion.refs_0_), channel_id=1, source_target_pairs={{0,24},{8,16},{16,8},{24,0},{1,25},{9,17},{17,9},{25,1},{2,26},{10... | collective-permute-start | bytes 221192 | tf_op jit(solution)/shard_map/ppermute | solution.py:455
  15.5 4.4 %collective-permute-start.4 = (bf16[4,72,128]{2,1,0:T(8,128)(2,1)S(1)}, bf16[4,72,128]{2,1,0:T(8,128)(2,1)S(1)}, u32[]{:S(2)}, u32[]{:S(2)}) collective-permute-start(bf16[4,72,128]{2,1,0:T(8,128)(2,1)S(1)} %pad_maximum_fusion.refs_0_), channel_id=1, source_target_pairs={{0,16},{8,24},{16,0},{24,8},{1,17},{9,25},{17,1},{25,9},{2,18},{10... | collective-permute-start | bytes 221192 | tf_op jit(solution)/shard_map/ppermute | solution.py:455
  16.0 4.4 %collective-permute-start.3 = (bf16[4,72,128]{2,1,0:T(8,128)(2,1)S(1)}, bf16[4,72,128]{2,1,0:T(8,128)(2,1)S(1)}, u32[]{:S(2)}, u32[]{:S(2)}) collective-permute-start(bf16[4,72,128]{2,1,0:T(8,128)(2,1)S(1)} %pad_maximum_fusion.refs_0_), channel_id=1, source_target_pairs={{0,8},{8,0},{16,24},{24,16},{1,9},{9,1},{17,25},{25,17},{2,10},{10... | collective-permute-start | bytes 221192 | tf_op jit(solution)/shard_map/ppermute | solution.py:455
  16.5 3.8 %collective-permute-start.9 = (bf16[4,72,128]{2,1,0:T(8,128)(2,1)S(1)}, bf16[4,72,128]{2,1,0:T(8,128)(2,1)S(1)}, u32[]{:S(2)}, u32[]{:S(2)}) collective-permute-start(bf16[4,72,128]{2,1,0:T(8,128)(2,1)S(1)} %pad_maximum_fusion.refs_0_), channel_id=1, source_target_pairs={{0,1},{1,0},{2,3},{3,2},{4,5},{5,4},{6,7},{7,6},{8,9},{9,8},{10,11... | collective-permute-start | bytes 221192 | tf_op jit(solution)/shard_map/ppermute | solution.py:455
  18.7 3.9 %collective-permute-start.8 = (bf16[4,72,128]{2,1,0:T(8,128)(2,1)S(1)}, bf16[4,72,128]{2,1,0:T(8,128)(2,1)S(1)}, u32[]{:S(2)}, u32[]{:S(2)}) collective-permute-start(bf16[4,72,128]{2,1,0:T(8,128)(2,1)S(1)} %collective-permute-done.5.refs_2_), channel_id=1, source_target_pairs={{0,1},{1,0},{2,3},{3,2},{4,5},{5,4},{6,7},{7,6},{8,9},{9,8},{10,11... | collective-permute-start | bytes 221192 | tf_op jit(solution)/shard_map/ppermute | solution.py:455
  19.8 2.8 %collective-permute-start.7 = (bf16[4,72,128]{2,1,0:T(8,128)(2,1)S(1)}, bf16[4,72,128]{2,1,0:T(8,128)(2,1)S(1)}, u32[]{:S(2)}, u32[]{:S(2)}) collective-permute-start(bf16[4,72,128]{2,1,0:T(8,128)(2,1)S(1)} %collective-permute-done.4.refs_1_), channel_id=1, source_target_pairs={{0,1},{1,0},{2,3},{3,2},{4,5},{5,4},{6,7},{7,6},{8,9},{9,8},{10,11... | collective-permute-start | bytes 221192 | tf_op jit(solution)/shard_map/ppermute | solution.py:455
  20.3 2.5 %collective-permute-start.6 = (bf16[4,72,128]{2,1,0:T(8,128)(2,1)S(1)}, bf16[4,72,128]{2,1,0:T(8,128)(2,1)S(1)}, u32[]{:S(2)}, u32[]{:S(2)}) collective-permute-start(bf16[4,72,128]{2,1,0:T(8,128)(2,1)S(1)} %collective-permute-done.3.refs_0_), channel_id=1, source_target_pairs={{0,1},{1,0},{2,3},{3,2},{4,5},{5,4},{6,7},{7,6},{8,9},{9,8},{10,11... | collective-permute-start | bytes 221192 | tf_op jit(solution)/shard_map/ppermute | solution.py:455
  23.0 7.7 %collective-permute-start.10 = (bf16[2,32,128]{2,1,0:T(8,128)(2,1)S(1)}, bf16[2,32,128]{2,1,0:T(8,128)(2,1)S(1)}, u32[]{:S(2)}, u32[]{:S(2)}) collective-permute-start(bf16[2,32,128]{2,1,0:T(8,128)(2,1)S(1)} %get-tuple-element.41), channel_id=1, source_target_pairs={{0,2},{1,3},{2,0},{3,1},{4,6},{5,7},{6,4},{7,5},{8,10},{9,11},{10,... | collective-permute-start | bytes 49160 | tf_op jit(solution)/shard_map/ppermute | solution.py:455
  23.1 7.7 %collective-permute-start.11 = (bf16[2,32,128]{2,1,0:T(8,128)(2,1)S(1)}, bf16[2,32,128]{2,1,0:T(8,128)(2,1)S(1)}, u32[]{:S(2)}, u32[]{:S(2)}) collective-permute-start(bf16[2,32,128]{2,1,0:T(8,128)(2,1)S(1)} %get-tuple-element.42), channel_id=1, source_target_pairs={{0,4},{1,5},{2,6},{3,7},{4,0},{5,1},{6,2},{7,3},{8,12},{9,13},{10,... | collective-permute-start | bytes 49160 | tf_op jit(solution)/shard_map/ppermute | solution.py:455
  23.9 6.9 %collective-permute-start.12 = (bf16[2,32,128]{2,1,0:T(8,128)(2,1)S(1)}, bf16[2,32,128]{2,1,0:T(8,128)(2,1)S(1)}, u32[]{:S(2)}, u32[]{:S(2)}) collective-permute-start(bf16[2,32,128]{2,1,0:T(8,128)(2,1)S(1)} %get-tuple-element.43), channel_id=1, source_target_pairs={{0,6},{1,7},{2,4},{3,5},{4,2},{5,3},{6,0},{7,1},{8,14},{9,15},{10,... | collective-permute-start | bytes 49160 | tf_op jit(solution)/shard_map/ppermute | solution.py:455
